TPU v7x, 32 devices: a whole 2x2x4 slice. The times are simulated.
32 devices in a mesh: gx: 4 (over z), gy: 2 (over y), gz: 4 (over x, core).
Axes of the slice: x: 2, y: 2, z: 4, core: 2. Of those that a mesh axis runs over, the one named last changes fastest.
Arguments:
- start_disp: float32 [3, 32, 16, 512], P(None, 'gx', 'gy', 'gz'), may hold values from -2 to 2
- inertial: float32 [3, 32, 16, 512], P(None, 'gx', 'gy', 'gz'), may hold values from -1 to 1
- material: int32 [32, 16, 512], P('gx', 'gy', 'gz'), may hold values from 0 to 7
- pinned: int32 [32, 16, 512], P('gx', 'gy', 'gz'), may hold values 0 or 1
- stiffness: float32 [8], replicated, may hold values from 3 to 100
Outputs:
- displacement: float32 [3, 32, 16, 512], P(None, 'gx', 'gy', 'gz')
All inputs are finite; a program needn't handle non-finite values. No bound on the sum of `pinned` on one device may be relied on, other than what follows from the above.
Results may differ from a plain program's by a relative error of at most 0.0003.
Values sent between devices are 32-bit elements; how exact they have to be, the bound alone decides.
No kernel may reach another device: no remote copies, remote signals or barrier semaphores. Data moves between devices by JAX's collectives and lax.ppermute only.
A program may use at most 64 MiB of HBM per device.

v0:
```python
import jax
import jax.numpy as jnp
from jax import lax
from jax.sharding import PartitionSpec as P

ITERS = 4
POLAR_STEPS = 6
MATS = 8


inertia = 1.0
relax = 0.6
radius = 0.9


def with_halo(cells, sides, width):
    for axis, dim in sides:
        count = lax.axis_size(axis)
        ends = count - 1
        head = lax.slice_in_dim(cells, 0, width, axis=dim)
        tail = lax.slice_in_dim(cells, cells.shape[dim] - width, cells.shape[dim], axis=dim)
        cells = jnp.concatenate(
            [
                lax.ppermute(tail, axis, [(i, (i + 1) % count) for i in range(ends)]),
                cells,
                lax.ppermute(head, axis, [((i + 1) % count, i) for i in range(ends)]),
            ],
            axis=dim,
        )
    return cells


def forward_diff(field, axis):
    size = field.shape[axis]
    return lax.slice_in_dim(field, 1, size, axis=axis) - lax.slice_in_dim(
        field, 0, size - 1, axis=axis
    )


def pair_sum(field, axis):
    size = field.shape[axis]
    return lax.slice_in_dim(field, 1, size, axis=axis) + lax.slice_in_dim(
        field, 0, size - 1, axis=axis
    )


def gradient(field, axis):
    result = forward_diff(field, axis)
    for other in range(3):
        if other != axis:
            result = pair_sum(result, other)
    return 0.25 * result


def project(nodes, welem):
    deform = [
        [gradient(nodes[c], d) + (1.0 if c == d else 0.0) for d in range(3)] for c in range(3)
    ]
    total = sum((deform[c][d] * deform[c][d] for c in range(3) for d in range(3)))
    scale = jnp.maximum(jnp.sqrt(total / 3.0), 1.0)
    rotate = [[deform[c][d] / scale for d in range(3)] for c in range(3)]
    for step in range(POLAR_STEPS):
        middle = [
            [
                (1.5 if i == j else 0.0)
                - 0.5 * sum((rotate[k][i] * rotate[k][j] for k in range(3)))
                for j in range(3)
            ]
            for i in range(3)
        ]
        rotate = [
            [sum((rotate[c][j] * middle[j][d] for j in range(3))) for d in range(3)]
            for c in range(3)
        ]
    return [welem * (deform[c][d] - rotate[c][d]) for c in range(3) for d in range(3)]


def assemble(stress):
    forces = []
    for c in range(3):
        total = 0.0
        for d in range(3):
            term = stress[3 * c + d]
            for other in range(3):
                if other != d:
                    term = pair_sum(term, other)
            total = total - 0.25 * forward_diff(term, d)
        forces.append(total)
    return jnp.stack(forces)


def diagonal(welem):
    total = welem
    for axis in range(3):
        total = pair_sum(total, axis)
    return inertia + 3.0 / 16.0 * total


def node_halo(disp, weights):
    joined = jnp.concatenate([disp, weights[None]], axis=0)
    return with_halo(joined, (("gx", 1), ("gy", 2), ("gz", 3)), 1)


def per_device(start_disp, inertial, material, pinned, stiffness):
    size_x, size_y, size_z = material.shape
    grid_x = lax.broadcasted_iota(jnp.int32, material.shape, 0) + lax.axis_index("gx") * size_x
    grid_y = lax.broadcasted_iota(jnp.int32, material.shape, 1) + lax.axis_index("gy") * size_y
    grid_z = lax.broadcasted_iota(jnp.int32, material.shape, 2) + lax.axis_index("gz") * size_z
    valid = (
        (grid_x < size_x * lax.axis_size("gx") - 1)
        & (grid_y < size_y * lax.axis_size("gy") - 1)
        & (grid_z < size_z * lax.axis_size("gz") - 1)
    )
    table = jnp.zeros(material.shape, jnp.float32)
    for index in range(MATS):
        table = table + jnp.where(material == index, stiffness[index], 0.0)
    weights = jnp.where(valid, table, 0.0)
    pins = pinned[None] > 0
    disp = jnp.where(pins, inertial, start_disp)
    previous = disp
    omega = 1.0
    for step in range(ITERS):
        padded = node_halo(disp, weights)
        welem = padded[3, : size_x + 1, : size_y + 1, : size_z + 1]
        diag = diagonal(welem)
        forces = assemble(project([padded[0], padded[1], padded[2]], welem))
        target = disp - relax * (inertia * (disp - inertial) + forces) / diag[None]
        if step == 0:
            fresh = target
        else:
            omega = (
                2.0 / (2.0 - radius * radius)
                if step == 1
                else 4.0 / (4.0 - radius * radius * omega)
            )
            fresh = omega * (target - previous) + previous
        fresh = jnp.where(pins, inertial, fresh)
        previous = disp
        disp = fresh
    return disp


def solution(mesh):
    placed = (
        P(None, "gx", "gy", "gz"),
        P(None, "gx", "gy", "gz"),
        P("gx", "gy", "gz"),
        P("gx", "gy", "gz"),
        P(),
    )
    return jax.shard_map(
        per_device, mesh=mesh, in_specs=placed, out_specs=P(None, "gx", "gy", "gz"), check_vma=False
    )
```

profile of v0, /device:TPU:1, one launch (start us, length us, event | category | flops | bytes accessed | tf_op | source)
XLA Modules:
  0.0 147.5 jit_solution(12972849443909755106)
XLA Ops:
  0.0 1.6 %fusion.333 = (f32[1]{0:T(128)}, f32[1]{0:T(128)}, f32[1]{0:T(128)}, f32[1]{0:T(128)}, f32[1]{0:T(128)}, /*index=5*/f32[1]{0:T(128)}, f32[1]{0:T(128)}, f32[1]{0:T(128)}) fusion(f32[8]{0:T(128)} %param.9), kind=kLoop, calls=%fused_computation.940 | loop fusion | bytes 64 | tf_op jit(solution)/shard_map/slice | solution.py:116
  1.7 1.0 broadcast_select_fusion
  2.6 0.7 copy-done.3
  3.4 4.9 %select_bitcast_fusion = f32[1,8,8,128]{3,2,1,0:T(8,128)S(1)} fusion(s32[8,8,128]{2,1,0:T(8,128)S(1)} %copy-done.3, f32[]{:T(128)} %bitcast.7, f32[]{:T(128)} %bitcast.6, f32[]{:T(128)} %bitcast.5, f32[]{:T(128)} %bitcast.4, f32[]{:T(128)} %bitcast.3, f32[]{:T(128)} %bitcast.2, f32[]{:T(128)} %bitcast.1, f32[]{:T(128)} %bitcast, ...), kind=kLoop, calls=%fused_computation.883 | loop fusion | flops 212992 | bytes 65712 | tf_op jit(solution)/shard_map/broadcast_in_dim | solution.py:100
  8.3 4.0 %collective-permute-start = (f32[4,1,8,128]{3,2,1,0:T(8,128)S(1)}, f32[4,1,8,128]{3,2,1,0:T(8,128)S(1)}, u32[]{:S(2)}, u32[]{:S(2)}) collective-permute-start(f32[4,1,8,128]{3,2,1,0:T(8,128)S(1)} %get-tuple-element.373), channel_id=1, source_target_pairs={{0,8},{8,16},{16,24},{1,9},{9,17},{17,25},{2,10},{10,18},{18,26},{... | collective-permute-start | bytes 49160 | tf_op jit(solution)/shard_map/ppermute | solution.py:24
  12.3 1.3 collective-permute-start.1
  13.6 3.2 %collective-permute-done.1 = f32[4,1,8,128]{3,2,1,0:T(8,128)S(1)} collective-permute-done((f32[4,1,8,128]{3,2,1,0:T(8,128)S(1)}, f32[4,1,8,128]{3,2,1,0:T(8,128)S(1)}, u32[]{:S(2)}, u32[]{:S(2)}) %collective-permute-start.1) | collective-permute-done | bytes 16416 | tf_op jit(solution)/shard_map/ppermute | solution.py:26
  16.9 3.1 %collective-permute-start.2 = (f32[4,10,1,128]{3,2,1,0:T(1,128)S(1)}, f32[4,10,1,128]{3,2,1,0:T(1,128)S(1)}, u32[]{:S(2)}, u32[]{:S(2)}) collective-permute-start(f32[4,10,1,128]{3,2,1,0:T(1,128)S(1)} %get-tuple-element.365), channel_id=1, source_target_pairs={{0,4},{1,5},{2,6},{3,7},{8,12},{9,13},{10,14},{11,15},{16,20},{17,... | collective-permute-start | bytes 61448 | tf_op jit(solution)/shard_map/ppermute | solution.py:24
  20.0 1.3 collective-permute-start.3
  21.3 3.2 %collective-permute-done.3 = f32[4,10,1,128]{3,2,1,0:T(1,128)S(1)} collective-permute-done((f32[4,10,1,128]{3,2,1,0:T(1,128)S(1)}, f32[4,10,1,128]{3,2,1,0:T(1,128)S(1)}, u32[]{:S(2)}, u32[]{:S(2)}) %collective-permute-start.3) | collective-permute-done | bytes 20512 | tf_op jit(solution)/shard_map/ppermute | solution.py:26
  24.8 6.5 %collective-permute-start.4 = (f32[4,10,10,1]{3,2,1,0:T(8,128)S(1)}, f32[4,10,10,1]{3,2,1,0:T(8,128)S(1)}, u32[]{:S(2)}, u32[]{:S(2)}) collective-permute-start(f32[4,10,10,1]{3,2,1,0:T(8,128)S(1)} %get-tuple-element.358), channel_id=1, source_target_pairs={{0,1},{1,2},{2,3},{4,5},{5,6},{6,7},{8,9},{9,10},{10,11},{12,13},{... | collective-permute-start | bytes 4808 | tf_op jit(solution)/shard_map/ppermute | solution.py:24
  31.3 1.9 %collective-permute-start.5 = (f32[4,10,10,1]{3,2,1,0:T(8,128)S(1)}, f32[4,10,10,1]{3,2,1,0:T(8,128)S(1)}, u32[]{:S(2)}, u32[]{:S(2)}) collective-permute-start(f32[4,10,10,1]{3,2,1,0:T(8,128)S(1)} %get-tuple-element.357), channel_id=1, source_target_pairs={{1,0},{2,1},{3,2},{5,4},{6,5},{7,6},{9,8},{10,9},{11,10},{13,12},{... | collective-permute-start | bytes 4808 | tf_op jit(solution)/shard_map/ppermute | solution.py:26
  33.2 2.1 %collective-permute-done.4 = f32[4,10,10,1]{3,2,1,0:T(8,128)S(1)} collective-permute-done((f32[4,10,10,1]{3,2,1,0:T(8,128)S(1)}, f32[4,10,10,1]{3,2,1,0:T(8,128)S(1)}, u32[]{:S(2)}, u32[]{:S(2)}) %collective-permute-start.4) | collective-permute-done | bytes 1632 | tf_op jit(solution)/shard_map/ppermute | solution.py:24
  35.3 4.4 %collective-permute-done.5 = f32[4,10,10,1]{3,2,1,0:T(8,128)S(1)} collective-permute-done((f32[4,10,10,1]{3,2,1,0:T(8,128)S(1)}, f32[4,10,10,1]{3,2,1,0:T(8,128)S(1)}, u32[]{:S(2)}, u32[]{:S(2)}) %collective-permute-start.5) | collective-permute-done | bytes 1632 | tf_op jit(solution)/shard_map/ppermute | solution.py:26
  43.9 0.5 subtract_multiply_fusion.35
  46.5 0.8 copy-done
  47.4 3.2 %collective-permute-start.6 = (f32[4,1,8,128]{3,2,1,0:T(8,128)S(1)}, f32[4,1,8,128]{3,2,1,0:T(8,128)S(1)}, u32[]{:S(2)}, u32[]{:S(2)}) collective-permute-start(f32[4,1,8,128]{3,2,1,0:T(8,128)S(1)} %get-tuple-element.371), channel_id=1, source_target_pairs={{0,8},{8,16},{16,24},{1,9},{9,17},{17,25},{2,10},{10,18},{18,26},{... | collective-permute-start | bytes 49160 | tf_op jit(solution)/shard_map/ppermute | solution.py:24
  50.6 1.3 collective-permute-start.7
  51.9 3.2 %collective-permute-done.7 = f32[4,1,8,128]{3,2,1,0:T(8,128)S(1)} collective-permute-done((f32[4,1,8,128]{3,2,1,0:T(8,128)S(1)}, f32[4,1,8,128]{3,2,1,0:T(8,128)S(1)}, u32[]{:S(2)}, u32[]{:S(2)}) %collective-permute-start.7) | collective-permute-done | bytes 16416 | tf_op jit(solution)/shard_map/ppermute | solution.py:26
  55.1 1.4 collective-permute-start.8
  56.5 1.3 collective-permute-start.9
  57.8 3.2 %collective-permute-done.9 = f32[4,10,1,128]{3,2,1,0:T(1,128)S(1)} collective-permute-done((f32[4,10,1,128]{3,2,1,0:T(1,128)S(1)}, f32[4,10,1,128]{3,2,1,0:T(1,128)S(1)}, u32[]{:S(2)}, u32[]{:S(2)}) %collective-permute-start.9) | collective-permute-done | bytes 20512 | tf_op jit(solution)/shard_map/ppermute | solution.py:26
  61.2 4.6 %collective-permute-start.10 = (f32[4,10,10,1]{3,2,1,0:T(8,128)S(1)}, f32[4,10,10,1]{3,2,1,0:T(8,128)S(1)}, u32[]{:S(2)}, u32[]{:S(2)}) collective-permute-start(f32[4,10,10,1]{3,2,1,0:T(8,128)S(1)} %get-tuple-element.356), channel_id=1, source_target_pairs={{0,1},{1,2},{2,3},{4,5},{5,6},{6,7},{8,9},{9,10},{10,11},{12,13},{... | collective-permute-start | bytes 4808 | tf_op jit(solution)/shard_map/ppermute | solution.py:24
  65.8 2.1 %collective-permute-start.11 = (f32[4,10,10,1]{3,2,1,0:T(8,128)S(1)}, f32[4,10,10,1]{3,2,1,0:T(8,128)S(1)}, u32[]{:S(2)}, u32[]{:S(2)}) collective-permute-start(f32[4,10,10,1]{3,2,1,0:T(8,128)S(1)} %get-tuple-element.355), channel_id=1, source_target_pairs={{1,0},{2,1},{3,2},{5,4},{6,5},{7,6},{9,8},{10,9},{11,10},{13,12},{... | collective-permute-start | bytes 4808 | tf_op jit(solution)/shard_map/ppermute | solution.py:26
  68.0 1.9 %collective-permute-done.10 = f32[4,10,10,1]{3,2,1,0:T(8,128)S(1)} collective-permute-done((f32[4,10,10,1]{3,2,1,0:T(8,128)S(1)}, f32[4,10,10,1]{3,2,1,0:T(8,128)S(1)}, u32[]{:S(2)}, u32[]{:S(2)}) %collective-permute-start.10) | collective-permute-done | bytes 1632 | tf_op jit(solution)/shard_map/ppermute | solution.py:24
  69.8 4.4 %collective-permute-done.11 = f32[4,10,10,1]{3,2,1,0:T(8,128)S(1)} collective-permute-done((f32[4,10,10,1]{3,2,1,0:T(8,128)S(1)}, f32[4,10,10,1]{3,2,1,0:T(8,128)S(1)}, u32[]{:S(2)}, u32[]{:S(2)}) %collective-permute-start.11) | collective-permute-done | bytes 1632 | tf_op jit(solution)/shard_map/ppermute | solution.py:26
  78.4 0.5 subtract_multiply_fusion.26
  81.1 3.2 %collective-permute-start.12 = (f32[4,1,8,128]{3,2,1,0:T(8,128)S(1)}, f32[4,1,8,128]{3,2,1,0:T(8,128)S(1)}, u32[]{:S(2)}, u32[]{:S(2)}) collective-permute-start(f32[4,1,8,128]{3,2,1,0:T(8,128)S(1)} %get-tuple-element.369), channel_id=1, source_target_pairs={{0,8},{8,16},{16,24},{1,9},{9,17},{17,25},{2,10},{10,18},{18,26},{... | collective-permute-start | bytes 49160 | tf_op jit(solution)/shard_map/ppermute | solution.py:24
  84.3 1.3 collective-permute-start.13
  85.6 3.2 %collective-permute-done.13 = f32[4,1,8,128]{3,2,1,0:T(8,128)S(1)} collective-permute-done((f32[4,1,8,128]{3,2,1,0:T(8,128)S(1)}, f32[4,1,8,128]{3,2,1,0:T(8,128)S(1)}, u32[]{:S(2)}, u32[]{:S(2)}) %collective-permute-start.13) | collective-permute-done | bytes 16416 | tf_op jit(solution)/shard_map/ppermute | solution.py:26
  88.8 1.4 collective-permute-start.14
  90.2 1.3 collective-permute-start.15
  91.5 3.2 %collective-permute-done.15 = f32[4,10,1,128]{3,2,1,0:T(1,128)S(1)} collective-permute-done((f32[4,10,1,128]{3,2,1,0:T(1,128)S(1)}, f32[4,10,1,128]{3,2,1,0:T(1,128)S(1)}, u32[]{:S(2)}, u32[]{:S(2)}) %collective-permute-start.15) | collective-permute-done | bytes 20512 | tf_op jit(solution)/shard_map/ppermute | solution.py:26
  94.9 4.6 %collective-permute-start.16 = (f32[4,10,10,1]{3,2,1,0:T(8,128)S(1)}, f32[4,10,10,1]{3,2,1,0:T(8,128)S(1)}, u32[]{:S(2)}, u32[]{:S(2)}) collective-permute-start(f32[4,10,10,1]{3,2,1,0:T(8,128)S(1)} %get-tuple-element.354), channel_id=1, source_target_pairs={{0,1},{1,2},{2,3},{4,5},{5,6},{6,7},{8,9},{9,10},{10,11},{12,13},{... | collective-permute-start | bytes 4808 | tf_op jit(solution)/shard_map/ppermute | solution.py:24
  99.5 2.1 %collective-permute-start.17 = (f32[4,10,10,1]{3,2,1,0:T(8,128)S(1)}, f32[4,10,10,1]{3,2,1,0:T(8,128)S(1)}, u32[]{:S(2)}, u32[]{:S(2)}) collective-permute-start(f32[4,10,10,1]{3,2,1,0:T(8,128)S(1)} %get-tuple-element.353), channel_id=1, source_target_pairs={{1,0},{2,1},{3,2},{5,4},{6,5},{7,6},{9,8},{10,9},{11,10},{13,12},{... | collective-permute-start | bytes 4808 | tf_op jit(solution)/shard_map/ppermute | solution.py:26
  101.7 1.8 %collective-permute-done.16 = f32[4,10,10,1]{3,2,1,0:T(8,128)S(1)} collective-permute-done((f32[4,10,10,1]{3,2,1,0:T(8,128)S(1)}, f32[4,10,10,1]{3,2,1,0:T(8,128)S(1)}, u32[]{:S(2)}, u32[]{:S(2)}) %collective-permute-start.16) | collective-permute-done | bytes 1632 | tf_op jit(solution)/shard_map/ppermute | solution.py:24
  103.5 4.4 %collective-permute-done.17 = f32[4,10,10,1]{3,2,1,0:T(8,128)S(1)} collective-permute-done((f32[4,10,10,1]{3,2,1,0:T(8,128)S(1)}, f32[4,10,10,1]{3,2,1,0:T(8,128)S(1)}, u32[]{:S(2)}, u32[]{:S(2)}) %collective-permute-start.17) | collective-permute-done | bytes 1632 | tf_op jit(solution)/shard_map/ppermute | solution.py:26
  114.8 1.6 %collective-permute-start.18 = (f32[4,1,8,128]{3,2,1,0:T(8,128)S(1)}, f32[4,1,8,128]{3,2,1,0:T(8,128)S(1)}, u32[]{:S(2)}, u32[]{:S(2)}) collective-permute-start(f32[4,1,8,128]{3,2,1,0:T(8,128)S(1)} %get-tuple-element.367), channel_id=1, source_target_pairs={{0,8},{8,16},{16,24},{1,9},{9,17},{17,25},{2,10},{10,18},{18,26},{... | collective-permute-start | bytes 49160 | tf_op jit(solution)/shard_map/ppermute | solution.py:24
  116.4 1.3 collective-permute-start.19
  117.7 3.2 %collective-permute-done.19 = f32[4,1,8,128]{3,2,1,0:T(8,128)S(1)} collective-permute-done((f32[4,1,8,128]{3,2,1,0:T(8,128)S(1)}, f32[4,1,8,128]{3,2,1,0:T(8,128)S(1)}, u32[]{:S(2)}, u32[]{:S(2)}) %collective-permute-start.19) | collective-permute-done | bytes 16416 | tf_op jit(solution)/shard_map/ppermute | solution.py:26
  120.9 1.4 collective-permute-start.20
  122.3 1.3 collective-permute-start.21
  123.6 3.2 %collective-permute-done.21 = f32[4,10,1,128]{3,2,1,0:T(1,128)S(1)} collective-permute-done((f32[4,10,1,128]{3,2,1,0:T(1,128)S(1)}, f32[4,10,1,128]{3,2,1,0:T(1,128)S(1)}, u32[]{:S(2)}, u32[]{:S(2)}) %collective-permute-start.21) | collective-permute-done | bytes 20512 | tf_op jit(solution)/shard_map/ppermute | solution.py:26
  127.0 4.6 %collective-permute-start.22 = (f32[4,10,10,1]{3,2,1,0:T(8,128)S(1)}, f32[4,10,10,1]{3,2,1,0:T(8,128)S(1)}, u32[]{:S(2)}, u32[]{:S(2)}) collective-permute-start(f32[4,10,10,1]{3,2,1,0:T(8,128)S(1)} %get-tuple-element.352), channel_id=1, source_target_pairs={{0,1},{1,2},{2,3},{4,5},{5,6},{6,7},{8,9},{9,10},{10,11},{12,13},{... | collective-permute-start | bytes 4808 | tf_op jit(solution)/shard_map/ppermute | solution.py:24
  131.7 2.2 %collective-permute-start.23 = (f32[4,10,10,1]{3,2,1,0:T(8,128)S(1)}, f32[4,10,10,1]{3,2,1,0:T(8,128)S(1)}, u32[]{:S(2)}, u32[]{:S(2)}) collective-permute-start(f32[4,10,10,1]{3,2,1,0:T(8,128)S(1)} %get-tuple-element.351), channel_id=1, source_target_pairs={{1,0},{2,1},{3,2},{5,4},{6,5},{7,6},{9,8},{10,9},{11,10},{13,12},{... | collective-permute-start | bytes 4808 | tf_op jit(solution)/shard_map/ppermute | solution.py:26
  133.8 1.8 %collective-permute-done.22 = f32[4,10,10,1]{3,2,1,0:T(8,128)S(1)} collective-permute-done((f32[4,10,10,1]{3,2,1,0:T(8,128)S(1)}, f32[4,10,10,1]{3,2,1,0:T(8,128)S(1)}, u32[]{:S(2)}, u32[]{:S(2)}) %collective-permute-start.22) | collective-permute-done | bytes 1632 | tf_op jit(solution)/shard_map/ppermute | solution.py:24
  135.7 4.4 %collective-permute-done.23 = f32[4,10,10,1]{3,2,1,0:T(8,128)S(1)} collective-permute-done((f32[4,10,10,1]{3,2,1,0:T(8,128)S(1)}, f32[4,10,10,1]{3,2,1,0:T(8,128)S(1)}, u32[]{:S(2)}, u32[]{:S(2)}) %collective-permute-start.23) | collective-permute-done | bytes 1632 | tf_op jit(solution)/shard_map/ppermute | solution.py:26
  146.8 0.7 fusion.156
  (258 shorter events, 25.9 us)
Async XLA Ops:
  0.0 1.6 %copy-start.2 = (s32[8,8,128]{2,1,0:T(8,128)S(1)}, s32[8,8,128]{2,1,0:T(8,128)}, u32[]{:S(2)}) copy-start(s32[8,8,128]{2,1,0:T(8,128)} %param.8) | copy-start | bytes 98308
  2.6 0.8 copy-start.3
  8.3 5.3 %collective-permute-start = (f32[4,1,8,128]{3,2,1,0:T(8,128)S(1)}, f32[4,1,8,128]{3,2,1,0:T(8,128)S(1)}, u32[]{:S(2)}, u32[]{:S(2)}) collective-permute-start(f32[4,1,8,128]{3,2,1,0:T(8,128)S(1)} %get-tuple-element.373), channel_id=1, source_target_pairs={{0,8},{8,16},{16,24},{1,9},{9,17},{17,25},{2,10},{10,18},{18,26},{... | collective-permute-start | bytes 49160 | tf_op jit(solution)/shard_map/ppermute | solution.py:24
  12.3 4.5 %collective-permute-start.1 = (f32[4,1,8,128]{3,2,1,0:T(8,128)S(1)}, f32[4,1,8,128]{3,2,1,0:T(8,128)S(1)}, u32[]{:S(2)}, u32[]{:S(2)}) collective-permute-start(f32[4,1,8,128]{3,2,1,0:T(8,128)S(1)} %get-tuple-element.301), channel_id=1, source_target_pairs={{8,0},{16,8},{24,16},{9,1},{17,9},{25,17},{10,2},{18,10},{26,18},{... | collective-permute-start | bytes 49160 | tf_op jit(solution)/shard_map/ppermute | solution.py:26
  16.9 4.5 %collective-permute-start.2 = (f32[4,10,1,128]{3,2,1,0:T(1,128)S(1)}, f32[4,10,1,128]{3,2,1,0:T(1,128)S(1)}, u32[]{:S(2)}, u32[]{:S(2)}) collective-permute-start(f32[4,10,1,128]{3,2,1,0:T(1,128)S(1)} %get-tuple-element.365), channel_id=1, source_target_pairs={{0,4},{1,5},{2,6},{3,7},{8,12},{9,13},{10,14},{11,15},{16,20},{17,... | collective-permute-start | bytes 61448 | tf_op jit(solution)/shard_map/ppermute | solution.py:24
  20.0 4.5 %collective-permute-start.3 = (f32[4,10,1,128]{3,2,1,0:T(1,128)S(1)}, f32[4,10,1,128]{3,2,1,0:T(1,128)S(1)}, u32[]{:S(2)}, u32[]{:S(2)}) collective-permute-start(f32[4,10,1,128]{3,2,1,0:T(1,128)S(1)} %get-tuple-element.366), channel_id=1, source_target_pairs={{4,0},{5,1},{6,2},{7,3},{12,8},{13,9},{14,10},{15,11},{20,16},{21,... | collective-permute-start | bytes 61448 | tf_op jit(solution)/shard_map/ppermute | solution.py:26
  24.8 10.5 %collective-permute-start.4 = (f32[4,10,10,1]{3,2,1,0:T(8,128)S(1)}, f32[4,10,10,1]{3,2,1,0:T(8,128)S(1)}, u32[]{:S(2)}, u32[]{:S(2)}) collective-permute-start(f32[4,10,10,1]{3,2,1,0:T(8,128)S(1)} %get-tuple-element.358), channel_id=1, source_target_pairs={{0,1},{1,2},{2,3},{4,5},{5,6},{6,7},{8,9},{9,10},{10,11},{12,13},{... | collective-permute-start | bytes 4808 | tf_op jit(solution)/shard_map/ppermute | solution.py:24
  31.3 8.4 %collective-permute-start.5 = (f32[4,10,10,1]{3,2,1,0:T(8,128)S(1)}, f32[4,10,10,1]{3,2,1,0:T(8,128)S(1)}, u32[]{:S(2)}, u32[]{:S(2)}) collective-permute-start(f32[4,10,10,1]{3,2,1,0:T(8,128)S(1)} %get-tuple-element.357), channel_id=1, source_target_pairs={{1,0},{2,1},{3,2},{5,4},{6,5},{7,6},{9,8},{10,9},{11,10},{13,12},{... | collective-permute-start | bytes 4808 | tf_op jit(solution)/shard_map/ppermute | solution.py:26
  46.4 0.9 copy-start
  46.4 0.9 copy-start.1
  47.4 4.5 %collective-permute-start.6 = (f32[4,1,8,128]{3,2,1,0:T(8,128)S(1)}, f32[4,1,8,128]{3,2,1,0:T(8,128)S(1)}, u32[]{:S(2)}, u32[]{:S(2)}) collective-permute-start(f32[4,1,8,128]{3,2,1,0:T(8,128)S(1)} %get-tuple-element.371), channel_id=1, source_target_pairs={{0,8},{8,16},{16,24},{1,9},{9,17},{17,25},{2,10},{10,18},{18,26},{... | collective-permute-start | bytes 49160 | tf_op jit(solution)/shard_map/ppermute | solution.py:24
  50.6 4.5 %collective-permute-start.7 = (f32[4,1,8,128]{3,2,1,0:T(8,128)S(1)}, f32[4,1,8,128]{3,2,1,0:T(8,128)S(1)}, u32[]{:S(2)}, u32[]{:S(2)}) collective-permute-start(f32[4,1,8,128]{3,2,1,0:T(8,128)S(1)} %get-tuple-element.372), channel_id=1, source_target_pairs={{8,0},{16,8},{24,16},{9,1},{17,9},{25,17},{10,2},{18,10},{26,18},{... | collective-permute-start | bytes 49160 | tf_op jit(solution)/shard_map/ppermute | solution.py:26
  55.1 2.7 %collective-permute-start.8 = (f32[4,10,1,128]{3,2,1,0:T(1,128)S(1)}, f32[4,10,1,128]{3,2,1,0:T(1,128)S(1)}, u32[]{:S(2)}, u32[]{:S(2)}) collective-permute-start(f32[4,10,1,128]{3,2,1,0:T(1,128)S(1)} %get-tuple-element.363), channel_id=1, source_target_pairs={{0,4},{1,5},{2,6},{3,7},{8,12},{9,13},{10,14},{11,15},{16,20},{17,... | collective-permute-start | bytes 61448 | tf_op jit(solution)/shard_map/ppermute | solution.py:24
  56.5 4.5 %collective-permute-start.9 = (f32[4,10,1,128]{3,2,1,0:T(1,128)S(1)}, f32[4,10,1,128]{3,2,1,0:T(1,128)S(1)}, u32[]{:S(2)}, u32[]{:S(2)}) collective-permute-start(f32[4,10,1,128]{3,2,1,0:T(1,128)S(1)} %get-tuple-element.364), channel_id=1, source_target_pairs={{4,0},{5,1},{6,2},{7,3},{12,8},{13,9},{14,10},{15,11},{20,16},{21,... | collective-permute-start | bytes 61448 | tf_op jit(solution)/shard_map/ppermute | solution.py:26
  61.2 8.6 %collective-permute-start.10 = (f32[4,10,10,1]{3,2,1,0:T(8,128)S(1)}, f32[4,10,10,1]{3,2,1,0:T(8,128)S(1)}, u32[]{:S(2)}, u32[]{:S(2)}) collective-permute-start(f32[4,10,10,1]{3,2,1,0:T(8,128)S(1)} %get-tuple-element.356), channel_id=1, source_target_pairs={{0,1},{1,2},{2,3},{4,5},{5,6},{6,7},{8,9},{9,10},{10,11},{12,13},{... | collective-permute-start | bytes 4808 | tf_op jit(solution)/shard_map/ppermute | solution.py:24
  65.8 8.4 %collective-permute-start.11 = (f32[4,10,10,1]{3,2,1,0:T(8,128)S(1)}, f32[4,10,10,1]{3,2,1,0:T(8,128)S(1)}, u32[]{:S(2)}, u32[]{:S(2)}) collective-permute-start(f32[4,10,10,1]{3,2,1,0:T(8,128)S(1)} %get-tuple-element.355), channel_id=1, source_target_pairs={{1,0},{2,1},{3,2},{5,4},{6,5},{7,6},{9,8},{10,9},{11,10},{13,12},{... | collective-permute-start | bytes 4808 | tf_op jit(solution)/shard_map/ppermute | solution.py:26
  81.1 4.5 %collective-permute-start.12 = (f32[4,1,8,128]{3,2,1,0:T(8,128)S(1)}, f32[4,1,8,128]{3,2,1,0:T(8,128)S(1)}, u32[]{:S(2)}, u32[]{:S(2)}) collective-permute-start(f32[4,1,8,128]{3,2,1,0:T(8,128)S(1)} %get-tuple-element.369), channel_id=1, source_target_pairs={{0,8},{8,16},{16,24},{1,9},{9,17},{17,25},{2,10},{10,18},{18,26},{... | collective-permute-start | bytes 49160 | tf_op jit(solution)/shard_map/ppermute | solution.py:24
  84.3 4.5 %collective-permute-start.13 = (f32[4,1,8,128]{3,2,1,0:T(8,128)S(1)}, f32[4,1,8,128]{3,2,1,0:T(8,128)S(1)}, u32[]{:S(2)}, u32[]{:S(2)}) collective-permute-start(f32[4,1,8,128]{3,2,1,0:T(8,128)S(1)} %get-tuple-element.370), channel_id=1, source_target_pairs={{8,0},{16,8},{24,16},{9,1},{17,9},{25,17},{10,2},{18,10},{26,18},{... | collective-permute-start | bytes 49160 | tf_op jit(solution)/shard_map/ppermute | solution.py:26
  88.8 2.7 %collective-permute-start.14 = (f32[4,10,1,128]{3,2,1,0:T(1,128)S(1)}, f32[4,10,1,128]{3,2,1,0:T(1,128)S(1)}, u32[]{:S(2)}, u32[]{:S(2)}) collective-permute-start(f32[4,10,1,128]{3,2,1,0:T(1,128)S(1)} %get-tuple-element.361), channel_id=1, source_target_pairs={{0,4},{1,5},{2,6},{3,7},{8,12},{9,13},{10,14},{11,15},{16,20},{17,... | collective-permute-start | bytes 61448 | tf_op jit(solution)/shard_map/ppermute | solution.py:24
  90.2 4.5 %collective-permute-start.15 = (f32[4,10,1,128]{3,2,1,0:T(1,128)S(1)}, f32[4,10,1,128]{3,2,1,0:T(1,128)S(1)}, u32[]{:S(2)}, u32[]{:S(2)}) collective-permute-start(f32[4,10,1,128]{3,2,1,0:T(1,128)S(1)} %get-tuple-element.362), channel_id=1, source_target_pairs={{4,0},{5,1},{6,2},{7,3},{12,8},{13,9},{14,10},{15,11},{20,16},{21,... | collective-permute-start | bytes 61448 | tf_op jit(solution)/shard_map/ppermute | solution.py:26
  94.9 8.6 %collective-permute-start.16 = (f32[4,10,10,1]{3,2,1,0:T(8,128)S(1)}, f32[4,10,10,1]{3,2,1,0:T(8,128)S(1)}, u32[]{:S(2)}, u32[]{:S(2)}) collective-permute-start(f32[4,10,10,1]{3,2,1,0:T(8,128)S(1)} %get-tuple-element.354), channel_id=1, source_target_pairs={{0,1},{1,2},{2,3},{4,5},{5,6},{6,7},{8,9},{9,10},{10,11},{12,13},{... | collective-permute-start | bytes 4808 | tf_op jit(solution)/shard_map/ppermute | solution.py:24
  99.5 8.4 %collective-permute-start.17 = (f32[4,10,10,1]{3,2,1,0:T(8,128)S(1)}, f32[4,10,10,1]{3,2,1,0:T(8,128)S(1)}, u32[]{:S(2)}, u32[]{:S(2)}) collective-permute-start(f32[4,10,10,1]{3,2,1,0:T(8,128)S(1)} %get-tuple-element.353), channel_id=1, source_target_pairs={{1,0},{2,1},{3,2},{5,4},{6,5},{7,6},{9,8},{10,9},{11,10},{13,12},{... | collective-permute-start | bytes 4808 | tf_op jit(solution)/shard_map/ppermute | solution.py:26
  114.8 3.0 %collective-permute-start.18 = (f32[4,1,8,128]{3,2,1,0:T(8,128)S(1)}, f32[4,1,8,128]{3,2,1,0:T(8,128)S(1)}, u32[]{:S(2)}, u32[]{:S(2)}) collective-permute-start(f32[4,1,8,128]{3,2,1,0:T(8,128)S(1)} %get-tuple-element.367), channel_id=1, source_target_pairs={{0,8},{8,16},{16,24},{1,9},{9,17},{17,25},{2,10},{10,18},{18,26},{... | collective-permute-start | bytes 49160 | tf_op jit(solution)/shard_map/ppermute | solution.py:24
  116.4 4.5 %collective-permute-start.19 = (f32[4,1,8,128]{3,2,1,0:T(8,128)S(1)}, f32[4,1,8,128]{3,2,1,0:T(8,128)S(1)}, u32[]{:S(2)}, u32[]{:S(2)}) collective-permute-start(f32[4,1,8,128]{3,2,1,0:T(8,128)S(1)} %get-tuple-element.368), channel_id=1, source_target_pairs={{8,0},{16,8},{24,16},{9,1},{17,9},{25,17},{10,2},{18,10},{26,18},{... | collective-permute-start | bytes 49160 | tf_op jit(solution)/shard_map/ppermute | solution.py:26
  120.9 2.7 %collective-permute-start.20 = (f32[4,10,1,128]{3,2,1,0:T(1,128)S(1)}, f32[4,10,1,128]{3,2,1,0:T(1,128)S(1)}, u32[]{:S(2)}, u32[]{:S(2)}) collective-permute-start(f32[4,10,1,128]{3,2,1,0:T(1,128)S(1)} %get-tuple-element.359), channel_id=1, source_target_pairs={{0,4},{1,5},{2,6},{3,7},{8,12},{9,13},{10,14},{11,15},{16,20},{17,... | collective-permute-start | bytes 61448 | tf_op jit(solution)/shard_map/ppermute | solution.py:24
  122.3 4.5 %collective-permute-start.21 = (f32[4,10,1,128]{3,2,1,0:T(1,128)S(1)}, f32[4,10,1,128]{3,2,1,0:T(1,128)S(1)}, u32[]{:S(2)}, u32[]{:S(2)}) collective-permute-start(f32[4,10,1,128]{3,2,1,0:T(1,128)S(1)} %get-tuple-element.360), channel_id=1, source_target_pairs={{4,0},{5,1},{6,2},{7,3},{12,8},{13,9},{14,10},{15,11},{20,16},{21,... | collective-permute-start | bytes 61448 | tf_op jit(solution)/shard_map/ppermute | solution.py:26
  127.0 8.6 %collective-permute-start.22 = (f32[4,10,10,1]{3,2,1,0:T(8,128)S(1)}, f32[4,10,10,1]{3,2,1,0:T(8,128)S(1)}, u32[]{:S(2)}, u32[]{:S(2)}) collective-permute-start(f32[4,10,10,1]{3,2,1,0:T(8,128)S(1)} %get-tuple-element.352), channel_id=1, source_target_pairs={{0,1},{1,2},{2,3},{4,5},{5,6},{6,7},{8,9},{9,10},{10,11},{12,13},{... | collective-permute-start | bytes 4808 | tf_op jit(solution)/shard_map/ppermute | solution.py:24
  131.7 8.4 %collective-permute-start.23 = (f32[4,10,10,1]{3,2,1,0:T(8,128)S(1)}, f32[4,10,10,1]{3,2,1,0:T(8,128)S(1)}, u32[]{:S(2)}, u32[]{:S(2)}) collective-permute-start(f32[4,10,10,1]{3,2,1,0:T(8,128)S(1)} %get-tuple-element.351), channel_id=1, source_target_pairs={{1,0},{2,1},{3,2},{5,4},{6,5},{7,6},{9,8},{10,9},{11,10},{13,12},{... | collective-permute-start | bytes 4808 | tf_op jit(solution)/shard_map/ppermute | solution.py:26
where the time goes:
time: 148 us; the launch traced here: 147 us
  starting transfers between devices  58.3 us (39%)
  waiting for transfers between devices  50.8 us (34%)
  other arithmetic  32.5 us (22%)
  local copies, waits for them, and re-layouts  4.11 us (3%)
  between operations  1.78 us (1%)
    ppermute x12, waiting for transfers between devices, with_halo(): lax.ppermute(head, axis, [((i + 1) % count, i) for i in range(ends)])  43.1 us
    ppermute x12, starting transfers between devices, with_halo(): lax.ppermute(tail, axis, [(i, (i + 1) % count) for i in range(ends)])  39.6 us
    ppermute x12, starting transfers between devices, with_halo(): lax.ppermute(head, axis, [((i + 1) % count, i) for i in range(ends)])  18.7 us
    sub x24, other arithmetic, project(): (1.5 if i == j else 0.0) - 0.5 * sum((rotate[k][i] * rotate[k][j] for k i...  10.1 us
    ppermute x12, waiting for transfers between devices, with_halo(): lax.ppermute(tail, axis, [(i, (i + 1) % count) for i in range(ends)])  7.64 us
    mul x24, other arithmetic, project(): welem * (deform[c][d] - rotate[c][d])  5.75 us
    broadcast_in_dim x1, other arithmetic, node_halo(): joined = jnp.concatenate([disp, weights[None]], axis=0)  4.89 us
    concatenate x16, other arithmetic, with_halo(): jnp.concatenate([lax.ppermute(tail, axis, [(i, (i + 1) % count) for i in...  3.9 us
  transfers between devices with their start and end apart: 24, of which 16 were waited for; matrix products, arithmetic and copies ran while one was open for 0% of the time, Pallas kernels for 0%

commit v1 on v0

v1 whole, which is shorter than its diff:
```python
import functools
import math

import jax
import jax.numpy as jnp
from jax import lax
from jax.experimental import pallas as pl
from jax.experimental.pallas import tpu as pltpu
from jax.sharding import PartitionSpec as P

ITERS = 4
POLAR_STEPS = 6
MATS = 8
RELAX = 0.6
RADIUS = 0.9

HALO = ITERS
SCALE = 0.25 / math.sqrt(2.0)
UNIT = 1.0 / math.sqrt(2.0)
CH = 8
W_CH = 6
FREE_CH = 7
GROUPS = 4
SPAN = 32

VM = pl.BlockSpec(memory_space=pltpu.VMEM)
SM = pl.BlockSpec(memory_space=pltpu.SMEM)


def omegas():
    values = [1.0]
    for step in range(1, ITERS):
        if step == 1:
            values.append(2.0 / (2.0 - RADIUS * RADIUS))
        else:
            values.append(4.0 / (4.0 - RADIUS * RADIUS * values[-1]))
    return values


def lane_ids():
    return lax.broadcasted_iota(jnp.int32, (8, 128), 1)


def sub_ids():
    return lax.broadcasted_iota(jnp.int32, (8, 128), 0)


def roll_z(value, amount):
    amount = amount % 128
    return value if amount == 0 else pltpu.roll(value, amount, 1)


def next_x(pair):
    return (pair[1], pltpu.roll(pair[0], 7, 0))


def prev_x(pair):
    return (pltpu.roll(pair[1], 1, 0), pair[0])


def add2(a, b):
    return tuple(x + y for x, y in zip(a, b))


def sub2(a, b):
    return tuple(x - y for x, y in zip(a, b))


def gradient_row(vrow):
    out = []
    for pair in vrow:
        ahead = tuple(roll_z(t, -1) for t in pair)
        sz = add2(pair, ahead)
        dz = sub2(ahead, pair)
        nsz = next_x(sz)
        out.append((add2(sz, nsz), sub2(nsz, sz), add2(dz, next_x(dz))))
    return out


def polar_stress(f, weight):
    def gram(z):
        return {
            (i, j): z[0][i] * z[0][j] + z[1][i] * z[1][j] + z[2][i] * z[2][j]
            for i in range(3)
            for j in range(i, 3)
        }

    def apply(z, diag, off):
        rows = []
        for c in range(3):
            row = []
            for d in range(3):
                value = z[c][d] * diag[d]
                for j in range(3):
                    if j != d:
                        value = value - z[c][j] * off[(min(j, d), max(j, d))]
                row.append(value)
            rows.append(row)
        return rows

    g = gram(f)
    trace = g[(0, 0)] + g[(1, 1)] + g[(2, 2)]
    s = jnp.minimum(lax.rsqrt(trace * (2.0 / 3.0)), 1.0)
    cube = s * s * s
    base = 1.5 * s
    z = apply(
        f,
        [base - cube * g[(i, i)] for i in range(3)],
        {key: cube * g[key] for key in ((0, 1), (0, 2), (1, 2))},
    )
    for _ in range(POLAR_STEPS - 1):
        g = gram(z)
        z = apply(z, [1.5 - g[(i, i)] for i in range(3)], g)
    return [[weight * (z[c][d] - f[c][d]) for d in range(3)] for c in range(3)]


def deform_rows(low, high):
    out = []
    for c in range(3):
        row = [
            add2(low[c][1], high[c][1]),
            sub2(high[c][0], low[c][0]),
            add2(low[c][2], high[c][2]),
        ]
        row[c] = tuple(t + UNIT for t in row[c])
        out.append(row)
    return out


def stress_row(f, weight):
    tiles = [
        polar_stress([[f[c][d][t] for d in range(3)] for c in range(3)], weight[t])
        for t in range(2)
    ]
    return [[(tiles[0][c][d], tiles[1][c][d]) for d in range(3)] for c in range(3)]


def force_parts(now, before):
    out = []
    for c in range(3):
        a = add2(now[c][0], before[c][0])
        b = sub2(now[c][1], before[c][1])
        e = add2(now[c][2], before[c][2])
        left = add2(add2(a, b), prev_x(sub2(b, a)))
        right = add2(e, prev_x(e))
        out.append((add2(left, right), sub2(left, right)))
    return out


def update_row(part, v, vin, prev, g, omega):
    new = []
    for c in range(3):
        row = []
        for t in range(2):
            force = part[c][0][t] + roll_z(part[c][1][t], 1)
            y = v[c][t] - g[t] * ((v[c][t] - vin[c][t]) + force)
            row.append(prev[c][t] + omega * (y - prev[c][t]))
        new.append(tuple(row))
    return new


def omega_at(step):
    values = omegas()
    out = jnp.float32(values[0])
    for index in range(1, ITERS):
        out = jnp.where(step == index, jnp.float32(values[index]), out)
    return out


class Shape:
    def __init__(self, mesh, size):
        self.n = tuple(mesh.shape[a] for a in ("gx", "gy", "gz"))
        self.size = size
        self.mirror = self.n[1] == 2
        self.own = 0 if self.mirror else HALO
        self.rows = size[1] + HALO * (1 if self.mirror else 2)
        self.erows = self.rows // GROUPS


def even(axis):
    return lax.rem(lax.axis_index(axis), 2) == 0


def pack_faces(first, second):
    upper = sub_ids() >= HALO
    low = jnp.where(upper, pltpu.roll(second, HALO, 0), first)
    high = jnp.where(upper, second, pltpu.roll(first, HALO, 0))
    return low, high


def prep_kernel(shape, start, inert, mat, pin, stiff, own, ysend, xsend, xysend):
    sx, sy, sz = shape.size
    gx, gy, gz = (lax.axis_index(a) for a in ("gx", "gy", "gz"))
    flip = (gy == 1) if shape.mirror else False
    sign = jnp.where(flip, -1.0, 1.0).astype(jnp.float32) if shape.mirror else jnp.float32(1.0)
    inside = (sub_ids() + gx * sx < shape.n[0] * sx - 1) & (
        lane_ids() + gz * sz < shape.n[2] * sz - 1
    )
    levels = [stiff[i] * (1.0 / 16.0) for i in range(MATS)]
    own[W_CH, sy] = jnp.zeros((8, 128), jnp.float32)
    for r in range(sy):
        at = pl.ds(r, sx, stride=sy)
        fixed = pin[at, :] > 0
        kind = mat[at, :]
        weight = jnp.zeros((8, 128), jnp.float32)
        for index in range(MATS):
            weight = jnp.where(kind == index, levels[index], weight)
        valid = inside & (r + gy * sy < shape.n[1] * sy - 1)
        weight = jnp.where(valid, weight, 0.0)
        node = jnp.where(flip, sy - 1 - r, r) + 1 if shape.mirror else r + 1
        cell = jnp.where(flip, sy - 2 - r, r) + 1 if shape.mirror else r + 1
        for c in range(3):
            factor = SCALE * sign if c == 1 else SCALE
            goal = inert[c, at, :] * factor
            own[c, node] = jnp.where(fixed, goal, start[c, at, :] * factor)
            own[3 + c, node] = goal
        own[W_CH, cell] = weight
        own[FREE_CH, node] = jnp.where(fixed, 0.0, 1.0)
    ex = even("gx")
    for c in range(CH):
        for k in range(sy // 2):
            low, high = pack_faces(own[c, 2 * k + 1], own[c, 2 * k + 2])
            xsend[0][c, k] = jnp.where(ex, high, low)
            xsend[1][c, k] = jnp.where(ex, low, high)
        for side in range(len(ysend)):
            rows = []
            for d in range(HALO):
                if shape.mirror:
                    node = sy - 1 - d
                    if c == W_CH:
                        node = node - jnp.where(flip, 1, 0)
                else:
                    up = even("gy") if side == 0 else jnp.logical_not(even("gy"))
                    node = jnp.where(up, sy - HALO + d, d)
                rows.append(own[c, node + 1])
                ysend[side][c, d] = rows[-1]
            for k in range(HALO // 2):
                low, high = pack_faces(rows[2 * k], rows[2 * k + 1])
                xysend[2 * side][c, k] = jnp.where(ex, high, low)
                xysend[2 * side + 1][c, k] = jnp.where(ex, low, high)


def join_kernel(shape, own, yrecv, xrecv, xyrecv, full, zsend, nat):
    sx, sy, sz = shape.size
    rows = shape.rows
    ex, ez = even("gx"), even("gz")
    flip = (lax.axis_index("gy") == 1) if shape.mirror else False

    def put(c, row, low, mid, high):
        nat[c, row, 0:HALO] = low
        nat[c, row, HALO : HALO + sx] = mid
        nat[c, row, HALO + sx :] = high

    for c in range(CH):
        turned = shape.mirror and c in (1, 4)
        for k in range(sy // 2):
            a, b = xrecv[0][c, k], xrecv[1][c, k]
            low, high = jnp.where(ex, b, a), jnp.where(ex, a, b)
            for h in range(2):
                part = slice(HALO * h, HALO * h + HALO)
                put(c, shape.own + 2 * k + h, low[part], own[c, 2 * k + h + 1], high[part])
        for side in range(2 if not shape.mirror else 1):
            for k in range(HALO // 2):
                if shape.mirror:
                    a, b = xyrecv[0][c, k], xyrecv[1][c, k]
                    mids = [yrecv[0][c, 2 * k + h] for h in range(2)]
                    if turned:
                        a, b = -a, -b
                        mids = [-t for t in mids]
                else:
                    lower = even("gy") if side else jnp.logical_not(even("gy"))
                    a, b = (jnp.where(lower, xyrecv[i][c, k], xyrecv[2 + i][c, k]) for i in range(2))
                    mids = [
                        jnp.where(lower, yrecv[0][c, 2 * k + h], yrecv[1][c, 2 * k + h])
                        for h in range(2)
                    ]
                low, high = jnp.where(ex, b, a), jnp.where(ex, a, b)
                for h in range(2):
                    part = slice(HALO * h, HALO * h + HALO)
                    d = 2 * k + h
                    if shape.mirror:
                        row = sy + d
                        if c == W_CH:
                            row = row - jnp.where(flip, 1, 0)
                    else:
                        row = d + side * (HALO + sy)
                    put(c, row, low[part], mids[h], high[part])
        if c == W_CH:
            nat[c, rows - 1] = jnp.zeros((sx + 2 * HALO, 128), jnp.float32)
    slot = lane_ids() // HALO
    for m in range(shape.erows):
        for t in range(2):
            up = jnp.zeros((8, 128), jnp.float32)
            down = jnp.zeros((8, 128), jnp.float32)
            for g in range(GROUPS):
                for c in range(CH):
                    tile = nat[c, g * shape.erows + m, pl.ds(t, 8, stride=2), :]
                    full[c, g * shape.erows + m, t] = tile
                    place = slot == (SPAN // HALO) * g + c
                    to = SPAN * g + HALO * c
                    up = jnp.where(place, roll_z(tile, to - (sz - HALO)), up)
                    down = jnp.where(place, roll_z(tile, to), down)
            zsend[0][m, t] = jnp.where(ez, up, down)
            zsend[1][m, t] = jnp.where(ez, down, up)


def load_row(ref, row, channels=range(3)):
    return [(ref[c, row, 0], ref[c, row, 1]) for c in channels]


def step_size(now, before, free):
    total = add2(now, before)
    total = add2(total, prev_x(total))
    return tuple(
        RELAX * f / (1.0 + 3.0 * (t + roll_z(t, 1))) for t, f in zip(total, free)
    )


def main_kernel(shape, full, v, prev, gsize, grad, stress, part):
    rows = shape.rows
    zero = jnp.zeros((8, 128), jnp.float32)
    for row in range(rows):
        for c in range(3):
            for t in range(2):
                tile = full[c, row, t]
                v[c, row + 1, t] = tile
                prev[c, row + 1, t] = tile
        now = load_row(full, row, (W_CH,))[0]
        before = load_row(full, row - 1, (W_CH,))[0] if row else (zero, zero)
        g = step_size(now, before, load_row(full, row, (FREE_CH,))[0])
        for t in range(2):
            gsize[row + 1, t] = g[t]
    for i in range(9):
        for t in range(2):
            stress[i, 0, t] = zero
    for c in range(3):
        for t in range(2):
            v[c, 0, t] = zero
            v[c, rows + 1, t] = zero
            prev[c, 0, t] = zero
    for t in range(2):
        gsize[0, t] = zero

    def put_gradient(row, value):
        for c in range(3):
            for kind in range(3):
                for t in range(2):
                    grad[3 * c + kind, row, t] = value[c][kind][t]

    def get9(ref, row):
        return [[(ref[3 * c + k, row, 0], ref[3 * c + k, row, 1]) for k in range(3)] for c in range(3)]

    def iteration(step, carry):
        omega = omega_at(step)
        first = 0 if shape.mirror else step
        last = rows - 1 - step
        put_gradient(first, gradient_row(load_row(v, first + 1)))
        put_gradient(first + 1, gradient_row(load_row(v, first + 2)))

        def body(j, carry):
            ahead = load_row(v, j + 3)
            low, high = get9(grad, j), get9(grad, j + 1)
            weight = load_row(full, j, (W_CH,))[0]
            before = get9(stress, j)
            held = [
                tuple((part[2 * c + i, j, 0], part[2 * c + i, j, 1]) for i in range(2))
                for c in range(3)
            ]
            old = load_row(v, j)
            oldest = load_row(prev, j)
            goal = load_row(full, max(j - 1, 0), (3, 4, 5))
            g = (gsize[j, 0], gsize[j, 1])

            after = gradient_row(ahead)
            now = stress_row(deform_rows(low, high), weight)
            parts = force_parts(now, before)
            new = update_row(held, old, goal, oldest, g, omega)

            put_gradient(j + 2, after)
            for c in range(3):
                for t in range(2):
                    for d in range(3):
                        stress[3 * c + d, j + 1, t] = now[c][d][t]
                    for i in range(2):
                        part[2 * c + i, j + 1, t] = parts[c][i][t]
                    prev[c, j, t] = old[c][t]
                    v[c, j, t] = new[c][t]
            return carry

        for j in range(first, last):
            body(j, 0)
        held = [
            tuple((part[2 * c + i, last, 0], part[2 * c + i, last, 1]) for i in range(2))
            for c in range(3)
        ]
        old = load_row(v, last)
        new = update_row(
            held,
            old,
            load_row(full, last - 1, (3, 4, 5)),
            load_row(prev, last),
            (gsize[last, 0], gsize[last, 1]),
            omega,
        )
        for c in range(3):
            for t in range(2):
                prev[c, last, t] = old[c][t]
                v[c, last, t] = new[c][t]
        return carry

    for step in range(ITERS):
        iteration(step, 0)


def edge_kernel(shape, full, main, zrecv0, zrecv1, out, v, prev, goal, gsize, stiff, tiles):
    sx, sy, sz = shape.size
    erows = shape.erows
    ez = even("gz")
    lane = lane_ids()
    within = lane % SPAN
    half = SPAN // 2

    def window(c, m, t):
        value = jnp.zeros((8, 128), jnp.float32)
        for g in range(GROUPS):
            tile = full[c, g * erows + m, t]
            base = SPAN * g
            value = jnp.where(
                (lane >= base + HALO) & (lane < base + half), roll_z(tile, base + HALO), value
            )
            value = jnp.where(
                (lane >= base + half) & (lane < base + SPAN - HALO),
                roll_z(tile, base + SPAN - HALO - sz),
                value,
            )
        return value

    for m in range(erows):
        for t in range(2):
            a, b = zrecv0[m, t], zrecv1[m, t]
            low, high = jnp.where(ez, b, a), jnp.where(ez, a, b)

            def extended(c):
                value = window(c, m, t)
                value = jnp.where(within < HALO, roll_z(low, -HALO * c), value)
                return jnp.where(
                    within >= SPAN - HALO, roll_z(high, SPAN - HALO - HALO * c), value
                )

            for c in range(3):
                value = extended(c)
                v[c, m, t] = value
                prev[c, m, t] = value
                goal[c, m, t] = extended(3 + c)
            stiff[m, t] = extended(W_CH)
            gsize[m, t] = extended(FREE_CH)
    weights = [(stiff[m, 0], stiff[m, 1]) for m in range(erows)]
    behind = tuple(roll_z(t, SPAN) for t in weights[-1])
    for m in range(erows):
        g = step_size(weights[m], weights[m - 1] if m else behind, (gsize[m, 0], gsize[m, 1]))
        for t in range(2):
            gsize[m, t] = g[t]

    def iteration(step, carry):
        omega = omega_at(step)
        grads = [gradient_row(load_row(v, m)) for m in range(erows)]
        grads.append([[tuple(roll_z(t, -SPAN) for t in pair) for pair in row] for row in grads[0]])
        stress = [None] * erows
        for m in [erows - 1] + list(range(erows - 1)):
            stress[m] = stress_row(
                deform_rows(grads[m], grads[m + 1]), (stiff[m, 0], stiff[m, 1])
            )
        wrapped = [[tuple(roll_z(t, SPAN) for t in pair) for pair in row] for row in stress[-1]]
        for m in range(erows):
            parts = force_parts(stress[m], stress[m - 1] if m else wrapped)
            old = load_row(v, m)
            new = update_row(
                parts, old, load_row(goal, m), load_row(prev, m), (gsize[m, 0], gsize[m, 1]), omega
            )
            for c in range(3):
                for t in range(2):
                    prev[c, m, t] = old[c][t]
                    v[c, m, t] = new[c][t]
        return carry

    lax.fori_loop(0, ITERS, iteration, 0)
    flip = (lax.axis_index("gy") == 1) if shape.mirror else False
    for r in range(sy):
        row = shape.own + r
        g, m = divmod(row, erows)
        base = SPAN * g
        for c in range(3):
            factor = 1.0 / SCALE
            if shape.mirror and c == 1:
                factor = jnp.where(flip, -factor, factor).astype(jnp.float32)
            for t in range(2):
                edge = v[c, m, t]
                value = main[c, row + 1, t]
                value = jnp.where(lane < HALO, roll_z(edge, -(base + HALO)), value)
                value = jnp.where(
                    lane >= sz - HALO, roll_z(edge, sz - HALO - (base + SPAN - 2 * HALO)), value
                )
                tiles[pl.ds(t, 8, stride=2), :] = value * factor
            place = jnp.where(flip, sy - 1 - r, r) if shape.mirror else r
            out[c, pl.ds(place, sx, stride=sy), :] = tiles[HALO : HALO + sx]


def swap(size, parity):
    pairs = []
    for i in range(size):
        j = i + 1 if i % 2 == parity else i - 1
        if 0 <= j < size:
            pairs.append((i, j))
    return pairs


def swap2(nx, px, ny, py):
    return [
        (i * ny + j, a * ny + b)
        for i, a in swap(nx, px)
        for j, b in swap(ny, py)
    ]


def f32(*dims):
    return jax.ShapeDtypeStruct(dims, jnp.float32)


def scratch(*dims):
    return pltpu.VMEM(dims, jnp.float32)


def call(body, outs, args, scratches=(), specs=None):
    return pl.pallas_call(
        body,
        out_shape=outs,
        in_specs=specs or [VM] * len(args),
        out_specs=jax.tree.map(lambda _: VM, outs),
        scratch_shapes=list(scratches),
        compiler_params=pltpu.CompilerParams(vmem_limit_bytes=40 * 1024 * 1024),
        cost_estimate=pl.CostEstimate(flops=2_000_000, bytes_accessed=100_000, transcendentals=0),
    )(*args)


def per_device(mesh, start_disp, inertial, material, pinned, stiffness):
    shape = Shape(mesh, material.shape)
    sx, sy, sz = shape.size
    nx, ny, nz = shape.n
    sides = 1 if shape.mirror else 2
    rows, erows = shape.rows, shape.erows

    def prep(start, inert, mat, pin, stiff, own, *rest):
        prep_kernel(
            shape, start, inert, mat, pin, stiff, own,
            rest[2 : 2 + sides], rest[:2], rest[2 + sides :],
        )

    outs = prep_outs = [f32(CH, sy + 1, sx, sz)]
    outs += [f32(CH, sy // 2, 8, sz)] * 2 + [f32(CH, HALO, sx, sz)] * sides
    outs += [f32(CH, HALO // 2, 8, sz)] * (2 * sides)
    own, *sent = call(
        prep,
        outs,
        (
            start_disp.reshape(3, sx * sy, sz),
            inertial.reshape(3, sx * sy, sz),
            material.reshape(sx * sy, sz),
            pinned.reshape(sx * sy, sz),
            stiffness,
        ),
        specs=[VM] * 4 + [SM],
    )
    recv = [lax.ppermute(sent[p], "gx", swap(nx, p)) for p in range(2)]
    recv += [lax.ppermute(sent[2 + p], "gy", swap(ny, p)) for p in range(sides)]
    recv += [
        lax.ppermute(sent[2 + sides + 2 * q + p], ("gx", "gy"), swap2(nx, p, ny, q))
        for q in range(sides)
        for p in range(2)
    ]

    def join(own, *rest):
        x, rest = rest[:2], rest[2:]
        y, rest = rest[:sides], rest[sides:]
        xy, rest = rest[: 2 * sides], rest[2 * sides :]
        full, z0, z1, nat = rest
        join_kernel(shape, own, y, x, xy, full, (z0, z1), nat)

    full, z0, z1 = call(
        join,
        [f32(CH, rows, 2, 8, sz), f32(erows, 2, 8, sz), f32(erows, 2, 8, sz)],
        (own, *recv),
        [scratch(CH, rows, sx + 2 * HALO, sz)],
    )
    z0 = lax.ppermute(z0, "gz", swap(nz, 0))
    z1 = lax.ppermute(z1, "gz", swap(nz, 1))
    (main,) = call(
        functools.partial(main_kernel, shape),
        [f32(3, rows + 2, 2, 8, sz)],
        (full,),
        [
            scratch(3, rows + 2, 2, 8, sz),
            scratch(rows + 2, 2, 8, sz),
            scratch(9, rows + 2, 2, 8, sz),
            scratch(9, rows + 2, 2, 8, sz),
            scratch(6, rows + 2, 2, 8, sz),
        ],
    )
    (out,) = call(
        functools.partial(edge_kernel, shape),
        [f32(3, sx * sy, sz)],
        (full, main, z0, z1),
        [
            scratch(3, erows, 2, 8, sz),
            scratch(3, erows, 2, 8, sz),
            scratch(3, erows, 2, 8, sz),
            scratch(erows, 2, 8, sz),
            scratch(erows, 2, 8, sz),
            scratch(2 * 8, sz),
        ],
    )
    return out.reshape(3, sx, sy, sz)


def solution(mesh):
    placed = (
        P(None, "gx", "gy", "gz"),
        P(None, "gx", "gy", "gz"),
        P("gx", "gy", "gz"),
        P("gx", "gy", "gz"),
        P(),
    )
    return jax.shard_map(
        functools.partial(per_device, mesh),
        mesh=mesh,
        in_specs=placed,
        out_specs=P(None, "gx", "gy", "gz"),
        check_vma=False,
    )
```

time: 148 us -> 33.7 us (0.23)
  the two profiles are of different devices: /device:TPU:1 before, /device:TPU:9 now
where the time goes in v1:
time: 33.7 us; the launch traced here: 33.4 us
  starting transfers between devices  12.9 us (38%)
  Pallas kernels  11.9 us (35%)
  waiting for transfers between devices  4.6 us (14%)
  local copies, waits for them, and re-layouts  3.95 us (12%)
    pallas_call x4, Pallas kernels, call(): pl.pallas_call(body, out_shape=outs, in_specs=specs or [VM] * len(args),...  11.9 us
    ppermute x2, waiting for transfers between devices, per_device(): lax.ppermute(sent[2 + sides + 2 * q + p], ('gx', 'gy'), swap2(nx, p, ny, q))  4.59 us
    ppermute x2, starting transfers between devices, per_device(): recv = [lax.ppermute(sent[p], 'gx', swap(nx, p)) for p in range(2)]  4.55 us
    unnamed x10, local copies, waits for them, and re-layouts  3.95 us
    ppermute x1, starting transfers between devices, per_device(): z1 = lax.ppermute(z1, 'gz', swap(nz, 1))  3.02 us
    ppermute x1, starting transfers between devices, per_device(): z0 = lax.ppermute(z0, 'gz', swap(nz, 0))  2.12 us
    ppermute x2, starting transfers between devices, per_device(): lax.ppermute(sent[2 + sides + 2 * q + p], ('gx', 'gy'), swap2(nx, p, ny, q))  1.91 us
    ppermute x1, starting transfers between devices, per_device(): recv += [lax.ppermute(sent[2 + p], 'gy', swap(ny, p)) for p in range(sides)]  1.3 us
  transfers between devices with their start and end apart: 7, of which 2 were waited for; matrix products, arithmetic and copies ran while one was open for 0% of the time, Pallas kernels for 19%

profile of v1, /device:TPU:9, one launch (start us, length us, event | category | flops | bytes accessed | tf_op | source)
XLA Modules:
  0.0 33.4 jit_solution(10366148480525721663)
XLA Ops:
  0.0 0.0 copy-start.4
  0.0 0.7 %copy-done.4 = f32[8]{0:T(128)S(1)} copy-done((f32[8]{0:T(128)S(1)}, f32[8]{0:T(128)}, u32[]{:S(2)}) %copy-start.4) | copy-done | bytes 56
  0.7 0.0 copy-start
  0.7 0.9 %copy-done = f32[3,8,8,128]{3,2,1,0:T(8,128)S(1)} copy-done((f32[3,8,8,128]{3,2,1,0:T(8,128)S(1)}, f32[3,8,8,128]{3,2,1,0:T(8,128)}, u32[]{:S(2)}) %copy-start) | copy-done | bytes 98328
  1.5 0.0 copy-start.1
  1.6 0.9 %copy-done.1 = f32[3,8,8,128]{3,2,1,0:T(8,128)S(1)} copy-done((f32[3,8,8,128]{3,2,1,0:T(8,128)S(1)}, f32[3,8,8,128]{3,2,1,0:T(8,128)}, u32[]{:S(2)}) %copy-start.1) | copy-done | bytes 98328
  2.4 0.0 copy-start.2
  2.4 0.8 %copy-done.2 = s32[8,8,128]{2,1,0:T(8,128)S(1)} copy-done((s32[8,8,128]{2,1,0:T(8,128)S(1)}, s32[8,8,128]{2,1,0:T(8,128)}, u32[]{:S(2)}) %copy-start.2) | copy-done | bytes 32792
  3.2 0.0 copy-start.3
  3.2 0.8 %copy-done.3 = s32[8,8,128]{2,1,0:T(8,128)S(1)} copy-done((s32[8,8,128]{2,1,0:T(8,128)S(1)}, s32[8,8,128]{2,1,0:T(8,128)}, u32[]{:S(2)}) %copy-start.3) | copy-done | bytes 32792
  4.0 0.7 %shard_map.55 = (f32[8,9,8,128]{3,2,1,0:T(8,128)S(1)}, f32[8,4,8,128]{3,2,1,0:T(8,128)S(1)}, f32[8,4,8,128]{3,2,1,0:T(8,128)S(1)}, f32[8,4,8,128]{3,2,1,0:T(8,12...) custom-call(f32[3,64,128]{2,1,0:T(8,128)S(1)} %bitcast.5, f32[3,64,128]{2,1,0:T(8,128)S(1)} %bitcast.6, ...), custom_call_target="tpu_custom_call" | custom-call | flops 2000000 | bytes 100000 | tf_op jit(solution)/shard_map/pallas_call | solution.py:534
  4.6 0.1 collective-permute-start
  4.7 4.5 %collective-permute-start.1 = (f32[8,4,8,128]{3,2,1,0:T(8,128)S(1)}, f32[8,4,8,128]{3,2,1,0:T(8,128)S(1)}, u32[]{:S(2)}, u32[]{:S(2)}) collective-permute-start(f32[8,4,8,128]{3,2,1,0:T(8,128)S(1)} %get-tuple-element.16), channel_id=1, source_target_pairs={{8,16},{16,8},{9,17},{17,9},{10,18},{18,10},{11,19},{19,11},{12,20... | collective-permute-start | bytes 393224 | tf_op jit(solution)/shard_map/ppermute | solution.py:573
  9.2 1.3 %collective-permute-start.2 = (f32[8,4,8,128]{3,2,1,0:T(8,128)S(1)}, f32[8,4,8,128]{3,2,1,0:T(8,128)S(1)}, u32[]{:S(2)}, u32[]{:S(2)}) collective-permute-start(f32[8,4,8,128]{3,2,1,0:T(8,128)S(1)} %get-tuple-element.17), channel_id=1, source_target_pairs={{0,4},{4,0},{1,5},{5,1},{2,6},{6,2},{3,7},{7,3},{8,12},{12,8},{9,1... | collective-permute-start | bytes 393224 | tf_op jit(solution)/shard_map/ppermute | solution.py:574
  10.5 0.0 collective-permute-start.3
  10.5 1.9 %collective-permute-start.4 = (f32[8,2,8,128]{3,2,1,0:T(8,128)S(1)}, f32[8,2,8,128]{3,2,1,0:T(8,128)S(1)}, u32[]{:S(2)}, u32[]{:S(2)}) collective-permute-start(f32[8,2,8,128]{3,2,1,0:T(8,128)S(1)} %get-tuple-element.19), channel_id=1, source_target_pairs={{8,20},{12,16},{16,12},{20,8},{9,21},{13,17},{17,13},{21,9},{10,22... | collective-permute-start | bytes 196616 | tf_op jit(solution)/shard_map/ppermute | solution.py:576
  12.4 2.2 %collective-permute-done.3.rest_3_ = f32[8,2,8,128]{3,2,1,0:T(8,128)S(1)} collective-permute-done((f32[8,2,8,128]{3,2,1,0:T(8,128)S(1)}, f32[8,2,8,128]{3,2,1,0:T(8,128)S(1)}, u32[]{:S(2)}, u32[]{:S(2)}) %collective-permute-start.3) | collective-permute-done | bytes 65568 | tf_op jit(solution)/shard_map/ppermute | solution.py:576
  14.6 2.4 %collective-permute-done.4.rest_4_ = f32[8,2,8,128]{3,2,1,0:T(8,128)S(1)} collective-permute-done((f32[8,2,8,128]{3,2,1,0:T(8,128)S(1)}, f32[8,2,8,128]{3,2,1,0:T(8,128)S(1)}, u32[]{:S(2)}, u32[]{:S(2)}) %collective-permute-start.4) | collective-permute-done | bytes 65568 | tf_op jit(solution)/shard_map/ppermute | solution.py:576
  17.0 0.0 collective-permute-done.rest_0_
  17.0 0.0 collective-permute-done.1.rest_1_
  17.0 0.0 collective-permute-done.2.rest_2_
  17.0 0.5 %shard_map.56 = (f32[8,12,2,8,128]{4,3,2,1,0:T(8,128)S(1)}, f32[3,2,8,128]{3,2,1,0:T(8,128)S(1)}, f32[3,2,8,128]{3,2,1,0:T(8,128)S(1)}) custom-call(f32[8,9,8,128]{3,2,1,0:T(8,128)S(1)} %get-tuple-element.14.own, f32[8,4,8,128]{3,2,1,0:T(8,128)S(1)} %collective-permute-done.rest_0_, f32[8,4,8,128]{3,2,1,0:T(8,128)S(1)} %collective-permute-done.1.rest_1_, ...), custom_call_target="tpu_custom_call" | custom-call | flops 2000000 | bytes 100000 | tf_op jit(solution)/shard_map/pallas_call | solution.py:534
  17.6 2.1 %collective-permute-start.5 = (f32[3,2,8,128]{3,2,1,0:T(8,128)S(1)}, f32[3,2,8,128]{3,2,1,0:T(8,128)S(1)}, u32[]{:S(2)}, u32[]{:S(2)}) collective-permute-start(f32[3,2,8,128]{3,2,1,0:T(8,128)S(1)} %get-tuple-element.21), channel_id=1, source_target_pairs={{0,1},{1,0},{2,3},{3,2},{4,5},{5,4},{6,7},{7,6},{8,9},{9,8},{10,11... | collective-permute-start | bytes 73736 | tf_op jit(solution)/shard_map/ppermute | solution.py:594
  19.7 3.0 %collective-permute-start.6 = (f32[3,2,8,128]{3,2,1,0:T(8,128)S(1)}, f32[3,2,8,128]{3,2,1,0:T(8,128)S(1)}, u32[]{:S(2)}, u32[]{:S(2)}) collective-permute-start(f32[3,2,8,128]{3,2,1,0:T(8,128)S(1)} %get-tuple-element.22), channel_id=1, source_target_pairs={{1,2},{2,1},{5,6},{6,5},{9,10},{10,9},{13,14},{14,13},{17,18},{18,... | collective-permute-start | bytes 73736 | tf_op jit(solution)/shard_map/ppermute | solution.py:595
  22.7 6.4 %shard_map.57.main = f32[3,14,2,8,128]{4,3,2,1,0:T(8,128)S(1)} custom-call(f32[8,12,2,8,128]{4,3,2,1,0:T(8,128)S(1)} %get-tuple-element.20.full), custom_call_target="tpu_custom_call" | custom-call | flops 2000000 | bytes 100000 | tf_op jit(solution)/shard_map/pallas_call | solution.py:534
  29.1 0.0 collective-permute-done.5.zrecv0
  29.1 0.0 collective-permute-done.6.zrecv1
  29.1 4.3 %shard_map.58 = f32[3,64,128]{2,1,0:T(8,128)} custom-call(f32[8,12,2,8,128]{4,3,2,1,0:T(8,128)S(1)} %get-tuple-element.20.full, f32[3,14,2,8,128]{4,3,2,1,0:T(8,128)S(1)} %shard_map.57.main, f32[3,2,8,128]{3,2,1,0:T(8,128)S(1)} %collective-permute-done.5.zrecv0, f32[3,2,8,128]{3,2,1,0:T(8,128)S(1)} %collective-permute-done.6.zrecv1), custom_call_target="tpu_custom_call" | custom-call | flops 2000000 | bytes 100000 | tf_op jit(solution)/shard_map/pallas_call | solution.py:534
Async XLA Ops:
  0.0 0.7 %copy-start.4 = (f32[8]{0:T(128)S(1)}, f32[8]{0:T(128)}, u32[]{:S(2)}) copy-start(f32[8]{0:T(128)} %stiff.1) | copy-start | bytes 100
  0.7 0.9 %copy-start = (f32[3,8,8,128]{3,2,1,0:T(8,128)S(1)}, f32[3,8,8,128]{3,2,1,0:T(8,128)}, u32[]{:S(2)}) copy-start(f32[3,8,8,128]{3,2,1,0:T(8,128)} %param.5) | copy-start | bytes 294916
  1.5 0.9 %copy-start.1 = (f32[3,8,8,128]{3,2,1,0:T(8,128)S(1)}, f32[3,8,8,128]{3,2,1,0:T(8,128)}, u32[]{:S(2)}) copy-start(f32[3,8,8,128]{3,2,1,0:T(8,128)} %param.6) | copy-start | bytes 294916
  2.4 0.8 %copy-start.2 = (s32[8,8,128]{2,1,0:T(8,128)S(1)}, s32[8,8,128]{2,1,0:T(8,128)}, u32[]{:S(2)}) copy-start(s32[8,8,128]{2,1,0:T(8,128)} %param.7) | copy-start | bytes 98308
  3.2 0.8 %copy-start.3 = (s32[8,8,128]{2,1,0:T(8,128)S(1)}, s32[8,8,128]{2,1,0:T(8,128)}, u32[]{:S(2)}) copy-start(s32[8,8,128]{2,1,0:T(8,128)} %param.8) | copy-start | bytes 98308
  4.6 12.4 %collective-permute-start = (f32[8,4,8,128]{3,2,1,0:T(8,128)S(1)}, f32[8,4,8,128]{3,2,1,0:T(8,128)S(1)}, u32[]{:S(2)}, u32[]{:S(2)}) collective-permute-start(f32[8,4,8,128]{3,2,1,0:T(8,128)S(1)} %get-tuple-element.15), channel_id=1, source_target_pairs={{0,8},{8,0},{16,24},{24,16},{1,9},{9,1},{17,25},{25,17},{2,10},{10... | collective-permute-start | bytes 393224 | tf_op jit(solution)/shard_map/ppermute | solution.py:573
  4.7 12.3 %collective-permute-start.1 = (f32[8,4,8,128]{3,2,1,0:T(8,128)S(1)}, f32[8,4,8,128]{3,2,1,0:T(8,128)S(1)}, u32[]{:S(2)}, u32[]{:S(2)}) collective-permute-start(f32[8,4,8,128]{3,2,1,0:T(8,128)S(1)} %get-tuple-element.16), channel_id=1, source_target_pairs={{8,16},{16,8},{9,17},{17,9},{10,18},{18,10},{11,19},{19,11},{12,20... | collective-permute-start | bytes 393224 | tf_op jit(solution)/shard_map/ppermute | solution.py:573
  9.2 7.8 %collective-permute-start.2 = (f32[8,4,8,128]{3,2,1,0:T(8,128)S(1)}, f32[8,4,8,128]{3,2,1,0:T(8,128)S(1)}, u32[]{:S(2)}, u32[]{:S(2)}) collective-permute-start(f32[8,4,8,128]{3,2,1,0:T(8,128)S(1)} %get-tuple-element.17), channel_id=1, source_target_pairs={{0,4},{4,0},{1,5},{5,1},{2,6},{6,2},{3,7},{7,3},{8,12},{12,8},{9,1... | collective-permute-start | bytes 393224 | tf_op jit(solution)/shard_map/ppermute | solution.py:574
  10.5 4.1 %collective-permute-start.3 = (f32[8,2,8,128]{3,2,1,0:T(8,128)S(1)}, f32[8,2,8,128]{3,2,1,0:T(8,128)S(1)}, u32[]{:S(2)}, u32[]{:S(2)}) collective-permute-start(f32[8,2,8,128]{3,2,1,0:T(8,128)S(1)} %get-tuple-element.18), channel_id=1, source_target_pairs={{0,12},{4,8},{8,4},{12,0},{16,28},{20,24},{24,20},{28,16},{1,13},{... | collective-permute-start | bytes 196616 | tf_op jit(solution)/shard_map/ppermute | solution.py:576
  10.5 6.5 %collective-permute-start.4 = (f32[8,2,8,128]{3,2,1,0:T(8,128)S(1)}, f32[8,2,8,128]{3,2,1,0:T(8,128)S(1)}, u32[]{:S(2)}, u32[]{:S(2)}) collective-permute-start(f32[8,2,8,128]{3,2,1,0:T(8,128)S(1)} %get-tuple-element.19), channel_id=1, source_target_pairs={{8,20},{12,16},{16,12},{20,8},{9,21},{13,17},{17,13},{21,9},{10,22... | collective-permute-start | bytes 196616 | tf_op jit(solution)/shard_map/ppermute | solution.py:576
  17.6 11.5 %collective-permute-start.5 = (f32[3,2,8,128]{3,2,1,0:T(8,128)S(1)}, f32[3,2,8,128]{3,2,1,0:T(8,128)S(1)}, u32[]{:S(2)}, u32[]{:S(2)}) collective-permute-start(f32[3,2,8,128]{3,2,1,0:T(8,128)S(1)} %get-tuple-element.21), channel_id=1, source_target_pairs={{0,1},{1,0},{2,3},{3,2},{4,5},{5,4},{6,7},{7,6},{8,9},{9,8},{10,11... | collective-permute-start | bytes 73736 | tf_op jit(solution)/shard_map/ppermute | solution.py:594
  19.7 9.4 %collective-permute-start.6 = (f32[3,2,8,128]{3,2,1,0:T(8,128)S(1)}, f32[3,2,8,128]{3,2,1,0:T(8,128)S(1)}, u32[]{:S(2)}, u32[]{:S(2)}) collective-permute-start(f32[3,2,8,128]{3,2,1,0:T(8,128)S(1)} %get-tuple-element.22), channel_id=1, source_target_pairs={{1,2},{2,1},{5,6},{6,5},{9,10},{10,9},{13,14},{14,13},{17,18},{18,... | collective-permute-start | bytes 73736 | tf_op jit(solution)/shard_map/ppermute | solution.py:595

commit v2 on v1

--- a/solution.py
+++ b/solution.py
@@ -24,7 +24,7 @@
 SPAN = 32
 
 VM = pl.BlockSpec(memory_space=pltpu.VMEM)
-SM = pl.BlockSpec(memory_space=pltpu.SMEM)
+HBM = pl.BlockSpec(memory_space=pltpu.MemorySpace.HBM)
 
 
 def omegas():
@@ -246,7 +246,12 @@
     ex, ez = even("gx"), even("gz")
     flip = (lax.axis_index("gy") == 1) if shape.mirror else False
 
+    gx, gy = lax.axis_index("gx"), lax.axis_index("gy")
+    inner = (gx > 0).astype(jnp.float32), (gx < shape.n[0] - 1).astype(jnp.float32)
+
     def put(c, row, low, mid, high):
+        if c == W_CH:
+            low, high = low * inner[0], high * inner[1]
         nat[c, row, 0:HALO] = low
         nat[c, row, HALO : HALO + sx] = mid
         nat[c, row, HALO + sx :] = high
@@ -274,6 +279,9 @@
                         jnp.where(lower, yrecv[0][c, 2 * k + h], yrecv[1][c, 2 * k + h])
                         for h in range(2)
                     ]
+                    if c == W_CH:
+                        near = gy < shape.n[1] - 1 if side else gy > 0
+                        a, b, *mids = (t * near.astype(jnp.float32) for t in (a, b, *mids))
                 low, high = jnp.where(ex, b, a), jnp.where(ex, a, b)
                 for h in range(2):
                     part = slice(HALO * h, HALO * h + HALO)
@@ -418,6 +426,8 @@
     ez = even("gz")
     lane = lane_ids()
     within = lane % SPAN
+    gz = lax.axis_index("gz")
+    inner = (gz > 0).astype(jnp.float32), (gz < shape.n[2] - 1).astype(jnp.float32)
     half = SPAN // 2
 
     def window(c, m, t):
@@ -441,11 +451,11 @@
             low, high = jnp.where(ez, b, a), jnp.where(ez, a, b)
 
             def extended(c):
-                value = window(c, m, t)
-                value = jnp.where(within < HALO, roll_z(low, -HALO * c), value)
-                return jnp.where(
-                    within >= SPAN - HALO, roll_z(high, SPAN - HALO - HALO * c), value
-                )
+                below, above = roll_z(low, -HALO * c), roll_z(high, SPAN - HALO - HALO * c)
+                if c == W_CH:
+                    below, above = below * inner[0], above * inner[1]
+                value = jnp.where(within < HALO, below, window(c, m, t))
+                return jnp.where(within >= SPAN - HALO, above, value)
 
             for c in range(3):
                 value = extended(c)
@@ -505,25 +515,45 @@
             out[c, pl.ds(place, sx, stride=sy), :] = tiles[HALO : HALO + sx]
 
 
-def swap(size, parity):
+def partner(size, parity, i):
+    j = i + 1 if i % 2 == parity else i - 1
+    return j if 0 <= j < size else None
+
+
+def exchange(shape, parities):
+    n = shape.n
     pairs = []
-    for i in range(size):
-        j = i + 1 if i % 2 == parity else i - 1
-        if 0 <= j < size:
-            pairs.append((i, j))
+    for i in range(n[0]):
+        for j in range(n[1]):
+            for k in range(n[2]):
+                here = (i, j, k)
+                there = [
+                    at if parity is None else partner(size, parity, at)
+                    for at, size, parity in zip(here, n, parities)
+                ]
+                if None in there:
+                    axis = 1 if parities[2] is not None else 2
+                    other = partner(n[axis], 0, here[axis])
+                    if other is None:
+                        continue
+                    there = list(here)
+                    there[axis] = other
+                pairs.append(
+                    ((i * n[1] + j) * n[2] + k, (there[0] * n[1] + there[1]) * n[2] + there[2])
+                )
     return pairs
 
 
-def swap2(nx, px, ny, py):
-    return [
-        (i * ny + j, a * ny + b)
-        for i, a in swap(nx, px)
-        for j, b in swap(ny, py)
-    ]
+def send(shape, value, *parities):
+    return lax.ppermute(value, ("gx", "gy", "gz"), exchange(shape, parities))
 
 
 def f32(*dims):
     return jax.ShapeDtypeStruct(dims, jnp.float32)
+
+
+def in_hbm(value):
+    return pltpu.with_memory_space_constraint(value, pltpu.MemorySpace.HBM)
 
 
 def scratch(*dims):
@@ -545,37 +575,46 @@
 def per_device(mesh, start_disp, inertial, material, pinned, stiffness):
     shape = Shape(mesh, material.shape)
     sx, sy, sz = shape.size
-    nx, ny, nz = shape.n
     sides = 1 if shape.mirror else 2
     rows, erows = shape.rows, shape.erows
 
-    def prep(start, inert, mat, pin, stiff, own, *rest):
-        prep_kernel(
-            shape, start, inert, mat, pin, stiff, own,
-            rest[2 : 2 + sides], rest[:2], rest[2 + sides :],
-        )
-
-    outs = prep_outs = [f32(CH, sy + 1, sx, sz)]
+    def prep(*refs):
+        count = 3 + 3 * sides
+        given, (own, *sent), held, sems = refs[:5], refs[5 : 5 + count], refs[5 + count : -1], refs[-1]
+        copies = [pltpu.make_async_copy(a, b, sems.at[i]) for i, (a, b) in enumerate(zip(given, held))]
+        for copy in copies:
+            copy.start()
+        for copy in copies:
+            copy.wait()
+        prep_kernel(shape, *held, own, sent[2 : 2 + sides], sent[:2], sent[2 + sides :])
+
+    outs = [f32(CH, sy + 1, sx, sz)]
     outs += [f32(CH, sy // 2, 8, sz)] * 2 + [f32(CH, HALO, sx, sz)] * sides
     outs += [f32(CH, HALO // 2, 8, sz)] * (2 * sides)
     own, *sent = call(
         prep,
         outs,
         (
-            start_disp.reshape(3, sx * sy, sz),
-            inertial.reshape(3, sx * sy, sz),
-            material.reshape(sx * sy, sz),
-            pinned.reshape(sx * sy, sz),
-            stiffness,
+            in_hbm(start_disp.reshape(3, sx * sy, sz)),
+            in_hbm(inertial.reshape(3, sx * sy, sz)),
+            in_hbm(material.reshape(sx * sy, sz)),
+            in_hbm(pinned.reshape(sx * sy, sz)),
+            in_hbm(stiffness),
         ),
-        specs=[VM] * 4 + [SM],
-    )
-    recv = [lax.ppermute(sent[p], "gx", swap(nx, p)) for p in range(2)]
-    recv += [lax.ppermute(sent[2 + p], "gy", swap(ny, p)) for p in range(sides)]
+        [
+            scratch(3, sx * sy, sz),
+            scratch(3, sx * sy, sz),
+            pltpu.VMEM((sx * sy, sz), jnp.int32),
+            pltpu.VMEM((sx * sy, sz), jnp.int32),
+            pltpu.SMEM((MATS,), jnp.float32),
+            pltpu.SemaphoreType.DMA((5,)),
+        ],
+        [HBM] * 5,
+    )
+    recv = [send(shape, sent[p], p, None, None) for p in range(2)]
+    recv += [send(shape, sent[2 + p], None, p, None) for p in range(sides)]
     recv += [
-        lax.ppermute(sent[2 + sides + 2 * q + p], ("gx", "gy"), swap2(nx, p, ny, q))
-        for q in range(sides)
-        for p in range(2)
+        send(shape, sent[2 + sides + 2 * q + p], p, q, None) for q in range(sides) for p in range(2)
     ]
 
     def join(own, *rest):
@@ -591,8 +630,8 @@
         (own, *recv),
         [scratch(CH, rows, sx + 2 * HALO, sz)],
     )
-    z0 = lax.ppermute(z0, "gz", swap(nz, 0))
-    z1 = lax.ppermute(z1, "gz", swap(nz, 1))
+    z0 = send(shape, z0, None, None, 0)
+    z1 = send(shape, z1, None, None, 1)
     (main,) = call(
         functools.partial(main_kernel, shape),
         [f32(3, rows + 2, 2, 8, sz)],

time: 33.7 us -> 25.4 us (0.75)
  local copies, waits for them, and re-layouts: 3.95 us -> 0 us
  starting transfers between devices: 12.9 us -> 10.1 us
  waiting for transfers between devices: 4.6 us -> 2.81 us
  Pallas kernels: 11.9 us -> 12.3 us
    unnamed x10 -> x0, local copies, waits for them, and re-layouts: 3.95 us -> none
    ppermute x7, starting transfers between devices: 12.9 us -> 10.1 us  [send(): return lax.ppermute(value, ('gx', 'gy', 'gz'), exchange(shape, parities))]
    ppermute x7, waiting for transfers between devices: 4.6 us -> 2.81 us  [send(): return lax.ppermute(value, ('gx', 'gy', 'gz'), exchange(shape, parities))]
    pallas_call x4, Pallas kernels: 11.9 us -> 12.3 us  [call(): pl.pallas_call(body, out_shape=outs, in_specs=specs or [VM] * len(args),...]
  transfers between devices with their start and end apart: 7 -> 7, of which waited for: 2 -> 2; matrix products, arithmetic and copies ran while one was open for 0% -> 0% of each run, Pallas kernels for 19% -> 25%
where the time goes in v2:
time: 25.4 us; the launch traced here: 25.3 us
  Pallas kernels  12.3 us (48%)
  starting transfers between devices  10.1 us (40%)
  waiting for transfers between devices  2.81 us (11%)
    pallas_call x4, Pallas kernels, call(): pl.pallas_call(body, out_shape=outs, in_specs=specs or [VM] * len(args),...  12.3 us
    ppermute x7, starting transfers between devices, send(): return lax.ppermute(value, ('gx', 'gy', 'gz'), exchange(shape, parities))  10.1 us
    ppermute x7, waiting for transfers between devices, send(): return lax.ppermute(value, ('gx', 'gy', 'gz'), exchange(shape, parities))  2.81 us
  transfers between devices with their start and end apart: 7, of which 2 were waited for; matrix products, arithmetic and copies ran while one was open for 0% of the time, Pallas kernels for 25%

profile of v2, /device:TPU:9, one launch (start us, length us, event | category | flops | bytes accessed | tf_op | source)
XLA Modules:
  0.0 25.3 jit_solution(18114767609441279162)
XLA Ops:
  0.0 1.1 %shard_map.55 = (f32[8,9,8,128]{3,2,1,0:T(8,128)S(1)}, f32[8,4,8,128]{3,2,1,0:T(8,128)S(1)}, f32[8,4,8,128]{3,2,1,0:T(8,128)S(1)}, f32[8,4,8,128]{3,2,1,0:T(8,12...) custom-call(f32[3,64,128]{2,1,0:T(8,128)} %bitcast.5, f32[3,64,128]{2,1,0:T(8,128)} %bitcast.6, ...), custom_call_target="tpu_custom_call" | custom-call | flops 2000000 | bytes 100000 | tf_op jit(solution)/shard_map/pallas_call | solution.py:564
  1.1 0.1 collective-permute-start
  1.2 2.6 %collective-permute-start.1 = (f32[8,4,8,128]{3,2,1,0:T(8,128)S(1)}, f32[8,4,8,128]{3,2,1,0:T(8,128)S(1)}, u32[]{:S(2)}, u32[]{:S(2)}) collective-permute-start(f32[8,4,8,128]{3,2,1,0:T(8,128)S(1)} %get-tuple-element.16), channel_id=1, source_target_pairs={{0,1},{1,0},{2,3},{3,2},{4,5},{5,4},{6,7},{7,6},{8,16},{9,17},{10,... | collective-permute-start | bytes 393224 | tf_op jit(solution)/shard_map/ppermute | solution.py:548
  3.8 1.2 %collective-permute-start.2 = (f32[8,4,8,128]{3,2,1,0:T(8,128)S(1)}, f32[8,4,8,128]{3,2,1,0:T(8,128)S(1)}, u32[]{:S(2)}, u32[]{:S(2)}) collective-permute-start(f32[8,4,8,128]{3,2,1,0:T(8,128)S(1)} %get-tuple-element.17), channel_id=1, source_target_pairs={{0,4},{1,5},{2,6},{3,7},{4,0},{5,1},{6,2},{7,3},{8,12},{9,13},{10,... | collective-permute-start | bytes 393224 | tf_op jit(solution)/shard_map/ppermute | solution.py:548
  5.0 0.0 collective-permute-start.3
  5.0 2.0 %collective-permute-start.4 = (f32[8,2,8,128]{3,2,1,0:T(8,128)S(1)}, f32[8,2,8,128]{3,2,1,0:T(8,128)S(1)}, u32[]{:S(2)}, u32[]{:S(2)}) collective-permute-start(f32[8,2,8,128]{3,2,1,0:T(8,128)S(1)} %get-tuple-element.19), channel_id=1, source_target_pairs={{0,1},{1,0},{2,3},{3,2},{4,5},{5,4},{6,7},{7,6},{8,20},{9,21},{10,... | collective-permute-start | bytes 196616 | tf_op jit(solution)/shard_map/ppermute | solution.py:548
  7.0 2.6 %collective-permute-done.3.rest_3_ = f32[8,2,8,128]{3,2,1,0:T(8,128)S(1)} collective-permute-done((f32[8,2,8,128]{3,2,1,0:T(8,128)S(1)}, f32[8,2,8,128]{3,2,1,0:T(8,128)S(1)}, u32[]{:S(2)}, u32[]{:S(2)}) %collective-permute-start.3) | collective-permute-done | bytes 65568 | tf_op jit(solution)/shard_map/ppermute | solution.py:548
  9.7 0.2 collective-permute-done.4.rest_4_
  9.8 0.0 collective-permute-done.rest_0_
  9.8 0.0 collective-permute-done.1.rest_1_
  9.8 0.0 collective-permute-done.2.rest_2_
  9.8 0.5 %shard_map.56 = (f32[8,12,2,8,128]{4,3,2,1,0:T(8,128)S(1)}, f32[3,2,8,128]{3,2,1,0:T(8,128)S(1)}, f32[3,2,8,128]{3,2,1,0:T(8,128)S(1)}) custom-call(f32[8,9,8,128]{3,2,1,0:T(8,128)S(1)} %get-tuple-element.14.own, f32[8,4,8,128]{3,2,1,0:T(8,128)S(1)} %collective-permute-done.rest_0_, f32[8,4,8,128]{3,2,1,0:T(8,128)S(1)} %collective-permute-done.1.rest_1_, ...), custom_call_target="tpu_custom_call" | custom-call | flops 2000000 | bytes 100000 | tf_op jit(solution)/shard_map/pallas_call | solution.py:564
  10.4 3.0 %collective-permute-start.5 = (f32[3,2,8,128]{3,2,1,0:T(8,128)S(1)}, f32[3,2,8,128]{3,2,1,0:T(8,128)S(1)}, u32[]{:S(2)}, u32[]{:S(2)}) collective-permute-start(f32[3,2,8,128]{3,2,1,0:T(8,128)S(1)} %get-tuple-element.21), channel_id=1, source_target_pairs={{0,1},{1,0},{2,3},{3,2},{4,5},{5,4},{6,7},{7,6},{8,9},{9,8},{10,11... | collective-permute-start | bytes 73736 | tf_op jit(solution)/shard_map/ppermute | solution.py:548
  13.4 1.2 %collective-permute-start.6 = (f32[3,2,8,128]{3,2,1,0:T(8,128)S(1)}, f32[3,2,8,128]{3,2,1,0:T(8,128)S(1)}, u32[]{:S(2)}, u32[]{:S(2)}) collective-permute-start(f32[3,2,8,128]{3,2,1,0:T(8,128)S(1)} %get-tuple-element.22), channel_id=1, source_target_pairs={{0,4},{1,2},{2,1},{3,7},{4,0},{5,6},{6,5},{7,3},{8,12},{9,10},{10,... | collective-permute-start | bytes 73736 | tf_op jit(solution)/shard_map/ppermute | solution.py:548
  14.6 6.4 %shard_map.57.main = f32[3,14,2,8,128]{4,3,2,1,0:T(8,128)S(1)} custom-call(f32[8,12,2,8,128]{4,3,2,1,0:T(8,128)S(1)} %get-tuple-element.20.full), custom_call_target="tpu_custom_call" | custom-call | flops 2000000 | bytes 100000 | tf_op jit(solution)/shard_map/pallas_call | solution.py:564
  20.9 0.0 collective-permute-done.5.zrecv0
  21.0 0.0 collective-permute-done.6.zrecv1
  21.0 4.3 %shard_map.58 = f32[3,64,128]{2,1,0:T(8,128)} custom-call(f32[8,12,2,8,128]{4,3,2,1,0:T(8,128)S(1)} %get-tuple-element.20.full, f32[3,14,2,8,128]{4,3,2,1,0:T(8,128)S(1)} %shard_map.57.main, f32[3,2,8,128]{3,2,1,0:T(8,128)S(1)} %collective-permute-done.5.zrecv0, f32[3,2,8,128]{3,2,1,0:T(8,128)S(1)} %collective-permute-done.6.zrecv1), custom_call_target="tpu_custom_call" | custom-call | flops 2000000 | bytes 100000 | tf_op jit(solution)/shard_map/pallas_call | solution.py:564
Async XLA Ops:
  1.1 8.7 %collective-permute-start = (f32[8,4,8,128]{3,2,1,0:T(8,128)S(1)}, f32[8,4,8,128]{3,2,1,0:T(8,128)S(1)}, u32[]{:S(2)}, u32[]{:S(2)}) collective-permute-start(f32[8,4,8,128]{3,2,1,0:T(8,128)S(1)} %get-tuple-element.15), channel_id=1, source_target_pairs={{0,8},{1,9},{2,10},{3,11},{4,12},{5,13},{6,14},{7,15},{8,0},{9,1},... | collective-permute-start | bytes 393224 | tf_op jit(solution)/shard_map/ppermute | solution.py:548
  1.2 8.6 %collective-permute-start.1 = (f32[8,4,8,128]{3,2,1,0:T(8,128)S(1)}, f32[8,4,8,128]{3,2,1,0:T(8,128)S(1)}, u32[]{:S(2)}, u32[]{:S(2)}) collective-permute-start(f32[8,4,8,128]{3,2,1,0:T(8,128)S(1)} %get-tuple-element.16), channel_id=1, source_target_pairs={{0,1},{1,0},{2,3},{3,2},{4,5},{5,4},{6,7},{7,6},{8,16},{9,17},{10,... | collective-permute-start | bytes 393224 | tf_op jit(solution)/shard_map/ppermute | solution.py:548
  3.8 6.1 %collective-permute-start.2 = (f32[8,4,8,128]{3,2,1,0:T(8,128)S(1)}, f32[8,4,8,128]{3,2,1,0:T(8,128)S(1)}, u32[]{:S(2)}, u32[]{:S(2)}) collective-permute-start(f32[8,4,8,128]{3,2,1,0:T(8,128)S(1)} %get-tuple-element.17), channel_id=1, source_target_pairs={{0,4},{1,5},{2,6},{3,7},{4,0},{5,1},{6,2},{7,3},{8,12},{9,13},{10,... | collective-permute-start | bytes 393224 | tf_op jit(solution)/shard_map/ppermute | solution.py:548
  5.0 4.7 %collective-permute-start.3 = (f32[8,2,8,128]{3,2,1,0:T(8,128)S(1)}, f32[8,2,8,128]{3,2,1,0:T(8,128)S(1)}, u32[]{:S(2)}, u32[]{:S(2)}) collective-permute-start(f32[8,2,8,128]{3,2,1,0:T(8,128)S(1)} %get-tuple-element.18), channel_id=1, source_target_pairs={{0,12},{1,13},{2,14},{3,15},{4,8},{5,9},{6,10},{7,11},{8,4},{9,5},... | collective-permute-start | bytes 196616 | tf_op jit(solution)/shard_map/ppermute | solution.py:548
  5.0 4.8 %collective-permute-start.4 = (f32[8,2,8,128]{3,2,1,0:T(8,128)S(1)}, f32[8,2,8,128]{3,2,1,0:T(8,128)S(1)}, u32[]{:S(2)}, u32[]{:S(2)}) collective-permute-start(f32[8,2,8,128]{3,2,1,0:T(8,128)S(1)} %get-tuple-element.19), channel_id=1, source_target_pairs={{0,1},{1,0},{2,3},{3,2},{4,5},{5,4},{6,7},{7,6},{8,20},{9,21},{10,... | collective-permute-start | bytes 196616 | tf_op jit(solution)/shard_map/ppermute | solution.py:548
  10.4 10.6 %collective-permute-start.5 = (f32[3,2,8,128]{3,2,1,0:T(8,128)S(1)}, f32[3,2,8,128]{3,2,1,0:T(8,128)S(1)}, u32[]{:S(2)}, u32[]{:S(2)}) collective-permute-start(f32[3,2,8,128]{3,2,1,0:T(8,128)S(1)} %get-tuple-element.21), channel_id=1, source_target_pairs={{0,1},{1,0},{2,3},{3,2},{4,5},{5,4},{6,7},{7,6},{8,9},{9,8},{10,11... | collective-permute-start | bytes 73736 | tf_op jit(solution)/shard_map/ppermute | solution.py:548
  13.4 7.6 %collective-permute-start.6 = (f32[3,2,8,128]{3,2,1,0:T(8,128)S(1)}, f32[3,2,8,128]{3,2,1,0:T(8,128)S(1)}, u32[]{:S(2)}, u32[]{:S(2)}) collective-permute-start(f32[3,2,8,128]{3,2,1,0:T(8,128)S(1)} %get-tuple-element.22), channel_id=1, source_target_pairs={{0,4},{1,2},{2,1},{3,7},{4,0},{5,6},{6,5},{7,3},{8,12},{9,10},{10,... | collective-permute-start | bytes 73736 | tf_op jit(solution)/shard_map/ppermute | solution.py:548

commit v3 on v2

--- a/solution.py
+++ b/solution.py
@@ -20,6 +20,9 @@
 CH = 8
 W_CH = 6
 FREE_CH = 7
+SHALLOW = (3, 4, 5, 7)
+CARRY = (0, 1, 2, 3, 4, 5, 7)
+LAYERS = tuple((c, d) for c in range(CH) for d in range(HALO - (c in SHALLOW)))
 GROUPS = 4
 SPAN = 32
 
@@ -48,6 +51,11 @@
 def roll_z(value, amount):
     amount = amount % 128
     return value if amount == 0 else pltpu.roll(value, amount, 1)
+
+
+def turn_x(value, amount):
+    amount = amount % 8
+    return value if amount == 0 else pltpu.roll(value, amount, 0)
 
 
 def next_x(pair):
@@ -157,14 +165,6 @@
             row.append(prev[c][t] + omega * (y - prev[c][t]))
         new.append(tuple(row))
     return new
-
-
-def omega_at(step):
-    values = omegas()
-    out = jnp.float32(values[0])
-    for index in range(1, ITERS):
-        out = jnp.where(step == index, jnp.float32(values[index]), out)
-    return out
 
 
 class Shape:
@@ -217,27 +217,33 @@
         own[W_CH, cell] = weight
         own[FREE_CH, node] = jnp.where(fixed, 0.0, 1.0)
     ex = even("gx")
-    for c in range(CH):
-        for k in range(sy // 2):
+    place = lax.rem(sub_ids(), HALO)
+    for k in range(sy // 2):
+        wlow, whigh = pack_faces(own[W_CH, 2 * k + 1], own[W_CH, 2 * k + 2])
+        for index, c in enumerate(CARRY):
             low, high = pack_faces(own[c, 2 * k + 1], own[c, 2 * k + 2])
-            xsend[0][c, k] = jnp.where(ex, high, low)
-            xsend[1][c, k] = jnp.where(ex, low, high)
-        for side in range(len(ysend)):
-            rows = []
-            for d in range(HALO):
-                if shape.mirror:
-                    node = sy - 1 - d
-                    if c == W_CH:
-                        node = node - jnp.where(flip, 1, 0)
-                else:
-                    up = even("gy") if side == 0 else jnp.logical_not(even("gy"))
-                    node = jnp.where(up, sy - HALO + d, d)
-                rows.append(own[c, node + 1])
-                ysend[side][c, d] = rows[-1]
-            for k in range(HALO // 2):
-                low, high = pack_faces(rows[2 * k], rows[2 * k + 1])
-                xysend[2 * side][c, k] = jnp.where(ex, high, low)
-                xysend[2 * side + 1][c, k] = jnp.where(ex, low, high)
+            if c in SHALLOW:
+                q = SHALLOW.index(c)
+                low = jnp.where(place == HALO - 1, turn_x(wlow, HALO - 1 - q), low)
+                high = jnp.where(place == 0, turn_x(whigh, -q), high)
+            xsend[0][index, k] = jnp.where(ex, high, low)
+            xsend[1][index, k] = jnp.where(ex, low, high)
+    for side in range(len(ysend)):
+        rows = []
+        for c, d in LAYERS:
+            if shape.mirror:
+                node = sy - 1 - d
+                if c == W_CH:
+                    node = node - jnp.where(flip, 1, 0)
+            else:
+                up = even("gy") if side == 0 else jnp.logical_not(even("gy"))
+                node = jnp.where(up, sy - 1 - d, d)
+            rows.append(own[c, node + 1])
+            ysend[side][len(rows) - 1] = rows[-1]
+        for k in range(len(rows) // 2):
+            low, high = pack_faces(rows[2 * k], rows[2 * k + 1])
+            xysend[2 * side][k] = jnp.where(ex, high, low)
+            xysend[2 * side + 1][k] = jnp.where(ex, low, high)
 
 
 def join_kernel(shape, own, yrecv, xrecv, xyrecv, full, zsend, nat):
@@ -256,45 +262,57 @@
         nat[c, row, HALO : HALO + sx] = mid
         nat[c, row, HALO + sx :] = high
 
-    for c in range(CH):
-        turned = shape.mirror and c in (1, 4)
-        for k in range(sy // 2):
-            a, b = xrecv[0][c, k], xrecv[1][c, k]
+    place = lax.rem(sub_ids(), HALO)
+    for k in range(sy // 2):
+        wlow = whigh = jnp.zeros((8, 128), jnp.float32)
+        faces = {}
+        for index, c in enumerate(CARRY):
+            a, b = xrecv[0][index, k], xrecv[1][index, k]
             low, high = jnp.where(ex, b, a), jnp.where(ex, a, b)
+            faces[c] = low, high
+            if c in SHALLOW:
+                q = SHALLOW.index(c)
+                wlow = jnp.where(place == q, turn_x(low, q), wlow)
+                whigh = jnp.where(place == q, turn_x(high, q + 1 - HALO), whigh)
+        faces[W_CH] = wlow, whigh
+        for c, (low, high) in faces.items():
             for h in range(2):
                 part = slice(HALO * h, HALO * h + HALO)
                 put(c, shape.own + 2 * k + h, low[part], own[c, 2 * k + h + 1], high[part])
-        for side in range(2 if not shape.mirror else 1):
-            for k in range(HALO // 2):
+    empty = jnp.zeros((sx + 2 * HALO, 128), jnp.float32)
+    for c in SHALLOW:
+        nat[c, rows - 1] = empty
+        if not shape.mirror:
+            nat[c, 0] = empty
+    for side in range(1 if shape.mirror else 2):
+        for k in range(len(LAYERS) // 2):
+            near = LAYERS[2 * k : 2 * k + 2]
+            if shape.mirror:
+                a, b = xyrecv[0][k], xyrecv[1][k]
+                mids = [yrecv[0][2 * k + h] for h in range(2)]
+            else:
+                lower = even("gy") if side else jnp.logical_not(even("gy"))
+                a, b = (jnp.where(lower, xyrecv[i][k], xyrecv[2 + i][k]) for i in range(2))
+                mids = [
+                    jnp.where(lower, yrecv[0][2 * k + h], yrecv[1][2 * k + h]) for h in range(2)
+                ]
+            low, high = jnp.where(ex, b, a), jnp.where(ex, a, b)
+            for h, (c, d) in enumerate(near):
+                part = slice(HALO * h, HALO * h + HALO)
+                values = [low[part], mids[h], high[part]]
                 if shape.mirror:
-                    a, b = xyrecv[0][c, k], xyrecv[1][c, k]
-                    mids = [yrecv[0][c, 2 * k + h] for h in range(2)]
-                    if turned:
-                        a, b = -a, -b
-                        mids = [-t for t in mids]
+                    row = sy + d
+                    if c == W_CH:
+                        row = row - jnp.where(flip, 1, 0)
+                    if c in (1, 4):
+                        values = [-t for t in values]
                 else:
-                    lower = even("gy") if side else jnp.logical_not(even("gy"))
-                    a, b = (jnp.where(lower, xyrecv[i][c, k], xyrecv[2 + i][c, k]) for i in range(2))
-                    mids = [
-                        jnp.where(lower, yrecv[0][c, 2 * k + h], yrecv[1][c, 2 * k + h])
-                        for h in range(2)
-                    ]
+                    row = HALO + sy + d if side else HALO - 1 - d
                     if c == W_CH:
-                        near = gy < shape.n[1] - 1 if side else gy > 0
-                        a, b, *mids = (t * near.astype(jnp.float32) for t in (a, b, *mids))
-                low, high = jnp.where(ex, b, a), jnp.where(ex, a, b)
-                for h in range(2):
-                    part = slice(HALO * h, HALO * h + HALO)
-                    d = 2 * k + h
-                    if shape.mirror:
-                        row = sy + d
-                        if c == W_CH:
-                            row = row - jnp.where(flip, 1, 0)
-                    else:
-                        row = d + side * (HALO + sy)
-                    put(c, row, low[part], mids[h], high[part])
-        if c == W_CH:
-            nat[c, rows - 1] = jnp.zeros((sx + 2 * HALO, 128), jnp.float32)
+                        there = (gy < shape.n[1] - 1 if side else gy > 0).astype(jnp.float32)
+                        values = [t * there for t in values]
+                put(c, row, *values)
+    nat[W_CH, rows - 1] = empty
     slot = lane_ids() // HALO
     for m in range(shape.erows):
         for t in range(2):
@@ -324,111 +342,105 @@
     )
 
 
-def main_kernel(shape, full, v, prev, gsize, grad, stress, part):
-    rows = shape.rows
+def step_sizes(shape, full, gsize):
     zero = jnp.zeros((8, 128), jnp.float32)
-    for row in range(rows):
-        for c in range(3):
-            for t in range(2):
-                tile = full[c, row, t]
-                v[c, row + 1, t] = tile
-                prev[c, row + 1, t] = tile
+    for row in range(shape.rows):
         now = load_row(full, row, (W_CH,))[0]
         before = load_row(full, row - 1, (W_CH,))[0] if row else (zero, zero)
         g = step_size(now, before, load_row(full, row, (FREE_CH,))[0])
         for t in range(2):
-            gsize[row + 1, t] = g[t]
-    for i in range(9):
-        for t in range(2):
-            stress[i, 0, t] = zero
+            gsize[row, t] = g[t]
+
+
+def put9(ref, row, value):
     for c in range(3):
-        for t in range(2):
-            v[c, 0, t] = zero
-            v[c, rows + 1, t] = zero
-            prev[c, 0, t] = zero
-    for t in range(2):
-        gsize[0, t] = zero
-
-    def put_gradient(row, value):
-        for c in range(3):
-            for kind in range(3):
-                for t in range(2):
-                    grad[3 * c + kind, row, t] = value[c][kind][t]
-
-    def get9(ref, row):
-        return [[(ref[3 * c + k, row, 0], ref[3 * c + k, row, 1]) for k in range(3)] for c in range(3)]
-
-    def iteration(step, carry):
-        omega = omega_at(step)
-        first = 0 if shape.mirror else step
-        last = rows - 1 - step
-        put_gradient(first, gradient_row(load_row(v, first + 1)))
-        put_gradient(first + 1, gradient_row(load_row(v, first + 2)))
-
-        def body(j, carry):
-            ahead = load_row(v, j + 3)
-            low, high = get9(grad, j), get9(grad, j + 1)
-            weight = load_row(full, j, (W_CH,))[0]
-            before = get9(stress, j)
-            held = [
-                tuple((part[2 * c + i, j, 0], part[2 * c + i, j, 1]) for i in range(2))
-                for c in range(3)
-            ]
-            old = load_row(v, j)
-            oldest = load_row(prev, j)
-            goal = load_row(full, max(j - 1, 0), (3, 4, 5))
-            g = (gsize[j, 0], gsize[j, 1])
-
-            after = gradient_row(ahead)
-            now = stress_row(deform_rows(low, high), weight)
-            parts = force_parts(now, before)
-            new = update_row(held, old, goal, oldest, g, omega)
-
-            put_gradient(j + 2, after)
-            for c in range(3):
-                for t in range(2):
-                    for d in range(3):
-                        stress[3 * c + d, j + 1, t] = now[c][d][t]
-                    for i in range(2):
-                        part[2 * c + i, j + 1, t] = parts[c][i][t]
-                    prev[c, j, t] = old[c][t]
-                    v[c, j, t] = new[c][t]
-            return carry
-
-        for j in range(first, last):
-            body(j, 0)
+        for k in range(3):
+            for t in range(2):
+                ref[3 * c + k, row, t] = value[c][k][t]
+
+
+def get9(ref, row):
+    return [[(ref[3 * c + k, row, 0], ref[3 * c + k, row, 1]) for k in range(3)] for c in range(3)]
+
+
+def main_steps(shape, full, gsize, old, oldest, write, grad, stress, part, step):
+    omega = omegas()[step]
+    first = 0 if shape.mirror else step
+    last = shape.rows - 1 - step
+    zero = jnp.zeros((8, 128), jnp.float32)
+
+    def update(row):
         held = [
-            tuple((part[2 * c + i, last, 0], part[2 * c + i, last, 1]) for i in range(2))
+            tuple((part[2 * c + i, row, 0], part[2 * c + i, row, 1]) for i in range(2))
             for c in range(3)
         ]
-        old = load_row(v, last)
-        new = update_row(
-            held,
-            old,
-            load_row(full, last - 1, (3, 4, 5)),
-            load_row(prev, last),
-            (gsize[last, 0], gsize[last, 1]),
-            omega,
+        write(
+            row,
+            update_row(
+                held,
+                load_row(old, row),
+                load_row(full, row, (3, 4, 5)),
+                load_row(oldest, row),
+                (gsize[row, 0], gsize[row, 1]),
+                omega,
+            ),
         )
+
+    def head():
+        for row in (first, first + 1):
+            put9(grad, row, gradient_row(load_row(old, row)))
+
+    def body(j):
+        after = gradient_row(load_row(old, j + 2)) if j + 2 <= last else None
+        now = stress_row(
+            deform_rows(get9(grad, j), get9(grad, j + 1)), load_row(full, j, (W_CH,))[0]
+        )
+        before = get9(stress, j - 1) if j > first else [[(zero, zero)] * 3] * 3
+        parts = force_parts(now, before)
+        if j > first:
+            update(j - 1)
+        if after is not None:
+            put9(grad, j + 2, after)
+        put9(stress, j, now)
         for c in range(3):
             for t in range(2):
-                prev[c, last, t] = old[c][t]
-                v[c, last, t] = new[c][t]
-        return carry
-
-    for step in range(ITERS):
-        iteration(step, 0)
-
-
-def edge_kernel(shape, full, main, zrecv0, zrecv1, out, v, prev, goal, gsize, stiff, tiles):
-    sx, sy, sz = shape.size
+                for i in range(2):
+                    part[2 * c + i, j, t] = parts[c][i][t]
+        if j == last - 1:
+            update(j)
+
+    return head, [functools.partial(body, j) for j in range(first, last)]
+
+
+def writer(ref):
+    def write(row, new):
+        for c in range(3):
+            for t in range(2):
+                ref[c, row, t] = new[c][t]
+
+    return write
+
+
+def main_kernel(shape, full, one, two, gsize, grad, stress, part):
+    step_sizes(shape, full, gsize)
+    for step, (old, oldest, new) in enumerate(((full, full, one), (one, full, two))):
+        head, steps = main_steps(
+            shape, full, gsize, old, oldest, writer(new), grad, stress, part, step
+        )
+        head()
+        for run in steps:
+            run()
+
+
+def edge_parts(shape, full, zrecv, bufs, goal, gsize, stiff, grad, stress):
+    sz = shape.size[2]
     erows = shape.erows
     ez = even("gz")
     lane = lane_ids()
     within = lane % SPAN
+    half = SPAN // 2
     gz = lax.axis_index("gz")
     inner = (gz > 0).astype(jnp.float32), (gz < shape.n[2] - 1).astype(jnp.float32)
-    half = SPAN // 2
 
     def window(c, m, t):
         value = jnp.zeros((8, 128), jnp.float32)
@@ -445,74 +457,109 @@
             )
         return value
 
-    for m in range(erows):
-        for t in range(2):
-            a, b = zrecv0[m, t], zrecv1[m, t]
-            low, high = jnp.where(ez, b, a), jnp.where(ez, a, b)
-
-            def extended(c):
-                below, above = roll_z(low, -HALO * c), roll_z(high, SPAN - HALO - HALO * c)
-                if c == W_CH:
-                    below, above = below * inner[0], above * inner[1]
-                value = jnp.where(within < HALO, below, window(c, m, t))
-                return jnp.where(within >= SPAN - HALO, above, value)
-
-            for c in range(3):
-                value = extended(c)
-                v[c, m, t] = value
-                prev[c, m, t] = value
-                goal[c, m, t] = extended(3 + c)
-            stiff[m, t] = extended(W_CH)
-            gsize[m, t] = extended(FREE_CH)
-    weights = [(stiff[m, 0], stiff[m, 1]) for m in range(erows)]
-    behind = tuple(roll_z(t, SPAN) for t in weights[-1])
-    for m in range(erows):
-        g = step_size(weights[m], weights[m - 1] if m else behind, (gsize[m, 0], gsize[m, 1]))
-        for t in range(2):
-            gsize[m, t] = g[t]
-
-    def iteration(step, carry):
-        omega = omega_at(step)
-        grads = [gradient_row(load_row(v, m)) for m in range(erows)]
-        grads.append([[tuple(roll_z(t, -SPAN) for t in pair) for pair in row] for row in grads[0]])
-        stress = [None] * erows
-        for m in [erows - 1] + list(range(erows - 1)):
-            stress[m] = stress_row(
-                deform_rows(grads[m], grads[m + 1]), (stiff[m, 0], stiff[m, 1])
-            )
-        wrapped = [[tuple(roll_z(t, SPAN) for t in pair) for pair in row] for row in stress[-1]]
+    def setup():
         for m in range(erows):
-            parts = force_parts(stress[m], stress[m - 1] if m else wrapped)
-            old = load_row(v, m)
-            new = update_row(
-                parts, old, load_row(goal, m), load_row(prev, m), (gsize[m, 0], gsize[m, 1]), omega
-            )
-            for c in range(3):
-                for t in range(2):
-                    prev[c, m, t] = old[c][t]
-                    v[c, m, t] = new[c][t]
-        return carry
-
-    lax.fori_loop(0, ITERS, iteration, 0)
+            for t in range(2):
+                a, b = zrecv[0][m, t], zrecv[1][m, t]
+                low, high = jnp.where(ez, b, a), jnp.where(ez, a, b)
+
+                def extended(c):
+                    below, above = roll_z(low, -HALO * c), roll_z(high, SPAN - HALO - HALO * c)
+                    if c == W_CH:
+                        below, above = below * inner[0], above * inner[1]
+                    value = jnp.where(within < HALO, below, window(c, m, t))
+                    return jnp.where(within >= SPAN - HALO, above, value)
+
+                for c in range(3):
+                    bufs[0][c, m, t] = extended(c)
+                    goal[c, m, t] = extended(3 + c)
+                stiff[m, t] = extended(W_CH)
+                gsize[m, t] = extended(FREE_CH)
+        weights = [(stiff[m, 0], stiff[m, 1]) for m in range(erows)]
+        behind = tuple(roll_z(t, SPAN) for t in weights[-1])
+        for m in range(erows):
+            g = step_size(weights[m], weights[m - 1] if m else behind, (gsize[m, 0], gsize[m, 1]))
+            for t in range(2):
+                gsize[m, t] = g[t]
+
+    def gradients(step):
+        for m in range(erows):
+            put9(grad, m, gradient_row(load_row(bufs[step], m)))
+        turned = [tuple(roll_z(t, -SPAN) for t in pair) for pair in load_row(bufs[step], 0)]
+        put9(grad, erows, gradient_row(turned))
+
+    def stresses(m):
+        now = stress_row(deform_rows(get9(grad, m), get9(grad, m + 1)), (stiff[m, 0], stiff[m, 1]))
+        put9(stress, m + 1, now)
+        if m == erows - 1:
+            put9(stress, 0, [[tuple(roll_z(t, SPAN) for t in pair) for pair in row] for row in now])
+
+    def updates(step, m):
+        new = update_row(
+            force_parts(get9(stress, m + 1), get9(stress, m)),
+            load_row(bufs[step], m),
+            load_row(goal, m),
+            load_row(bufs[max(step - 1, 0)], m),
+            (gsize[m, 0], gsize[m, 1]),
+            omegas()[step],
+        )
+        writer(bufs[step + 1])(m, new)
+
+    return setup, gradients, stresses, updates
+
+
+def last_kernel(
+    shape, full, one, two, gsize, zrecv0, zrecv1, out,
+    three, grad, stress, part, bufs, egoal, egsize, estiff, egrad, estress, tiles,
+):
+    sx, sy, sz = shape.size
+    erows = shape.erows
+    lane = lane_ids()
+    setup, gradients, stresses, updates = edge_parts(
+        shape, full, (zrecv0, zrecv1), bufs, egoal, egsize, estiff, egrad, estress
+    )
     flip = (lax.axis_index("gy") == 1) if shape.mirror else False
-    for r in range(sy):
-        row = shape.own + r
+    turned = jnp.where(flip, -1.0 / SCALE, 1.0 / SCALE).astype(jnp.float32) if shape.mirror else 1.0 / SCALE
+
+    def finish(row, new):
+        r = row - shape.own
+        if not 0 <= r < sy:
+            return
         g, m = divmod(row, erows)
         base = SPAN * g
+        place = jnp.where(flip, sy - 1 - r, r) if shape.mirror else r
         for c in range(3):
-            factor = 1.0 / SCALE
-            if shape.mirror and c == 1:
-                factor = jnp.where(flip, -factor, factor).astype(jnp.float32)
             for t in range(2):
-                edge = v[c, m, t]
-                value = main[c, row + 1, t]
-                value = jnp.where(lane < HALO, roll_z(edge, -(base + HALO)), value)
+                edge = bufs[ITERS][c, m, t]
+                value = jnp.where(lane < HALO, roll_z(edge, -(base + HALO)), new[c][t])
                 value = jnp.where(
                     lane >= sz - HALO, roll_z(edge, sz - HALO - (base + SPAN - 2 * HALO)), value
                 )
-                tiles[pl.ds(t, 8, stride=2), :] = value * factor
-            place = jnp.where(flip, sy - 1 - r, r) if shape.mirror else r
-            out[c, pl.ds(place, sx, stride=sy), :] = tiles[HALO : HALO + sx]
+                tiles[r, c, pl.ds(t, 8, stride=2), :] = value * (turned if c == 1 else 1.0 / SCALE)
+            out[c, pl.ds(place, sx, stride=sy), :] = tiles[r, c, HALO : HALO + sx]
+
+    edge = [setup]
+    for step in range(ITERS):
+        edge.append(functools.partial(gradients, step))
+        order = [erows - 1] + list(range(erows - 1))
+        edge.append(lambda order=order: [stresses(m) for m in order])
+        edge.append(lambda step=step: [updates(step, m) for m in range(erows)])
+    head, steps = main_steps(
+        shape, full, gsize, two, one, writer(three), grad, stress, part, 2
+    )
+    head()
+    total = len(steps)
+    given = 0
+    for index, run in enumerate(steps):
+        upto = -(-len(edge) * (index + 1) // total)
+        for work in edge[given:upto]:
+            work()
+        given = max(given, upto)
+        run()
+    head, steps = main_steps(shape, full, gsize, three, two, finish, grad, stress, part, 3)
+    head()
+    for run in steps:
+        run()
 
 
 def partner(size, parity, i):
@@ -589,8 +636,8 @@
         prep_kernel(shape, *held, own, sent[2 : 2 + sides], sent[:2], sent[2 + sides :])
 
     outs = [f32(CH, sy + 1, sx, sz)]
-    outs += [f32(CH, sy // 2, 8, sz)] * 2 + [f32(CH, HALO, sx, sz)] * sides
-    outs += [f32(CH, HALO // 2, 8, sz)] * (2 * sides)
+    outs += [f32(len(CARRY), sy // 2, 8, sz)] * 2 + [f32(len(LAYERS), sx, sz)] * sides
+    outs += [f32(len(LAYERS) // 2, 8, sz)] * (2 * sides)
     own, *sent = call(
         prep,
         outs,
@@ -632,30 +679,27 @@
     )
     z0 = send(shape, z0, None, None, 0)
     z1 = send(shape, z1, None, None, 1)
-    (main,) = call(
+    one, two, gsize = call(
         functools.partial(main_kernel, shape),
-        [f32(3, rows + 2, 2, 8, sz)],
+        [f32(3, rows, 2, 8, sz), f32(3, rows, 2, 8, sz), f32(rows, 2, 8, sz)],
         (full,),
-        [
-            scratch(3, rows + 2, 2, 8, sz),
-            scratch(rows + 2, 2, 8, sz),
-            scratch(9, rows + 2, 2, 8, sz),
-            scratch(9, rows + 2, 2, 8, sz),
-            scratch(6, rows + 2, 2, 8, sz),
-        ],
-    )
+        [scratch(count, rows, 2, 8, sz) for count in (9, 9, 6)],
+    )
+
+    def last(*refs):
+        ends = 11 + ITERS + 1
+        last_kernel(shape, *refs[:11], refs[11:ends], *refs[ends:])
+
     (out,) = call(
-        functools.partial(edge_kernel, shape),
+        last,
         [f32(3, sx * sy, sz)],
-        (full, main, z0, z1),
-        [
-            scratch(3, erows, 2, 8, sz),
-            scratch(3, erows, 2, 8, sz),
-            scratch(3, erows, 2, 8, sz),
-            scratch(erows, 2, 8, sz),
-            scratch(erows, 2, 8, sz),
-            scratch(2 * 8, sz),
-        ],
+        (full, one, two, gsize, z0, z1),
+        [scratch(3, rows, 2, 8, sz)]
+        + [scratch(count, rows, 2, 8, sz) for count in (9, 9, 6)]
+        + [scratch(3, erows, 2, 8, sz) for _ in range(ITERS + 2)]
+        + [scratch(erows, 2, 8, sz)] * 2
+        + [scratch(9, erows + 1, 2, 8, sz)] * 2
+        + [scratch(sy, 3, 2 * 8, sz)],
     )
     return out.reshape(3, sx, sy, sz)
 

time: 25.4 us -> 23.8 us (0.937)
  Pallas kernels: 12.3 us -> 11.2 us
  starting transfers between devices: 10.1 us -> 9.76 us
    pallas_call x4, Pallas kernels: 12.3 us -> 11.2 us  [call(): pl.pallas_call(body, out_shape=outs, in_specs=specs or [VM] * len(args),...]
    ppermute x7, starting transfers between devices: 10.1 us -> 9.76 us  [send(): return lax.ppermute(value, ('gx', 'gy', 'gz'), exchange(shape, parities))]
  transfers between devices with their start and end apart: 7 -> 7, of which waited for: 2 -> 1; matrix products, arithmetic and copies ran while one was open for 0% -> 0% of each run, Pallas kernels for 25% -> 15%
where the time goes in v3:
time: 23.8 us; the launch traced here: 23.6 us
  Pallas kernels  11.2 us (47%)
  starting transfers between devices  9.76 us (41%)
  waiting for transfers between devices  2.63 us (11%)
    pallas_call x4, Pallas kernels, call(): pl.pallas_call(body, out_shape=outs, in_specs=specs or [VM] * len(args),...  11.2 us
    ppermute x7, starting transfers between devices, send(): return lax.ppermute(value, ('gx', 'gy', 'gz'), exchange(shape, parities))  9.76 us
    ppermute x7, waiting for transfers between devices, send(): return lax.ppermute(value, ('gx', 'gy', 'gz'), exchange(shape, parities))  2.63 us
  transfers between devices with their start and end apart: 7, of which 1 were waited for; matrix products, arithmetic and copies ran while one was open for 0% of the time, Pallas kernels for 15%

profile of v3, /device:TPU:9, one launch (start us, length us, event | category | flops | bytes accessed | tf_op | source)
XLA Modules:
  0.0 23.6 jit_solution(8909771647559856050)
XLA Ops:
  0.0 1.1 %shard_map.55 = (f32[8,9,8,128]{3,2,1,0:T(8,128)S(1)}, f32[7,4,8,128]{3,2,1,0:T(8,128)S(1)}, f32[7,4,8,128]{3,2,1,0:T(8,128)S(1)}, f32[28,8,128]{2,1,0:T(8,128)S...) custom-call(f32[3,64,128]{2,1,0:T(8,128)} %bitcast.5, f32[3,64,128]{2,1,0:T(8,128)} %bitcast.6, ...), custom_call_target="tpu_custom_call" | custom-call | flops 2000000 | bytes 100000 | tf_op jit(solution)/shard_map/pallas_call | solution.py:611
  1.1 0.1 collective-permute-start
  1.2 2.6 %collective-permute-start.1 = (f32[7,4,8,128]{3,2,1,0:T(8,128)S(1)}, f32[7,4,8,128]{3,2,1,0:T(8,128)S(1)}, u32[]{:S(2)}, u32[]{:S(2)}) collective-permute-start(f32[7,4,8,128]{3,2,1,0:T(8,128)S(1)} %get-tuple-element.19), channel_id=1, source_target_pairs={{0,1},{1,0},{2,3},{3,2},{4,5},{5,4},{6,7},{7,6},{8,16},{9,17},{10,... | collective-permute-start | bytes 344072 | tf_op jit(solution)/shard_map/ppermute | solution.py:595
  3.8 1.2 %collective-permute-start.2 = (f32[28,8,128]{2,1,0:T(8,128)S(1)}, f32[28,8,128]{2,1,0:T(8,128)S(1)}, u32[]{:S(2)}, u32[]{:S(2)}) collective-permute-start(f32[28,8,128]{2,1,0:T(8,128)S(1)} %get-tuple-element.20), channel_id=1, source_target_pairs={{0,4},{1,5},{2,6},{3,7},{4,0},{5,1},{6,2},{7,3},{8,12},{9,13},{10,... | collective-permute-start | bytes 344072 | tf_op jit(solution)/shard_map/ppermute | solution.py:595
  5.0 0.0 collective-permute-start.3
  5.0 2.0 %collective-permute-start.4 = (f32[14,8,128]{2,1,0:T(8,128)S(1)}, f32[14,8,128]{2,1,0:T(8,128)S(1)}, u32[]{:S(2)}, u32[]{:S(2)}) collective-permute-start(f32[14,8,128]{2,1,0:T(8,128)S(1)} %get-tuple-element.22), channel_id=1, source_target_pairs={{0,1},{1,0},{2,3},{3,2},{4,5},{5,4},{6,7},{7,6},{8,20},{9,21},{10,... | collective-permute-start | bytes 172040 | tf_op jit(solution)/shard_map/ppermute | solution.py:595
  7.1 2.6 %collective-permute-done.3.rest_3_ = f32[14,8,128]{2,1,0:T(8,128)S(1)} collective-permute-done((f32[14,8,128]{2,1,0:T(8,128)S(1)}, f32[14,8,128]{2,1,0:T(8,128)S(1)}, u32[]{:S(2)}, u32[]{:S(2)}) %collective-permute-start.3) | collective-permute-done | bytes 57376 | tf_op jit(solution)/shard_map/ppermute | solution.py:595
  9.7 0.0 collective-permute-done.4.rest_4_
  9.7 0.0 collective-permute-done.rest_0_
  9.7 0.0 collective-permute-done.1.rest_1_
  9.7 0.0 collective-permute-done.2.rest_2_
  9.7 0.5 %shard_map.56 = (f32[8,12,2,8,128]{4,3,2,1,0:T(8,128)S(1)}, f32[3,2,8,128]{3,2,1,0:T(8,128)S(1)}, f32[3,2,8,128]{3,2,1,0:T(8,128)S(1)}) custom-call(f32[8,9,8,128]{3,2,1,0:T(8,128)S(1)} %get-tuple-element.17.own, f32[7,4,8,128]{3,2,1,0:T(8,128)S(1)} %collective-permute-done.rest_0_, f32[7,4,8,128]{3,2,1,0:T(8,128)S(1)} %collective-permute-done.1.rest_1_, ...), custom_call_target="tpu_custom_call" | custom-call | flops 2000000 | bytes 100000 | tf_op jit(solution)/shard_map/pallas_call | solution.py:611
  10.2 2.7 %collective-permute-start.5 = (f32[3,2,8,128]{3,2,1,0:T(8,128)S(1)}, f32[3,2,8,128]{3,2,1,0:T(8,128)S(1)}, u32[]{:S(2)}, u32[]{:S(2)}) collective-permute-start(f32[3,2,8,128]{3,2,1,0:T(8,128)S(1)} %get-tuple-element.27), channel_id=1, source_target_pairs={{0,1},{1,0},{2,3},{3,2},{4,5},{5,4},{6,7},{7,6},{8,9},{9,8},{10,11... | collective-permute-start | bytes 73736 | tf_op jit(solution)/shard_map/ppermute | solution.py:595
  12.9 1.2 %collective-permute-start.6 = (f32[3,2,8,128]{3,2,1,0:T(8,128)S(1)}, f32[3,2,8,128]{3,2,1,0:T(8,128)S(1)}, u32[]{:S(2)}, u32[]{:S(2)}) collective-permute-start(f32[3,2,8,128]{3,2,1,0:T(8,128)S(1)} %get-tuple-element.28), channel_id=1, source_target_pairs={{0,4},{1,2},{2,1},{3,7},{4,0},{5,6},{6,5},{7,3},{8,12},{9,10},{10,... | collective-permute-start | bytes 73736 | tf_op jit(solution)/shard_map/ppermute | solution.py:595
  14.1 3.5 %shard_map.57 = (f32[3,12,2,8,128]{4,3,2,1,0:T(8,128)S(1)}, f32[3,12,2,8,128]{4,3,2,1,0:T(8,128)S(1)}, f32[12,2,8,128]{3,2,1,0:T(8,128)S(1)}) custom-call(f32[8,12,2,8,128]{4,3,2,1,0:T(8,128)S(1)} %get-tuple-element.23.full.refs_0_), custom_call_target="tpu_custom_call" | custom-call | flops 2000000 | bytes 100000 | tf_op jit(solution)/shard_map/pallas_call | solution.py:611
  17.6 0.0 collective-permute-done.5.refs_4_
  17.6 0.0 collective-permute-done.6.refs_5_
  17.6 6.0 %shard_map.58 = f32[3,64,128]{2,1,0:T(8,128)} custom-call(f32[8,12,2,8,128]{4,3,2,1,0:T(8,128)S(1)} %get-tuple-element.23.full.refs_0_, f32[3,12,2,8,128]{4,3,2,1,0:T(8,128)S(1)} %get-tuple-element.24.refs_1_, f32[3,12,2,8,128]{4,3,2,1,0:T(8,128)S(1)} %get-tuple-element.25.refs_2_, f32[12,2,8,128]{3,2,1,0:T(8,128)S(1)} %get-tuple-element.26.refs_3_, ...), custom_call_target="tpu_custom_call" | custom-call | flops 2000000 | bytes 100000 | tf_op jit(solution)/shard_map/pallas_call | solution.py:611
Async XLA Ops:
  1.1 8.5 %collective-permute-start = (f32[7,4,8,128]{3,2,1,0:T(8,128)S(1)}, f32[7,4,8,128]{3,2,1,0:T(8,128)S(1)}, u32[]{:S(2)}, u32[]{:S(2)}) collective-permute-start(f32[7,4,8,128]{3,2,1,0:T(8,128)S(1)} %get-tuple-element.18), channel_id=1, source_target_pairs={{0,8},{1,9},{2,10},{3,11},{4,12},{5,13},{6,14},{7,15},{8,0},{9,1},... | collective-permute-start | bytes 344072 | tf_op jit(solution)/shard_map/ppermute | solution.py:595
  1.2 8.5 %collective-permute-start.1 = (f32[7,4,8,128]{3,2,1,0:T(8,128)S(1)}, f32[7,4,8,128]{3,2,1,0:T(8,128)S(1)}, u32[]{:S(2)}, u32[]{:S(2)}) collective-permute-start(f32[7,4,8,128]{3,2,1,0:T(8,128)S(1)} %get-tuple-element.19), channel_id=1, source_target_pairs={{0,1},{1,0},{2,3},{3,2},{4,5},{5,4},{6,7},{7,6},{8,16},{9,17},{10,... | collective-permute-start | bytes 344072 | tf_op jit(solution)/shard_map/ppermute | solution.py:595
  3.8 5.9 %collective-permute-start.2 = (f32[28,8,128]{2,1,0:T(8,128)S(1)}, f32[28,8,128]{2,1,0:T(8,128)S(1)}, u32[]{:S(2)}, u32[]{:S(2)}) collective-permute-start(f32[28,8,128]{2,1,0:T(8,128)S(1)} %get-tuple-element.20), channel_id=1, source_target_pairs={{0,4},{1,5},{2,6},{3,7},{4,0},{5,1},{6,2},{7,3},{8,12},{9,13},{10,... | collective-permute-start | bytes 344072 | tf_op jit(solution)/shard_map/ppermute | solution.py:595
  5.0 4.6 %collective-permute-start.3 = (f32[14,8,128]{2,1,0:T(8,128)S(1)}, f32[14,8,128]{2,1,0:T(8,128)S(1)}, u32[]{:S(2)}, u32[]{:S(2)}) collective-permute-start(f32[14,8,128]{2,1,0:T(8,128)S(1)} %get-tuple-element.21), channel_id=1, source_target_pairs={{0,12},{1,13},{2,14},{3,15},{4,8},{5,9},{6,10},{7,11},{8,4},{9,5},... | collective-permute-start | bytes 172040 | tf_op jit(solution)/shard_map/ppermute | solution.py:595
  5.0 4.6 %collective-permute-start.4 = (f32[14,8,128]{2,1,0:T(8,128)S(1)}, f32[14,8,128]{2,1,0:T(8,128)S(1)}, u32[]{:S(2)}, u32[]{:S(2)}) collective-permute-start(f32[14,8,128]{2,1,0:T(8,128)S(1)} %get-tuple-element.22), channel_id=1, source_target_pairs={{0,1},{1,0},{2,3},{3,2},{4,5},{5,4},{6,7},{7,6},{8,20},{9,21},{10,... | collective-permute-start | bytes 172040 | tf_op jit(solution)/shard_map/ppermute | solution.py:595
  10.2 7.4 %collective-permute-start.5 = (f32[3,2,8,128]{3,2,1,0:T(8,128)S(1)}, f32[3,2,8,128]{3,2,1,0:T(8,128)S(1)}, u32[]{:S(2)}, u32[]{:S(2)}) collective-permute-start(f32[3,2,8,128]{3,2,1,0:T(8,128)S(1)} %get-tuple-element.27), channel_id=1, source_target_pairs={{0,1},{1,0},{2,3},{3,2},{4,5},{5,4},{6,7},{7,6},{8,9},{9,8},{10,11... | collective-permute-start | bytes 73736 | tf_op jit(solution)/shard_map/ppermute | solution.py:595
  12.9 4.7 %collective-permute-start.6 = (f32[3,2,8,128]{3,2,1,0:T(8,128)S(1)}, f32[3,2,8,128]{3,2,1,0:T(8,128)S(1)}, u32[]{:S(2)}, u32[]{:S(2)}) collective-permute-start(f32[3,2,8,128]{3,2,1,0:T(8,128)S(1)} %get-tuple-element.28), channel_id=1, source_target_pairs={{0,4},{1,2},{2,1},{3,7},{4,0},{5,6},{6,5},{7,3},{8,12},{9,10},{10,... | collective-permute-start | bytes 73736 | tf_op jit(solution)/shard_map/ppermute | solution.py:595

commit v4 on v3

--- a/solution.py
+++ b/solution.py
@@ -85,41 +85,90 @@
     return out
 
 
+THIRD_ANGLE = (
+    0.866025405599564,
+    0.16666637114459312,
+    -0.04810444145461756,
+    0.02460429680494765,
+    -0.01510727520943827,
+    0.009383330672620772,
+    -0.004929691292929874,
+    0.0017648569477158788,
+    -0.0003028542202729437,
+)
+
+
 def polar_stress(f, weight):
-    def gram(z):
-        return {
-            (i, j): z[0][i] * z[0][j] + z[1][i] * z[1][j] + z[2][i] * z[2][j]
-            for i in range(3)
-            for j in range(i, 3)
-        }
-
-    def apply(z, diag, off):
-        rows = []
-        for c in range(3):
-            row = []
-            for d in range(3):
-                value = z[c][d] * diag[d]
-                for j in range(3):
-                    if j != d:
-                        value = value - z[c][j] * off[(min(j, d), max(j, d))]
-                row.append(value)
-            rows.append(row)
-        return rows
-
-    g = gram(f)
-    trace = g[(0, 0)] + g[(1, 1)] + g[(2, 2)]
+    xx, yy, zz = (f[0][i] * f[0][i] + f[1][i] * f[1][i] + f[2][i] * f[2][i] for i in range(3))
+    xy, xz, yz = (
+        f[0][i] * f[0][j] + f[1][i] * f[1][j] + f[2][i] * f[2][j]
+        for i, j in ((0, 1), (0, 2), (1, 2))
+    )
+    trace = xx + yy + zz
     s = jnp.minimum(lax.rsqrt(trace * (2.0 / 3.0)), 1.0)
-    cube = s * s * s
-    base = 1.5 * s
-    z = apply(
-        f,
-        [base - cube * g[(i, i)] for i in range(3)],
-        {key: cube * g[key] for key in ((0, 1), (0, 2), (1, 2))},
-    )
-    for _ in range(POLAR_STEPS - 1):
-        g = gram(z)
-        z = apply(z, [1.5 - g[(i, i)] for i in range(3)], g)
-    return [[weight * (z[c][d] - f[c][d]) for d in range(3)] for c in range(3)]
+    s2 = s * s
+    mean = trace * (1.0 / 3.0)
+    xx, yy, zz = xx - mean, yy - mean, zz - mean
+    xy2, xz2, yz2 = xy * xy, xz * xz, yz * yz
+    xyz = xy * xz
+    sx2, sy2, sz2 = xx * xx + xy2, yy * yy + yz2, zz * zz + xz2
+    spread = (sx2 + sy2 + sz2 + (xy2 + yz2 + xz2)) * (1.0 / 6.0)
+    inverse = lax.rsqrt(jnp.maximum(spread, 1e-24))
+    cross = xyz * yz
+    det = xx * (yy * zz - yz2) + (cross + cross) - yy * xz2 - zz * xy2
+    ratio = (det * 0.5) * inverse * inverse * inverse
+    radius = spread * inverse * s2
+    turn = jnp.minimum(jnp.abs(ratio), 1.0)
+    c = jnp.full_like(turn, THIRD_ANGLE[-1])
+    for value in THIRD_ANGLE[-2::-1]:
+        c = c * turn + value
+    square = jnp.maximum(1.0 - c * c, 1e-20)
+    apart = radius * math.sqrt(3.0) * (square * lax.rsqrt(square))
+    half = jnp.where(ratio < 0.0, -radius, radius) * c
+    near = (apart - half, -apart - half, half + half)
+    center = mean * s2
+    level = [v + center for v in near]
+    slope = None
+    for step in range(POLAR_STEPS):
+        m = [1.5 - v for v in level]
+        if step == 0:
+            q, dq = list(m), -1.0
+        else:
+            dq = dq * m[0] - q[1] * slope
+            q = [a * b for a, b in zip(q, m)]
+        if step < POLAR_STEPS - 1:
+            m2 = [v * v for v in m]
+            growth = m2[0] - level[1] * (m[0] + m[1])
+            slope = growth if slope is None else slope * growth
+            level = [a * b for a, b in zip(level, m2)]
+    gap1, gap2 = near[0] - near[2], near[1] - near[2]
+    inv = pl.reciprocal(jnp.maximum(gap1 * gap2, 1e-30))
+    bend = (dq - (q[1] - q[2]) * (gap1 * inv)) * (gap2 * inv)
+    k0 = (q[0] - dq * near[0] + bend * (near[0] * near[1])) * s
+    k1 = (dq - bend * (near[0] + near[1])) * (s * s2)
+    k2 = bend * (s * (s2 * s2))
+    diag = (
+        k0 + k1 * xx + k2 * (sx2 + xz2),
+        k0 + k1 * yy + k2 * (sy2 + xy2),
+        k0 + k1 * zz + k2 * (sz2 + yz2),
+    )
+    off = {
+        (0, 1): k1 * xy + k2 * (xy * (xx + yy) + xz * yz),
+        (0, 2): k1 * xz + k2 * (xz * (xx + zz) + xy * yz),
+        (1, 2): k1 * yz + k2 * (yz * (yy + zz) + xyz),
+    }
+    diag = tuple(v - 1.0 for v in diag)
+    out = []
+    for c in range(3):
+        row = []
+        for d in range(3):
+            value = f[c][d] * diag[d]
+            for j in range(3):
+                if j != d:
+                    value = value + f[c][j] * off[(min(j, d), max(j, d))]
+            row.append(weight * value)
+        out.append(row)
+    return out
 
 
 def deform_rows(low, high):

time: 23.8 us -> 21.8 us (0.916)
  Pallas kernels: 11.2 us -> 9.16 us
    pallas_call x4, Pallas kernels: 11.2 us -> 9.16 us  [call(): pl.pallas_call(body, out_shape=outs, in_specs=specs or [VM] * len(args),...]
  transfers between devices with their start and end apart: 7 -> 7, of which waited for: 1 -> 1; matrix products, arithmetic and copies ran while one was open for 0% -> 0% of each run, Pallas kernels for 15% -> 12%
where the time goes in v4:
time: 21.8 us; the launch traced here: 21.6 us
  starting transfers between devices  9.76 us (45%)
  Pallas kernels  9.16 us (42%)
  waiting for transfers between devices  2.63 us (12%)
    ppermute x7, starting transfers between devices, send(): return lax.ppermute(value, ('gx', 'gy', 'gz'), exchange(shape, parities))  9.76 us
    pallas_call x4, Pallas kernels, call(): pl.pallas_call(body, out_shape=outs, in_specs=specs or [VM] * len(args),...  9.16 us
    ppermute x7, waiting for transfers between devices, send(): return lax.ppermute(value, ('gx', 'gy', 'gz'), exchange(shape, parities))  2.63 us
  transfers between devices with their start and end apart: 7, of which 1 were waited for; matrix products, arithmetic and copies ran while one was open for 0% of the time, Pallas kernels for 12%

profile of v4, /device:TPU:9, one launch (start us, length us, event | category | flops | bytes accessed | tf_op | source)
XLA Modules:
  0.0 21.6 jit_solution(831543030347972156)
XLA Ops:
  0.0 1.1 %shard_map.55 = (f32[8,9,8,128]{3,2,1,0:T(8,128)S(1)}, f32[7,4,8,128]{3,2,1,0:T(8,128)S(1)}, f32[7,4,8,128]{3,2,1,0:T(8,128)S(1)}, f32[28,8,128]{2,1,0:T(8,128)S...) custom-call(f32[3,64,128]{2,1,0:T(8,128)} %bitcast.5, f32[3,64,128]{2,1,0:T(8,128)} %bitcast.6, ...), custom_call_target="tpu_custom_call" | custom-call | flops 2000000 | bytes 100000 | tf_op jit(solution)/shard_map/pallas_call | solution.py:660
  1.1 0.1 collective-permute-start
  1.2 2.6 %collective-permute-start.1 = (f32[7,4,8,128]{3,2,1,0:T(8,128)S(1)}, f32[7,4,8,128]{3,2,1,0:T(8,128)S(1)}, u32[]{:S(2)}, u32[]{:S(2)}) collective-permute-start(f32[7,4,8,128]{3,2,1,0:T(8,128)S(1)} %get-tuple-element.19), channel_id=1, source_target_pairs={{0,1},{1,0},{2,3},{3,2},{4,5},{5,4},{6,7},{7,6},{8,16},{9,17},{10,... | collective-permute-start | bytes 344072 | tf_op jit(solution)/shard_map/ppermute | solution.py:644
  3.8 1.2 %collective-permute-start.2 = (f32[28,8,128]{2,1,0:T(8,128)S(1)}, f32[28,8,128]{2,1,0:T(8,128)S(1)}, u32[]{:S(2)}, u32[]{:S(2)}) collective-permute-start(f32[28,8,128]{2,1,0:T(8,128)S(1)} %get-tuple-element.20), channel_id=1, source_target_pairs={{0,4},{1,5},{2,6},{3,7},{4,0},{5,1},{6,2},{7,3},{8,12},{9,13},{10,... | collective-permute-start | bytes 344072 | tf_op jit(solution)/shard_map/ppermute | solution.py:644
  5.0 0.0 collective-permute-start.3
  5.0 2.0 %collective-permute-start.4 = (f32[14,8,128]{2,1,0:T(8,128)S(1)}, f32[14,8,128]{2,1,0:T(8,128)S(1)}, u32[]{:S(2)}, u32[]{:S(2)}) collective-permute-start(f32[14,8,128]{2,1,0:T(8,128)S(1)} %get-tuple-element.22), channel_id=1, source_target_pairs={{0,1},{1,0},{2,3},{3,2},{4,5},{5,4},{6,7},{7,6},{8,20},{9,21},{10,... | collective-permute-start | bytes 172040 | tf_op jit(solution)/shard_map/ppermute | solution.py:644
  7.1 2.6 %collective-permute-done.3.rest_3_ = f32[14,8,128]{2,1,0:T(8,128)S(1)} collective-permute-done((f32[14,8,128]{2,1,0:T(8,128)S(1)}, f32[14,8,128]{2,1,0:T(8,128)S(1)}, u32[]{:S(2)}, u32[]{:S(2)}) %collective-permute-start.3) | collective-permute-done | bytes 57376 | tf_op jit(solution)/shard_map/ppermute | solution.py:644
  9.7 0.0 collective-permute-done.4.rest_4_
  9.7 0.0 collective-permute-done.rest_0_
  9.7 0.0 collective-permute-done.1.rest_1_
  9.7 0.0 collective-permute-done.2.rest_2_
  9.7 0.5 %shard_map.56 = (f32[8,12,2,8,128]{4,3,2,1,0:T(8,128)S(1)}, f32[3,2,8,128]{3,2,1,0:T(8,128)S(1)}, f32[3,2,8,128]{3,2,1,0:T(8,128)S(1)}) custom-call(f32[8,9,8,128]{3,2,1,0:T(8,128)S(1)} %get-tuple-element.17.own, f32[7,4,8,128]{3,2,1,0:T(8,128)S(1)} %collective-permute-done.rest_0_, f32[7,4,8,128]{3,2,1,0:T(8,128)S(1)} %collective-permute-done.1.rest_1_, ...), custom_call_target="tpu_custom_call" | custom-call | flops 2000000 | bytes 100000 | tf_op jit(solution)/shard_map/pallas_call | solution.py:660
  10.2 2.7 %collective-permute-start.5 = (f32[3,2,8,128]{3,2,1,0:T(8,128)S(1)}, f32[3,2,8,128]{3,2,1,0:T(8,128)S(1)}, u32[]{:S(2)}, u32[]{:S(2)}) collective-permute-start(f32[3,2,8,128]{3,2,1,0:T(8,128)S(1)} %get-tuple-element.27), channel_id=1, source_target_pairs={{0,1},{1,0},{2,3},{3,2},{4,5},{5,4},{6,7},{7,6},{8,9},{9,8},{10,11... | collective-permute-start | bytes 73736 | tf_op jit(solution)/shard_map/ppermute | solution.py:644
  12.9 1.2 %collective-permute-start.6 = (f32[3,2,8,128]{3,2,1,0:T(8,128)S(1)}, f32[3,2,8,128]{3,2,1,0:T(8,128)S(1)}, u32[]{:S(2)}, u32[]{:S(2)}) collective-permute-start(f32[3,2,8,128]{3,2,1,0:T(8,128)S(1)} %get-tuple-element.28), channel_id=1, source_target_pairs={{0,4},{1,2},{2,1},{3,7},{4,0},{5,6},{6,5},{7,3},{8,12},{9,10},{10,... | collective-permute-start | bytes 73736 | tf_op jit(solution)/shard_map/ppermute | solution.py:644
  14.1 2.5 %shard_map.57 = (f32[3,12,2,8,128]{4,3,2,1,0:T(8,128)S(1)}, f32[3,12,2,8,128]{4,3,2,1,0:T(8,128)S(1)}, f32[12,2,8,128]{3,2,1,0:T(8,128)S(1)}) custom-call(f32[8,12,2,8,128]{4,3,2,1,0:T(8,128)S(1)} %get-tuple-element.23.full.refs_0_), custom_call_target="tpu_custom_call" | custom-call | flops 2000000 | bytes 100000 | tf_op jit(solution)/shard_map/pallas_call | solution.py:660
  16.6 0.0 collective-permute-done.5.refs_4_
  16.6 0.0 collective-permute-done.6.refs_5_
  16.6 5.0 %shard_map.58 = f32[3,64,128]{2,1,0:T(8,128)} custom-call(f32[8,12,2,8,128]{4,3,2,1,0:T(8,128)S(1)} %get-tuple-element.23.full.refs_0_, f32[3,12,2,8,128]{4,3,2,1,0:T(8,128)S(1)} %get-tuple-element.24.refs_1_, f32[3,12,2,8,128]{4,3,2,1,0:T(8,128)S(1)} %get-tuple-element.25.refs_2_, f32[12,2,8,128]{3,2,1,0:T(8,128)S(1)} %get-tuple-element.26.refs_3_, ...), custom_call_target="tpu_custom_call" | custom-call | flops 2000000 | bytes 100000 | tf_op jit(solution)/shard_map/pallas_call | solution.py:660
Async XLA Ops:
  1.1 8.5 %collective-permute-start = (f32[7,4,8,128]{3,2,1,0:T(8,128)S(1)}, f32[7,4,8,128]{3,2,1,0:T(8,128)S(1)}, u32[]{:S(2)}, u32[]{:S(2)}) collective-permute-start(f32[7,4,8,128]{3,2,1,0:T(8,128)S(1)} %get-tuple-element.18), channel_id=1, source_target_pairs={{0,8},{1,9},{2,10},{3,11},{4,12},{5,13},{6,14},{7,15},{8,0},{9,1},... | collective-permute-start | bytes 344072 | tf_op jit(solution)/shard_map/ppermute | solution.py:644
  1.2 8.5 %collective-permute-start.1 = (f32[7,4,8,128]{3,2,1,0:T(8,128)S(1)}, f32[7,4,8,128]{3,2,1,0:T(8,128)S(1)}, u32[]{:S(2)}, u32[]{:S(2)}) collective-permute-start(f32[7,4,8,128]{3,2,1,0:T(8,128)S(1)} %get-tuple-element.19), channel_id=1, source_target_pairs={{0,1},{1,0},{2,3},{3,2},{4,5},{5,4},{6,7},{7,6},{8,16},{9,17},{10,... | collective-permute-start | bytes 344072 | tf_op jit(solution)/shard_map/ppermute | solution.py:644
  3.8 5.9 %collective-permute-start.2 = (f32[28,8,128]{2,1,0:T(8,128)S(1)}, f32[28,8,128]{2,1,0:T(8,128)S(1)}, u32[]{:S(2)}, u32[]{:S(2)}) collective-permute-start(f32[28,8,128]{2,1,0:T(8,128)S(1)} %get-tuple-element.20), channel_id=1, source_target_pairs={{0,4},{1,5},{2,6},{3,7},{4,0},{5,1},{6,2},{7,3},{8,12},{9,13},{10,... | collective-permute-start | bytes 344072 | tf_op jit(solution)/shard_map/ppermute | solution.py:644
  5.0 4.6 %collective-permute-start.3 = (f32[14,8,128]{2,1,0:T(8,128)S(1)}, f32[14,8,128]{2,1,0:T(8,128)S(1)}, u32[]{:S(2)}, u32[]{:S(2)}) collective-permute-start(f32[14,8,128]{2,1,0:T(8,128)S(1)} %get-tuple-element.21), channel_id=1, source_target_pairs={{0,12},{1,13},{2,14},{3,15},{4,8},{5,9},{6,10},{7,11},{8,4},{9,5},... | collective-permute-start | bytes 172040 | tf_op jit(solution)/shard_map/ppermute | solution.py:644
  5.0 4.6 %collective-permute-start.4 = (f32[14,8,128]{2,1,0:T(8,128)S(1)}, f32[14,8,128]{2,1,0:T(8,128)S(1)}, u32[]{:S(2)}, u32[]{:S(2)}) collective-permute-start(f32[14,8,128]{2,1,0:T(8,128)S(1)} %get-tuple-element.22), channel_id=1, source_target_pairs={{0,1},{1,0},{2,3},{3,2},{4,5},{5,4},{6,7},{7,6},{8,20},{9,21},{10,... | collective-permute-start | bytes 172040 | tf_op jit(solution)/shard_map/ppermute | solution.py:644
  10.2 6.4 %collective-permute-start.5 = (f32[3,2,8,128]{3,2,1,0:T(8,128)S(1)}, f32[3,2,8,128]{3,2,1,0:T(8,128)S(1)}, u32[]{:S(2)}, u32[]{:S(2)}) collective-permute-start(f32[3,2,8,128]{3,2,1,0:T(8,128)S(1)} %get-tuple-element.27), channel_id=1, source_target_pairs={{0,1},{1,0},{2,3},{3,2},{4,5},{5,4},{6,7},{7,6},{8,9},{9,8},{10,11... | collective-permute-start | bytes 73736 | tf_op jit(solution)/shard_map/ppermute | solution.py:644
  12.9 3.7 %collective-permute-start.6 = (f32[3,2,8,128]{3,2,1,0:T(8,128)S(1)}, f32[3,2,8,128]{3,2,1,0:T(8,128)S(1)}, u32[]{:S(2)}, u32[]{:S(2)}) collective-permute-start(f32[3,2,8,128]{3,2,1,0:T(8,128)S(1)} %get-tuple-element.28), channel_id=1, source_target_pairs={{0,4},{1,2},{2,1},{3,7},{4,0},{5,6},{6,5},{7,3},{8,12},{9,10},{10,... | collective-permute-start | bytes 73736 | tf_op jit(solution)/shard_map/ppermute | solution.py:644

commit v5 on v4

--- a/solution.py
+++ b/solution.py
@@ -412,7 +412,57 @@
     return [[(ref[3 * c + k, row, 0], ref[3 * c + k, row, 1]) for k in range(3)] for c in range(3)]
 
 
-def main_steps(shape, full, gsize, old, oldest, write, grad, stress, part, step):
+def packed_stresses(shape, full, step, rows, flat):
+    fflat, wflat, pflat = flat
+    width = shape.size[0] + 2 * HALO - 1 - 2 * step
+    spans = []
+    for t in range(2):
+        first = -(-(step - t) // 2)
+        spans.append((first, (shape.size[0] + 2 * HALO - 2 - t - step) // 2 - first + 1))
+    begin = rows[0]
+    state = {"tiles": 0, "rows": 0}
+
+    def at(j, t, first, count):
+        return pl.ds(8 + (j - begin) * width + 2 * first + t - step, count, stride=2)
+
+    def run(j, f):
+        for t, (first, count) in enumerate(spans):
+            here = at(j, t, first, count)
+            part = slice(first, first + count)
+            for c in range(3):
+                for d in range(3):
+                    fflat[3 * c + d, here, :] = f[c][d][t][part]
+            wflat[here, :] = full[W_CH, j, t][part]
+        filled = (j - begin + 1) * width
+        upto = filled // 8 if j < rows[-1] else -(-filled // 8)
+        for i in range(state["tiles"], upto):
+            tile = pl.ds(8 + 8 * i, 8)
+            p = polar_stress(
+                [[fflat[3 * c + d, tile, :] for d in range(3)] for c in range(3)], wflat[tile, :]
+            )
+            for c in range(3):
+                for d in range(3):
+                    pflat[3 * c + d, tile, :] = p[c][d]
+        state["tiles"] = upto
+        known = []
+        while state["rows"] < len(rows) and (state["rows"] + 1) * width <= 8 * upto:
+            r = begin + state["rows"]
+            known.append(
+                (
+                    r,
+                    [
+                        [tuple(pflat[3 * c + d, at(r, t, 0, 8), :] for t in range(2)) for d in range(3)]
+                        for c in range(3)
+                    ],
+                )
+            )
+            state["rows"] += 1
+        return known
+
+    return run
+
+
+def main_steps(shape, full, gsize, old, oldest, write, grad, stress, part, step, flat=None):
     omega = omegas()[step]
     first = 0 if shape.mirror else step
     last = shape.rows - 1 - step
@@ -439,24 +489,30 @@
         for row in (first, first + 1):
             put9(grad, row, gradient_row(load_row(old, row)))
 
+    if flat:
+        packed = packed_stresses(shape, full, step, range(first, last), flat)
+
     def body(j):
         after = gradient_row(load_row(old, j + 2)) if j + 2 <= last else None
-        now = stress_row(
-            deform_rows(get9(grad, j), get9(grad, j + 1)), load_row(full, j, (W_CH,))[0]
-        )
-        before = get9(stress, j - 1) if j > first else [[(zero, zero)] * 3] * 3
-        parts = force_parts(now, before)
-        if j > first:
-            update(j - 1)
+        f = deform_rows(get9(grad, j), get9(grad, j + 1))
+        if flat:
+            known = packed(j, f)
+        else:
+            known = [(j, stress_row(f, load_row(full, j, (W_CH,))[0]))]
         if after is not None:
             put9(grad, j + 2, after)
-        put9(stress, j, now)
-        for c in range(3):
-            for t in range(2):
-                for i in range(2):
-                    part[2 * c + i, j, t] = parts[c][i][t]
-        if j == last - 1:
-            update(j)
+        for r, now in known:
+            before = get9(stress, r - 1) if r > first else [[(zero, zero)] * 3] * 3
+            parts = force_parts(now, before)
+            if r > first:
+                update(r - 1)
+            put9(stress, r, now)
+            for c in range(3):
+                for t in range(2):
+                    for i in range(2):
+                        part[2 * c + i, r, t] = parts[c][i][t]
+            if r == last - 1:
+                update(r)
 
     return head, [functools.partial(body, j) for j in range(first, last)]
 
@@ -559,7 +615,7 @@
 
 def last_kernel(
     shape, full, one, two, gsize, zrecv0, zrecv1, out,
-    three, grad, stress, part, bufs, egoal, egsize, estiff, egrad, estress, tiles,
+    three, grad, stress, part, bufs, egoal, egsize, estiff, egrad, estress, tiles, *flat,
 ):
     sx, sy, sz = shape.size
     erows = shape.erows
@@ -594,7 +650,7 @@
         edge.append(lambda order=order: [stresses(m) for m in order])
         edge.append(lambda step=step: [updates(step, m) for m in range(erows)])
     head, steps = main_steps(
-        shape, full, gsize, two, one, writer(three), grad, stress, part, 2
+        shape, full, gsize, two, one, writer(three), grad, stress, part, 2, flat
     )
     head()
     total = len(steps)
@@ -605,7 +661,7 @@
             work()
         given = max(given, upto)
         run()
-    head, steps = main_steps(shape, full, gsize, three, two, finish, grad, stress, part, 3)
+    head, steps = main_steps(shape, full, gsize, three, two, finish, grad, stress, part, 3, flat)
     head()
     for run in steps:
         run()
@@ -748,7 +804,8 @@
         + [scratch(3, erows, 2, 8, sz) for _ in range(ITERS + 2)]
         + [scratch(erows, 2, 8, sz)] * 2
         + [scratch(9, erows + 1, 2, 8, sz)] * 2
-        + [scratch(sy, 3, 2 * 8, sz)],
+        + [scratch(sy, 3, 2 * 8, sz)]
+        + [scratch(9, 16 * (rows + 2), sz), scratch(16 * (rows + 2), sz), scratch(9, 16 * (rows + 2), sz)],
     )
     return out.reshape(3, sx, sy, sz)
 

time: 21.8 us -> 21.4 us (0.982)
  Pallas kernels: 9.16 us -> 8.8 us
    pallas_call x4, Pallas kernels: 9.16 us -> 8.8 us  [call(): pl.pallas_call(body, out_shape=outs, in_specs=specs or [VM] * len(args),...]
where the time goes in v5:
time: 21.4 us; the launch traced here: 21.2 us
  starting transfers between devices  9.76 us (46%)
  Pallas kernels  8.8 us (41%)
  waiting for transfers between devices  2.63 us (12%)
    ppermute x7, starting transfers between devices, send(): return lax.ppermute(value, ('gx', 'gy', 'gz'), exchange(shape, parities))  9.76 us
    pallas_call x4, Pallas kernels, call(): pl.pallas_call(body, out_shape=outs, in_specs=specs or [VM] * len(args),...  8.8 us
    ppermute x7, waiting for transfers between devices, send(): return lax.ppermute(value, ('gx', 'gy', 'gz'), exchange(shape, parities))  2.63 us
  transfers between devices with their start and end apart: 7, of which 1 were waited for; matrix products, arithmetic and copies ran while one was open for 0% of the time, Pallas kernels for 12%

profile of v5, /device:TPU:9, one launch (start us, length us, event | category | flops | bytes accessed | tf_op | source)
XLA Modules:
  0.0 21.2 jit_solution(6322623952671151627)
XLA Ops:
  0.0 1.1 %shard_map.55 = (f32[8,9,8,128]{3,2,1,0:T(8,128)S(1)}, f32[7,4,8,128]{3,2,1,0:T(8,128)S(1)}, f32[7,4,8,128]{3,2,1,0:T(8,128)S(1)}, f32[28,8,128]{2,1,0:T(8,128)S...) custom-call(f32[3,64,128]{2,1,0:T(8,128)} %bitcast.5, f32[3,64,128]{2,1,0:T(8,128)} %bitcast.6, ...), custom_call_target="tpu_custom_call" | custom-call | flops 2000000 | bytes 100000 | tf_op jit(solution)/shard_map/pallas_call | solution.py:716
  1.1 0.1 collective-permute-start
  1.2 2.6 %collective-permute-start.1 = (f32[7,4,8,128]{3,2,1,0:T(8,128)S(1)}, f32[7,4,8,128]{3,2,1,0:T(8,128)S(1)}, u32[]{:S(2)}, u32[]{:S(2)}) collective-permute-start(f32[7,4,8,128]{3,2,1,0:T(8,128)S(1)} %get-tuple-element.19), channel_id=1, source_target_pairs={{0,1},{1,0},{2,3},{3,2},{4,5},{5,4},{6,7},{7,6},{8,16},{9,17},{10,... | collective-permute-start | bytes 344072 | tf_op jit(solution)/shard_map/ppermute | solution.py:700
  3.8 1.2 %collective-permute-start.2 = (f32[28,8,128]{2,1,0:T(8,128)S(1)}, f32[28,8,128]{2,1,0:T(8,128)S(1)}, u32[]{:S(2)}, u32[]{:S(2)}) collective-permute-start(f32[28,8,128]{2,1,0:T(8,128)S(1)} %get-tuple-element.20), channel_id=1, source_target_pairs={{0,4},{1,5},{2,6},{3,7},{4,0},{5,1},{6,2},{7,3},{8,12},{9,13},{10,... | collective-permute-start | bytes 344072 | tf_op jit(solution)/shard_map/ppermute | solution.py:700
  5.0 0.0 collective-permute-start.3
  5.0 2.0 %collective-permute-start.4 = (f32[14,8,128]{2,1,0:T(8,128)S(1)}, f32[14,8,128]{2,1,0:T(8,128)S(1)}, u32[]{:S(2)}, u32[]{:S(2)}) collective-permute-start(f32[14,8,128]{2,1,0:T(8,128)S(1)} %get-tuple-element.22), channel_id=1, source_target_pairs={{0,1},{1,0},{2,3},{3,2},{4,5},{5,4},{6,7},{7,6},{8,20},{9,21},{10,... | collective-permute-start | bytes 172040 | tf_op jit(solution)/shard_map/ppermute | solution.py:700
  7.1 2.6 %collective-permute-done.3.rest_3_ = f32[14,8,128]{2,1,0:T(8,128)S(1)} collective-permute-done((f32[14,8,128]{2,1,0:T(8,128)S(1)}, f32[14,8,128]{2,1,0:T(8,128)S(1)}, u32[]{:S(2)}, u32[]{:S(2)}) %collective-permute-start.3) | collective-permute-done | bytes 57376 | tf_op jit(solution)/shard_map/ppermute | solution.py:700
  9.7 0.0 collective-permute-done.4.rest_4_
  9.7 0.0 collective-permute-done.rest_0_
  9.7 0.0 collective-permute-done.1.rest_1_
  9.7 0.0 collective-permute-done.2.rest_2_
  9.7 0.5 %shard_map.56 = (f32[8,12,2,8,128]{4,3,2,1,0:T(8,128)S(1)}, f32[3,2,8,128]{3,2,1,0:T(8,128)S(1)}, f32[3,2,8,128]{3,2,1,0:T(8,128)S(1)}) custom-call(f32[8,9,8,128]{3,2,1,0:T(8,128)S(1)} %get-tuple-element.17.own, f32[7,4,8,128]{3,2,1,0:T(8,128)S(1)} %collective-permute-done.rest_0_, f32[7,4,8,128]{3,2,1,0:T(8,128)S(1)} %collective-permute-done.1.rest_1_, ...), custom_call_target="tpu_custom_call" | custom-call | flops 2000000 | bytes 100000 | tf_op jit(solution)/shard_map/pallas_call | solution.py:716
  10.2 2.7 %collective-permute-start.5 = (f32[3,2,8,128]{3,2,1,0:T(8,128)S(1)}, f32[3,2,8,128]{3,2,1,0:T(8,128)S(1)}, u32[]{:S(2)}, u32[]{:S(2)}) collective-permute-start(f32[3,2,8,128]{3,2,1,0:T(8,128)S(1)} %get-tuple-element.27), channel_id=1, source_target_pairs={{0,1},{1,0},{2,3},{3,2},{4,5},{5,4},{6,7},{7,6},{8,9},{9,8},{10,11... | collective-permute-start | bytes 73736 | tf_op jit(solution)/shard_map/ppermute | solution.py:700
  12.9 1.2 %collective-permute-start.6 = (f32[3,2,8,128]{3,2,1,0:T(8,128)S(1)}, f32[3,2,8,128]{3,2,1,0:T(8,128)S(1)}, u32[]{:S(2)}, u32[]{:S(2)}) collective-permute-start(f32[3,2,8,128]{3,2,1,0:T(8,128)S(1)} %get-tuple-element.28), channel_id=1, source_target_pairs={{0,4},{1,2},{2,1},{3,7},{4,0},{5,6},{6,5},{7,3},{8,12},{9,10},{10,... | collective-permute-start | bytes 73736 | tf_op jit(solution)/shard_map/ppermute | solution.py:700
  14.1 2.5 %shard_map.57 = (f32[3,12,2,8,128]{4,3,2,1,0:T(8,128)S(1)}, f32[3,12,2,8,128]{4,3,2,1,0:T(8,128)S(1)}, f32[12,2,8,128]{3,2,1,0:T(8,128)S(1)}) custom-call(f32[8,12,2,8,128]{4,3,2,1,0:T(8,128)S(1)} %get-tuple-element.23.full.refs_0_), custom_call_target="tpu_custom_call" | custom-call | flops 2000000 | bytes 100000 | tf_op jit(solution)/shard_map/pallas_call | solution.py:716
  16.6 0.0 collective-permute-done.5.refs_4_
  16.6 0.0 collective-permute-done.6.refs_5_
  16.6 4.6 %shard_map.58 = f32[3,64,128]{2,1,0:T(8,128)} custom-call(f32[8,12,2,8,128]{4,3,2,1,0:T(8,128)S(1)} %get-tuple-element.23.full.refs_0_, f32[3,12,2,8,128]{4,3,2,1,0:T(8,128)S(1)} %get-tuple-element.24.refs_1_, f32[3,12,2,8,128]{4,3,2,1,0:T(8,128)S(1)} %get-tuple-element.25.refs_2_, f32[12,2,8,128]{3,2,1,0:T(8,128)S(1)} %get-tuple-element.26.refs_3_, ...), custom_call_target="tpu_custom_call" | custom-call | flops 2000000 | bytes 100000 | tf_op jit(solution)/shard_map/pallas_call | solution.py:716
Async XLA Ops:
  1.1 8.5 %collective-permute-start = (f32[7,4,8,128]{3,2,1,0:T(8,128)S(1)}, f32[7,4,8,128]{3,2,1,0:T(8,128)S(1)}, u32[]{:S(2)}, u32[]{:S(2)}) collective-permute-start(f32[7,4,8,128]{3,2,1,0:T(8,128)S(1)} %get-tuple-element.18), channel_id=1, source_target_pairs={{0,8},{1,9},{2,10},{3,11},{4,12},{5,13},{6,14},{7,15},{8,0},{9,1},... | collective-permute-start | bytes 344072 | tf_op jit(solution)/shard_map/ppermute | solution.py:700
  1.2 8.5 %collective-permute-start.1 = (f32[7,4,8,128]{3,2,1,0:T(8,128)S(1)}, f32[7,4,8,128]{3,2,1,0:T(8,128)S(1)}, u32[]{:S(2)}, u32[]{:S(2)}) collective-permute-start(f32[7,4,8,128]{3,2,1,0:T(8,128)S(1)} %get-tuple-element.19), channel_id=1, source_target_pairs={{0,1},{1,0},{2,3},{3,2},{4,5},{5,4},{6,7},{7,6},{8,16},{9,17},{10,... | collective-permute-start | bytes 344072 | tf_op jit(solution)/shard_map/ppermute | solution.py:700
  3.8 5.9 %collective-permute-start.2 = (f32[28,8,128]{2,1,0:T(8,128)S(1)}, f32[28,8,128]{2,1,0:T(8,128)S(1)}, u32[]{:S(2)}, u32[]{:S(2)}) collective-permute-start(f32[28,8,128]{2,1,0:T(8,128)S(1)} %get-tuple-element.20), channel_id=1, source_target_pairs={{0,4},{1,5},{2,6},{3,7},{4,0},{5,1},{6,2},{7,3},{8,12},{9,13},{10,... | collective-permute-start | bytes 344072 | tf_op jit(solution)/shard_map/ppermute | solution.py:700
  5.0 4.6 %collective-permute-start.3 = (f32[14,8,128]{2,1,0:T(8,128)S(1)}, f32[14,8,128]{2,1,0:T(8,128)S(1)}, u32[]{:S(2)}, u32[]{:S(2)}) collective-permute-start(f32[14,8,128]{2,1,0:T(8,128)S(1)} %get-tuple-element.21), channel_id=1, source_target_pairs={{0,12},{1,13},{2,14},{3,15},{4,8},{5,9},{6,10},{7,11},{8,4},{9,5},... | collective-permute-start | bytes 172040 | tf_op jit(solution)/shard_map/ppermute | solution.py:700
  5.0 4.6 %collective-permute-start.4 = (f32[14,8,128]{2,1,0:T(8,128)S(1)}, f32[14,8,128]{2,1,0:T(8,128)S(1)}, u32[]{:S(2)}, u32[]{:S(2)}) collective-permute-start(f32[14,8,128]{2,1,0:T(8,128)S(1)} %get-tuple-element.22), channel_id=1, source_target_pairs={{0,1},{1,0},{2,3},{3,2},{4,5},{5,4},{6,7},{7,6},{8,20},{9,21},{10,... | collective-permute-start | bytes 172040 | tf_op jit(solution)/shard_map/ppermute | solution.py:700
  10.2 6.4 %collective-permute-start.5 = (f32[3,2,8,128]{3,2,1,0:T(8,128)S(1)}, f32[3,2,8,128]{3,2,1,0:T(8,128)S(1)}, u32[]{:S(2)}, u32[]{:S(2)}) collective-permute-start(f32[3,2,8,128]{3,2,1,0:T(8,128)S(1)} %get-tuple-element.27), channel_id=1, source_target_pairs={{0,1},{1,0},{2,3},{3,2},{4,5},{5,4},{6,7},{7,6},{8,9},{9,8},{10,11... | collective-permute-start | bytes 73736 | tf_op jit(solution)/shard_map/ppermute | solution.py:700
  12.9 3.7 %collective-permute-start.6 = (f32[3,2,8,128]{3,2,1,0:T(8,128)S(1)}, f32[3,2,8,128]{3,2,1,0:T(8,128)S(1)}, u32[]{:S(2)}, u32[]{:S(2)}) collective-permute-start(f32[3,2,8,128]{3,2,1,0:T(8,128)S(1)} %get-tuple-element.28), channel_id=1, source_target_pairs={{0,4},{1,2},{2,1},{3,7},{4,0},{5,6},{6,5},{7,3},{8,12},{9,10},{10,... | collective-permute-start | bytes 73736 | tf_op jit(solution)/shard_map/ppermute | solution.py:700

commit v6 on v5

--- a/solution.py
+++ b/solution.py
@@ -412,7 +412,7 @@
     return [[(ref[3 * c + k, row, 0], ref[3 * c + k, row, 1]) for k in range(3)] for c in range(3)]
 
 
-def packed_stresses(shape, full, step, rows, flat):
+def packed_stresses(shape, weight, step, rows, flat):
     fflat, wflat, pflat = flat
     width = shape.size[0] + 2 * HALO - 1 - 2 * step
     spans = []
@@ -432,7 +432,7 @@
             for c in range(3):
                 for d in range(3):
                     fflat[3 * c + d, here, :] = f[c][d][t][part]
-            wflat[here, :] = full[W_CH, j, t][part]
+            wflat[here, :] = weight(j)[t][part]
         filled = (j - begin + 1) * width
         upto = filled // 8 if j < rows[-1] else -(-filled // 8)
         for i in range(state["tiles"], upto):
@@ -490,7 +490,13 @@
             put9(grad, row, gradient_row(load_row(old, row)))
 
     if flat:
-        packed = packed_stresses(shape, full, step, range(first, last), flat)
+        packed = packed_stresses(
+            shape,
+            lambda j: load_row(full, j, (W_CH,))[0],
+            step,
+            range(first, last),
+            flat,
+        )
 
     def body(j):
         after = gradient_row(load_row(old, j + 2)) if j + 2 <= last else None
@@ -526,18 +532,18 @@
     return write
 
 
-def main_kernel(shape, full, one, two, gsize, grad, stress, part):
+def main_kernel(shape, full, one, two, gsize, grad, stress, part, *flat):
     step_sizes(shape, full, gsize)
     for step, (old, oldest, new) in enumerate(((full, full, one), (one, full, two))):
         head, steps = main_steps(
-            shape, full, gsize, old, oldest, writer(new), grad, stress, part, step
+            shape, full, gsize, old, oldest, writer(new), grad, stress, part, step, flat if step else None
         )
         head()
         for run in steps:
             run()
 
 
-def edge_parts(shape, full, zrecv, bufs, goal, gsize, stiff, grad, stress):
+def edge_parts(shape, full, zrecv, bufs, goal, gsize, stiff, grad, stress, flat):
     sz = shape.size[2]
     erows = shape.erows
     ez = even("gz")
@@ -593,11 +599,22 @@
         turned = [tuple(roll_z(t, -SPAN) for t in pair) for pair in load_row(bufs[step], 0)]
         put9(grad, erows, gradient_row(turned))
 
-    def stresses(m):
-        now = stress_row(deform_rows(get9(grad, m), get9(grad, m + 1)), (stiff[m, 0], stiff[m, 1]))
+    def keep(m, now):
         put9(stress, m + 1, now)
         if m == erows - 1:
             put9(stress, 0, [[tuple(roll_z(t, SPAN) for t in pair) for pair in row] for row in now])
+
+    def stresses(step):
+        def weight(m):
+            return (stiff[m, 0], stiff[m, 1])
+
+        rows = range(erows)
+        if step:
+            packed = packed_stresses(shape, weight, step, rows, flat)
+        for m in rows if step else [erows - 1, *rows[:-1]]:
+            f = deform_rows(get9(grad, m), get9(grad, m + 1))
+            for known in packed(m, f) if step else [(m, stress_row(f, weight(m)))]:
+                keep(*known)
 
     def updates(step, m):
         new = update_row(
@@ -621,8 +638,9 @@
     erows = shape.erows
     lane = lane_ids()
     setup, gradients, stresses, updates = edge_parts(
-        shape, full, (zrecv0, zrecv1), bufs, egoal, egsize, estiff, egrad, estress
-    )
+        shape, full, (zrecv0, zrecv1), bufs, egoal, egsize, estiff, egrad, estress, flat[3:]
+    )
+    flat = flat[:3]
     flip = (lax.axis_index("gy") == 1) if shape.mirror else False
     turned = jnp.where(flip, -1.0 / SCALE, 1.0 / SCALE).astype(jnp.float32) if shape.mirror else 1.0 / SCALE
 
@@ -646,8 +664,7 @@
     edge = [setup]
     for step in range(ITERS):
         edge.append(functools.partial(gradients, step))
-        order = [erows - 1] + list(range(erows - 1))
-        edge.append(lambda order=order: [stresses(m) for m in order])
+        edge.append(functools.partial(stresses, step))
         edge.append(lambda step=step: [updates(step, m) for m in range(erows)])
     head, steps = main_steps(
         shape, full, gsize, two, one, writer(three), grad, stress, part, 2, flat
@@ -784,11 +801,15 @@
     )
     z0 = send(shape, z0, None, None, 0)
     z1 = send(shape, z1, None, None, 1)
+    def flat(count):
+        length = 16 * (count + 2)
+        return [scratch(9, length, sz), scratch(length, sz), scratch(9, length, sz)]
+
     one, two, gsize = call(
         functools.partial(main_kernel, shape),
         [f32(3, rows, 2, 8, sz), f32(3, rows, 2, 8, sz), f32(rows, 2, 8, sz)],
         (full,),
-        [scratch(count, rows, 2, 8, sz) for count in (9, 9, 6)],
+        [scratch(count, rows, 2, 8, sz) for count in (9, 9, 6)] + flat(rows),
     )
 
     def last(*refs):
@@ -805,7 +826,8 @@
         + [scratch(erows, 2, 8, sz)] * 2
         + [scratch(9, erows + 1, 2, 8, sz)] * 2
         + [scratch(sy, 3, 2 * 8, sz)]
-        + [scratch(9, 16 * (rows + 2), sz), scratch(16 * (rows + 2), sz), scratch(9, 16 * (rows + 2), sz)],
+        + flat(rows)
+        + flat(erows),
     )
     return out.reshape(3, sx, sy, sz)
 

time: 21.4 us -> 21.2 us (level)
  no operation moved by 1% of the time
where the time goes in v6:
time: 21.2 us; the launch traced here: 21.1 us
  starting transfers between devices  9.76 us (46%)
  Pallas kernels  8.62 us (41%)
  waiting for transfers between devices  2.63 us (12%)
    ppermute x7, starting transfers between devices, send(): return lax.ppermute(value, ('gx', 'gy', 'gz'), exchange(shape, parities))  9.76 us
    pallas_call x4, Pallas kernels, call(): pl.pallas_call(body, out_shape=outs, in_specs=specs or [VM] * len(args),...  8.62 us
    ppermute x7, waiting for transfers between devices, send(): return lax.ppermute(value, ('gx', 'gy', 'gz'), exchange(shape, parities))  2.63 us
  transfers between devices with their start and end apart: 7, of which 1 were waited for; matrix products, arithmetic and copies ran while one was open for 0% of the time, Pallas kernels for 12%

profile of v6, /device:TPU:9, one launch (start us, length us, event | category | flops | bytes accessed | tf_op | source)
XLA Modules:
  0.0 21.1 jit_solution(10057800351100080493)
XLA Ops:
  0.0 1.1 %shard_map.55 = (f32[8,9,8,128]{3,2,1,0:T(8,128)S(1)}, f32[7,4,8,128]{3,2,1,0:T(8,128)S(1)}, f32[7,4,8,128]{3,2,1,0:T(8,128)S(1)}, f32[28,8,128]{2,1,0:T(8,128)S...) custom-call(f32[3,64,128]{2,1,0:T(8,128)} %bitcast.5, f32[3,64,128]{2,1,0:T(8,128)} %bitcast.6, ...), custom_call_target="tpu_custom_call" | custom-call | flops 2000000 | bytes 100000 | tf_op jit(solution)/shard_map/pallas_call | solution.py:733
  1.1 0.1 collective-permute-start
  1.2 2.6 %collective-permute-start.1 = (f32[7,4,8,128]{3,2,1,0:T(8,128)S(1)}, f32[7,4,8,128]{3,2,1,0:T(8,128)S(1)}, u32[]{:S(2)}, u32[]{:S(2)}) collective-permute-start(f32[7,4,8,128]{3,2,1,0:T(8,128)S(1)} %get-tuple-element.19), channel_id=1, source_target_pairs={{0,1},{1,0},{2,3},{3,2},{4,5},{5,4},{6,7},{7,6},{8,16},{9,17},{10,... | collective-permute-start | bytes 344072 | tf_op jit(solution)/shard_map/ppermute | solution.py:717
  3.8 1.2 %collective-permute-start.2 = (f32[28,8,128]{2,1,0:T(8,128)S(1)}, f32[28,8,128]{2,1,0:T(8,128)S(1)}, u32[]{:S(2)}, u32[]{:S(2)}) collective-permute-start(f32[28,8,128]{2,1,0:T(8,128)S(1)} %get-tuple-element.20), channel_id=1, source_target_pairs={{0,4},{1,5},{2,6},{3,7},{4,0},{5,1},{6,2},{7,3},{8,12},{9,13},{10,... | collective-permute-start | bytes 344072 | tf_op jit(solution)/shard_map/ppermute | solution.py:717
  5.0 0.0 collective-permute-start.3
  5.0 2.0 %collective-permute-start.4 = (f32[14,8,128]{2,1,0:T(8,128)S(1)}, f32[14,8,128]{2,1,0:T(8,128)S(1)}, u32[]{:S(2)}, u32[]{:S(2)}) collective-permute-start(f32[14,8,128]{2,1,0:T(8,128)S(1)} %get-tuple-element.22), channel_id=1, source_target_pairs={{0,1},{1,0},{2,3},{3,2},{4,5},{5,4},{6,7},{7,6},{8,20},{9,21},{10,... | collective-permute-start | bytes 172040 | tf_op jit(solution)/shard_map/ppermute | solution.py:717
  7.1 2.6 %collective-permute-done.3.rest_3_ = f32[14,8,128]{2,1,0:T(8,128)S(1)} collective-permute-done((f32[14,8,128]{2,1,0:T(8,128)S(1)}, f32[14,8,128]{2,1,0:T(8,128)S(1)}, u32[]{:S(2)}, u32[]{:S(2)}) %collective-permute-start.3) | collective-permute-done | bytes 57376 | tf_op jit(solution)/shard_map/ppermute | solution.py:717
  9.7 0.0 collective-permute-done.4.rest_4_
  9.7 0.0 collective-permute-done.rest_0_
  9.7 0.0 collective-permute-done.1.rest_1_
  9.7 0.0 collective-permute-done.2.rest_2_
  9.7 0.5 %shard_map.56 = (f32[8,12,2,8,128]{4,3,2,1,0:T(8,128)S(1)}, f32[3,2,8,128]{3,2,1,0:T(8,128)S(1)}, f32[3,2,8,128]{3,2,1,0:T(8,128)S(1)}) custom-call(f32[8,9,8,128]{3,2,1,0:T(8,128)S(1)} %get-tuple-element.17.own, f32[7,4,8,128]{3,2,1,0:T(8,128)S(1)} %collective-permute-done.rest_0_, f32[7,4,8,128]{3,2,1,0:T(8,128)S(1)} %collective-permute-done.1.rest_1_, ...), custom_call_target="tpu_custom_call" | custom-call | flops 2000000 | bytes 100000 | tf_op jit(solution)/shard_map/pallas_call | solution.py:733
  10.2 2.7 %collective-permute-start.5 = (f32[3,2,8,128]{3,2,1,0:T(8,128)S(1)}, f32[3,2,8,128]{3,2,1,0:T(8,128)S(1)}, u32[]{:S(2)}, u32[]{:S(2)}) collective-permute-start(f32[3,2,8,128]{3,2,1,0:T(8,128)S(1)} %get-tuple-element.27), channel_id=1, source_target_pairs={{0,1},{1,0},{2,3},{3,2},{4,5},{5,4},{6,7},{7,6},{8,9},{9,8},{10,11... | collective-permute-start | bytes 73736 | tf_op jit(solution)/shard_map/ppermute | solution.py:717
  12.9 1.2 %collective-permute-start.6 = (f32[3,2,8,128]{3,2,1,0:T(8,128)S(1)}, f32[3,2,8,128]{3,2,1,0:T(8,128)S(1)}, u32[]{:S(2)}, u32[]{:S(2)}) collective-permute-start(f32[3,2,8,128]{3,2,1,0:T(8,128)S(1)} %get-tuple-element.28), channel_id=1, source_target_pairs={{0,4},{1,2},{2,1},{3,7},{4,0},{5,6},{6,5},{7,3},{8,12},{9,10},{10,... | collective-permute-start | bytes 73736 | tf_op jit(solution)/shard_map/ppermute | solution.py:717
  14.1 2.5 %shard_map.57 = (f32[3,12,2,8,128]{4,3,2,1,0:T(8,128)S(1)}, f32[3,12,2,8,128]{4,3,2,1,0:T(8,128)S(1)}, f32[12,2,8,128]{3,2,1,0:T(8,128)S(1)}) custom-call(f32[8,12,2,8,128]{4,3,2,1,0:T(8,128)S(1)} %get-tuple-element.23.full.refs_0_), custom_call_target="tpu_custom_call" | custom-call | flops 2000000 | bytes 100000 | tf_op jit(solution)/shard_map/pallas_call | solution.py:733
  16.6 0.0 collective-permute-done.5.refs_4_
  16.6 0.0 collective-permute-done.6.refs_5_
  16.6 4.5 %shard_map.58 = f32[3,64,128]{2,1,0:T(8,128)} custom-call(f32[8,12,2,8,128]{4,3,2,1,0:T(8,128)S(1)} %get-tuple-element.23.full.refs_0_, f32[3,12,2,8,128]{4,3,2,1,0:T(8,128)S(1)} %get-tuple-element.24.refs_1_, f32[3,12,2,8,128]{4,3,2,1,0:T(8,128)S(1)} %get-tuple-element.25.refs_2_, f32[12,2,8,128]{3,2,1,0:T(8,128)S(1)} %get-tuple-element.26.refs_3_, ...), custom_call_target="tpu_custom_call" | custom-call | flops 2000000 | bytes 100000 | tf_op jit(solution)/shard_map/pallas_call | solution.py:733
Async XLA Ops:
  1.1 8.5 %collective-permute-start = (f32[7,4,8,128]{3,2,1,0:T(8,128)S(1)}, f32[7,4,8,128]{3,2,1,0:T(8,128)S(1)}, u32[]{:S(2)}, u32[]{:S(2)}) collective-permute-start(f32[7,4,8,128]{3,2,1,0:T(8,128)S(1)} %get-tuple-element.18), channel_id=1, source_target_pairs={{0,8},{1,9},{2,10},{3,11},{4,12},{5,13},{6,14},{7,15},{8,0},{9,1},... | collective-permute-start | bytes 344072 | tf_op jit(solution)/shard_map/ppermute | solution.py:717
  1.2 8.5 %collective-permute-start.1 = (f32[7,4,8,128]{3,2,1,0:T(8,128)S(1)}, f32[7,4,8,128]{3,2,1,0:T(8,128)S(1)}, u32[]{:S(2)}, u32[]{:S(2)}) collective-permute-start(f32[7,4,8,128]{3,2,1,0:T(8,128)S(1)} %get-tuple-element.19), channel_id=1, source_target_pairs={{0,1},{1,0},{2,3},{3,2},{4,5},{5,4},{6,7},{7,6},{8,16},{9,17},{10,... | collective-permute-start | bytes 344072 | tf_op jit(solution)/shard_map/ppermute | solution.py:717
  3.8 5.9 %collective-permute-start.2 = (f32[28,8,128]{2,1,0:T(8,128)S(1)}, f32[28,8,128]{2,1,0:T(8,128)S(1)}, u32[]{:S(2)}, u32[]{:S(2)}) collective-permute-start(f32[28,8,128]{2,1,0:T(8,128)S(1)} %get-tuple-element.20), channel_id=1, source_target_pairs={{0,4},{1,5},{2,6},{3,7},{4,0},{5,1},{6,2},{7,3},{8,12},{9,13},{10,... | collective-permute-start | bytes 344072 | tf_op jit(solution)/shard_map/ppermute | solution.py:717
  5.0 4.6 %collective-permute-start.3 = (f32[14,8,128]{2,1,0:T(8,128)S(1)}, f32[14,8,128]{2,1,0:T(8,128)S(1)}, u32[]{:S(2)}, u32[]{:S(2)}) collective-permute-start(f32[14,8,128]{2,1,0:T(8,128)S(1)} %get-tuple-element.21), channel_id=1, source_target_pairs={{0,12},{1,13},{2,14},{3,15},{4,8},{5,9},{6,10},{7,11},{8,4},{9,5},... | collective-permute-start | bytes 172040 | tf_op jit(solution)/shard_map/ppermute | solution.py:717
  5.0 4.6 %collective-permute-start.4 = (f32[14,8,128]{2,1,0:T(8,128)S(1)}, f32[14,8,128]{2,1,0:T(8,128)S(1)}, u32[]{:S(2)}, u32[]{:S(2)}) collective-permute-start(f32[14,8,128]{2,1,0:T(8,128)S(1)} %get-tuple-element.22), channel_id=1, source_target_pairs={{0,1},{1,0},{2,3},{3,2},{4,5},{5,4},{6,7},{7,6},{8,20},{9,21},{10,... | collective-permute-start | bytes 172040 | tf_op jit(solution)/shard_map/ppermute | solution.py:717
  10.2 6.4 %collective-permute-start.5 = (f32[3,2,8,128]{3,2,1,0:T(8,128)S(1)}, f32[3,2,8,128]{3,2,1,0:T(8,128)S(1)}, u32[]{:S(2)}, u32[]{:S(2)}) collective-permute-start(f32[3,2,8,128]{3,2,1,0:T(8,128)S(1)} %get-tuple-element.27), channel_id=1, source_target_pairs={{0,1},{1,0},{2,3},{3,2},{4,5},{5,4},{6,7},{7,6},{8,9},{9,8},{10,11... | collective-permute-start | bytes 73736 | tf_op jit(solution)/shard_map/ppermute | solution.py:717
  12.9 3.7 %collective-permute-start.6 = (f32[3,2,8,128]{3,2,1,0:T(8,128)S(1)}, f32[3,2,8,128]{3,2,1,0:T(8,128)S(1)}, u32[]{:S(2)}, u32[]{:S(2)}) collective-permute-start(f32[3,2,8,128]{3,2,1,0:T(8,128)S(1)} %get-tuple-element.28), channel_id=1, source_target_pairs={{0,4},{1,2},{2,1},{3,7},{4,0},{5,6},{6,5},{7,3},{8,12},{9,10},{10,... | collective-permute-start | bytes 73736 | tf_op jit(solution)/shard_map/ppermute | solution.py:717

commit v7 on v6

--- a/solution.py
+++ b/solution.py
@@ -814,12 +814,13 @@
 
     def last(*refs):
         ends = 11 + ITERS + 1
-        last_kernel(shape, *refs[:11], refs[11:ends], *refs[ends:])
+        full, one, two, gsize, z1, z0 = refs[:6]
+        last_kernel(shape, full, one, two, gsize, z0, z1, *refs[6:11], refs[11:ends], *refs[ends:])
 
     (out,) = call(
         last,
         [f32(3, sx * sy, sz)],
-        (full, one, two, gsize, z0, z1),
+        (full, one, two, gsize, z1, z0),
         [scratch(3, rows, 2, 8, sz)]
         + [scratch(count, rows, 2, 8, sz) for count in (9, 9, 6)]
         + [scratch(3, erows, 2, 8, sz) for _ in range(ITERS + 2)]

time: 21.2 us -> 21.1 us (level)
  no operation moved by 1% of the time
where the time goes in v7:
time: 21.1 us; the launch traced here: 21 us
  starting transfers between devices  9.68 us (46%)
  Pallas kernels  8.62 us (41%)
  waiting for transfers between devices  2.63 us (12%)
    ppermute x7, starting transfers between devices, send(): return lax.ppermute(value, ('gx', 'gy', 'gz'), exchange(shape, parities))  9.68 us
    pallas_call x4, Pallas kernels, call(): pl.pallas_call(body, out_shape=outs, in_specs=specs or [VM] * len(args),...  8.62 us
    ppermute x7, waiting for transfers between devices, send(): return lax.ppermute(value, ('gx', 'gy', 'gz'), exchange(shape, parities))  2.63 us
  transfers between devices with their start and end apart: 7, of which 1 were waited for; matrix products, arithmetic and copies ran while one was open for 0% of the time, Pallas kernels for 12%

profile of v7, /device:TPU:9, one launch (start us, length us, event | category | flops | bytes accessed | tf_op | source)
XLA Modules:
  0.0 21.0 jit_solution(6177266917081867516)
XLA Ops:
  0.0 1.1 %shard_map.55 = (f32[8,9,8,128]{3,2,1,0:T(8,128)S(1)}, f32[7,4,8,128]{3,2,1,0:T(8,128)S(1)}, f32[7,4,8,128]{3,2,1,0:T(8,128)S(1)}, f32[28,8,128]{2,1,0:T(8,128)S...) custom-call(f32[3,64,128]{2,1,0:T(8,128)} %bitcast.5, f32[3,64,128]{2,1,0:T(8,128)} %bitcast.6, ...), custom_call_target="tpu_custom_call" | custom-call | flops 2000000 | bytes 100000 | tf_op jit(solution)/shard_map/pallas_call | solution.py:733
  1.1 0.1 collective-permute-start
  1.2 2.6 %collective-permute-start.1 = (f32[7,4,8,128]{3,2,1,0:T(8,128)S(1)}, f32[7,4,8,128]{3,2,1,0:T(8,128)S(1)}, u32[]{:S(2)}, u32[]{:S(2)}) collective-permute-start(f32[7,4,8,128]{3,2,1,0:T(8,128)S(1)} %get-tuple-element.19), channel_id=1, source_target_pairs={{0,1},{1,0},{2,3},{3,2},{4,5},{5,4},{6,7},{7,6},{8,16},{9,17},{10,... | collective-permute-start | bytes 344072 | tf_op jit(solution)/shard_map/ppermute | solution.py:717
  3.8 1.2 %collective-permute-start.2 = (f32[28,8,128]{2,1,0:T(8,128)S(1)}, f32[28,8,128]{2,1,0:T(8,128)S(1)}, u32[]{:S(2)}, u32[]{:S(2)}) collective-permute-start(f32[28,8,128]{2,1,0:T(8,128)S(1)} %get-tuple-element.20), channel_id=1, source_target_pairs={{0,4},{1,5},{2,6},{3,7},{4,0},{5,1},{6,2},{7,3},{8,12},{9,13},{10,... | collective-permute-start | bytes 344072 | tf_op jit(solution)/shard_map/ppermute | solution.py:717
  5.0 0.0 collective-permute-start.3
  5.0 2.0 %collective-permute-start.4 = (f32[14,8,128]{2,1,0:T(8,128)S(1)}, f32[14,8,128]{2,1,0:T(8,128)S(1)}, u32[]{:S(2)}, u32[]{:S(2)}) collective-permute-start(f32[14,8,128]{2,1,0:T(8,128)S(1)} %get-tuple-element.22), channel_id=1, source_target_pairs={{0,1},{1,0},{2,3},{3,2},{4,5},{5,4},{6,7},{7,6},{8,20},{9,21},{10,... | collective-permute-start | bytes 172040 | tf_op jit(solution)/shard_map/ppermute | solution.py:717
  7.1 2.6 %collective-permute-done.3.rest_3_ = f32[14,8,128]{2,1,0:T(8,128)S(1)} collective-permute-done((f32[14,8,128]{2,1,0:T(8,128)S(1)}, f32[14,8,128]{2,1,0:T(8,128)S(1)}, u32[]{:S(2)}, u32[]{:S(2)}) %collective-permute-start.3) | collective-permute-done | bytes 57376 | tf_op jit(solution)/shard_map/ppermute | solution.py:717
  9.7 0.0 collective-permute-done.4.rest_4_
  9.7 0.0 collective-permute-done.rest_0_
  9.7 0.0 collective-permute-done.1.rest_1_
  9.7 0.0 collective-permute-done.2.rest_2_
  9.7 0.5 %shard_map.56 = (f32[8,12,2,8,128]{4,3,2,1,0:T(8,128)S(1)}, f32[3,2,8,128]{3,2,1,0:T(8,128)S(1)}, f32[3,2,8,128]{3,2,1,0:T(8,128)S(1)}) custom-call(f32[8,9,8,128]{3,2,1,0:T(8,128)S(1)} %get-tuple-element.17.own, f32[7,4,8,128]{3,2,1,0:T(8,128)S(1)} %collective-permute-done.rest_0_, f32[7,4,8,128]{3,2,1,0:T(8,128)S(1)} %collective-permute-done.1.rest_1_, ...), custom_call_target="tpu_custom_call" | custom-call | flops 2000000 | bytes 100000 | tf_op jit(solution)/shard_map/pallas_call | solution.py:733
  10.2 3.8 %collective-permute-start.5 = (f32[3,2,8,128]{3,2,1,0:T(8,128)S(1)}, f32[3,2,8,128]{3,2,1,0:T(8,128)S(1)}, u32[]{:S(2)}, u32[]{:S(2)}) collective-permute-start(f32[3,2,8,128]{3,2,1,0:T(8,128)S(1)} %get-tuple-element.27), channel_id=1, source_target_pairs={{0,4},{1,2},{2,1},{3,7},{4,0},{5,6},{6,5},{7,3},{8,12},{9,10},{10,... | collective-permute-start | bytes 73736 | tf_op jit(solution)/shard_map/ppermute | solution.py:717
  14.0 0.0 collective-permute-start.6
  14.0 2.5 %shard_map.57 = (f32[3,12,2,8,128]{4,3,2,1,0:T(8,128)S(1)}, f32[3,12,2,8,128]{4,3,2,1,0:T(8,128)S(1)}, f32[12,2,8,128]{3,2,1,0:T(8,128)S(1)}) custom-call(f32[8,12,2,8,128]{4,3,2,1,0:T(8,128)S(1)} %get-tuple-element.23.full.refs_0_), custom_call_target="tpu_custom_call" | custom-call | flops 2000000 | bytes 100000 | tf_op jit(solution)/shard_map/pallas_call | solution.py:733
  16.5 0.0 collective-permute-done.5.refs_4_
  16.5 0.0 collective-permute-done.6.refs_5_
  16.5 4.5 %shard_map.58 = f32[3,64,128]{2,1,0:T(8,128)} custom-call(f32[8,12,2,8,128]{4,3,2,1,0:T(8,128)S(1)} %get-tuple-element.23.full.refs_0_, f32[3,12,2,8,128]{4,3,2,1,0:T(8,128)S(1)} %get-tuple-element.24.refs_1_, f32[3,12,2,8,128]{4,3,2,1,0:T(8,128)S(1)} %get-tuple-element.25.refs_2_, f32[12,2,8,128]{3,2,1,0:T(8,128)S(1)} %get-tuple-element.26.refs_3_, ...), custom_call_target="tpu_custom_call" | custom-call | flops 2000000 | bytes 100000 | tf_op jit(solution)/shard_map/pallas_call | solution.py:733
Async XLA Ops:
  1.1 8.5 %collective-permute-start = (f32[7,4,8,128]{3,2,1,0:T(8,128)S(1)}, f32[7,4,8,128]{3,2,1,0:T(8,128)S(1)}, u32[]{:S(2)}, u32[]{:S(2)}) collective-permute-start(f32[7,4,8,128]{3,2,1,0:T(8,128)S(1)} %get-tuple-element.18), channel_id=1, source_target_pairs={{0,8},{1,9},{2,10},{3,11},{4,12},{5,13},{6,14},{7,15},{8,0},{9,1},... | collective-permute-start | bytes 344072 | tf_op jit(solution)/shard_map/ppermute | solution.py:717
  1.2 8.5 %collective-permute-start.1 = (f32[7,4,8,128]{3,2,1,0:T(8,128)S(1)}, f32[7,4,8,128]{3,2,1,0:T(8,128)S(1)}, u32[]{:S(2)}, u32[]{:S(2)}) collective-permute-start(f32[7,4,8,128]{3,2,1,0:T(8,128)S(1)} %get-tuple-element.19), channel_id=1, source_target_pairs={{0,1},{1,0},{2,3},{3,2},{4,5},{5,4},{6,7},{7,6},{8,16},{9,17},{10,... | collective-permute-start | bytes 344072 | tf_op jit(solution)/shard_map/ppermute | solution.py:717
  3.8 5.9 %collective-permute-start.2 = (f32[28,8,128]{2,1,0:T(8,128)S(1)}, f32[28,8,128]{2,1,0:T(8,128)S(1)}, u32[]{:S(2)}, u32[]{:S(2)}) collective-permute-start(f32[28,8,128]{2,1,0:T(8,128)S(1)} %get-tuple-element.20), channel_id=1, source_target_pairs={{0,4},{1,5},{2,6},{3,7},{4,0},{5,1},{6,2},{7,3},{8,12},{9,13},{10,... | collective-permute-start | bytes 344072 | tf_op jit(solution)/shard_map/ppermute | solution.py:717
  5.0 4.6 %collective-permute-start.3 = (f32[14,8,128]{2,1,0:T(8,128)S(1)}, f32[14,8,128]{2,1,0:T(8,128)S(1)}, u32[]{:S(2)}, u32[]{:S(2)}) collective-permute-start(f32[14,8,128]{2,1,0:T(8,128)S(1)} %get-tuple-element.21), channel_id=1, source_target_pairs={{0,12},{1,13},{2,14},{3,15},{4,8},{5,9},{6,10},{7,11},{8,4},{9,5},... | collective-permute-start | bytes 172040 | tf_op jit(solution)/shard_map/ppermute | solution.py:717
  5.0 4.6 %collective-permute-start.4 = (f32[14,8,128]{2,1,0:T(8,128)S(1)}, f32[14,8,128]{2,1,0:T(8,128)S(1)}, u32[]{:S(2)}, u32[]{:S(2)}) collective-permute-start(f32[14,8,128]{2,1,0:T(8,128)S(1)} %get-tuple-element.22), channel_id=1, source_target_pairs={{0,1},{1,0},{2,3},{3,2},{4,5},{5,4},{6,7},{7,6},{8,20},{9,21},{10,... | collective-permute-start | bytes 172040 | tf_op jit(solution)/shard_map/ppermute | solution.py:717
  10.2 6.3 %collective-permute-start.5 = (f32[3,2,8,128]{3,2,1,0:T(8,128)S(1)}, f32[3,2,8,128]{3,2,1,0:T(8,128)S(1)}, u32[]{:S(2)}, u32[]{:S(2)}) collective-permute-start(f32[3,2,8,128]{3,2,1,0:T(8,128)S(1)} %get-tuple-element.27), channel_id=1, source_target_pairs={{0,4},{1,2},{2,1},{3,7},{4,0},{5,6},{6,5},{7,3},{8,12},{9,10},{10,... | collective-permute-start | bytes 73736 | tf_op jit(solution)/shard_map/ppermute | solution.py:717
  14.0 2.5 %collective-permute-start.6 = (f32[3,2,8,128]{3,2,1,0:T(8,128)S(1)}, f32[3,2,8,128]{3,2,1,0:T(8,128)S(1)}, u32[]{:S(2)}, u32[]{:S(2)}) collective-permute-start(f32[3,2,8,128]{3,2,1,0:T(8,128)S(1)} %get-tuple-element.28), channel_id=1, source_target_pairs={{0,1},{1,0},{2,3},{3,2},{4,5},{5,4},{6,7},{7,6},{8,9},{9,8},{10,11... | collective-permute-start | bytes 73736 | tf_op jit(solution)/shard_map/ppermute | solution.py:717
